TPU v7x, 32 devices: a whole 2x2x4 slice. The times are simulated.
32 devices in a mesh: tp: 32 (over z, y, x, core).
Axes of the slice: x: 2, y: 2, z: 4, core: 2. Of those that a mesh axis runs over, the one named last changes fastest.
Arguments:
- x_in: bfloat16 [16, 256, 4096], P(None, 'tp')
- grad_y: bfloat16 [16, 256, 4096], P(None, 'tp')
- ln_gain: float32 [4096], replicated
- w_query: bfloat16 [4096, 32, 128], P(None, 'tp')
- w_key: bfloat16 [4096, 128], replicated
- w_value: bfloat16 [4096, 128], replicated
- w_out: bfloat16 [32, 128, 4096], P('tp')
- w_gate: bfloat16 [4096, 16384], P(None, 'tp')
- w_up: bfloat16 [4096, 16384], P(None, 'tp')
- w_down: bfloat16 [16384, 4096], P('tp')
Outputs:
- output 1: bfloat16 [16, 256, 4096], P(None, 'tp')
- output 2: bfloat16 [16, 256, 4096], P(None, 'tp')
- output 3: float32 [4096], replicated
- output 4: bfloat16 [4096, 32, 128], P(None, 'tp')
- output 5: bfloat16 [4096, 128], replicated
- output 6: bfloat16 [4096, 128], replicated
- output 7: bfloat16 [32, 128, 4096], P('tp')
- output 8: bfloat16 [4096, 16384], P(None, 'tp')
- output 9: bfloat16 [4096, 16384], P(None, 'tp')
- output 10: bfloat16 [16384, 4096], P('tp')
All inputs are finite; a program needn't handle non-finite values.
Results may differ from a plain program's by a relative error of at most 0.0189316.
Values are sent between devices in bfloat16 or wider.
A program may use at most 1 GiB of HBM per device.

v0:
```python
import jax
import jax.numpy as jnp
from jax import lax
from jax.sharding import PartitionSpec as P

LN_EPS = 1e-6
ROPE_BASE = 10000.0


def rope_tables(seq_len, head_dim):
    half_dim = head_dim // 2
    inv_freq = ROPE_BASE ** (-jnp.arange(half_dim, dtype=jnp.float32) * 2.0 / head_dim)
    angles = jnp.arange(seq_len, dtype=jnp.float32)[:, None] * inv_freq[None, :]
    return jnp.cos(angles), jnp.sin(angles)


def rotate_half(values, cos_tab, sin_tab):
    half_dim = values.shape[-1] // 2
    first_half = values[..., :half_dim]
    second_half = values[..., half_dim:]
    return jnp.concatenate([first_half * cos_tab - second_half * sin_tab, second_half * cos_tab + first_half * sin_tab], axis=-1)


def solution(mesh):
    group_size = mesh.shape["tp"]

    def layer_shard(x_loc, grad_y_loc, ln_gain, w_query, w_key, w_value, w_out, w_gate, w_up, w_down):
        head_dim = w_key.shape[1]
        seq_len = x_loc.shape[1] * group_size
        score_scale = head_dim ** -0.5
        residual = x_loc.astype(jnp.float32)
        centered = residual - jnp.mean(residual, axis=-1, keepdims=True)
        inv_std = lax.rsqrt(jnp.mean(centered * centered, axis=-1, keepdims=True) + LN_EPS)
        x_hat = centered * inv_std
        normed_loc = (ln_gain * x_hat).astype(jnp.bfloat16)
        normed = lax.all_gather(normed_loc, "tp", axis=1, tiled=True)

        cos_tab, sin_tab = rope_tables(seq_len, head_dim)
        cos_head = cos_tab[:, None, :]
        sin_head = sin_tab[:, None, :]
        q_raw = jnp.einsum("bld,dnk->blnk", normed, w_query, preferred_element_type=jnp.float32)
        k_raw = jnp.einsum("bld,dk->blk", normed, w_key, preferred_element_type=jnp.float32)
        values = jnp.einsum("bld,dk->blk", normed, w_value, preferred_element_type=jnp.float32).astype(jnp.bfloat16)
        q_rot = rotate_half(q_raw, cos_head, sin_head).astype(jnp.bfloat16)
        k_rot = rotate_half(k_raw, cos_tab, sin_tab).astype(jnp.bfloat16)
        scores = jnp.einsum("bqnk,bsk->bnqs", q_rot, k_rot, preferred_element_type=jnp.float32) * score_scale
        positions = jnp.arange(seq_len)
        causal = positions[:, None] >= positions[None, :]
        attn_probs = jax.nn.softmax(jnp.where(causal, scores, -1e30), axis=-1)
        probs_low = attn_probs.astype(jnp.bfloat16)
        attn_heads = jnp.einsum("bnqs,bsk->bqnk", probs_low, values, preferred_element_type=jnp.float32).astype(jnp.bfloat16)
        attn_part = jnp.einsum("crol,ole->cre", attn_heads, w_out, preferred_element_type=jnp.float32)
        gate_pre = jnp.einsum("bld,df->blf", normed, w_gate, preferred_element_type=jnp.float32)
        up_pre = jnp.einsum("bld,df->blf", normed, w_up, preferred_element_type=jnp.float32)
        gate_sig = jax.nn.sigmoid(gate_pre)
        gate_act = gate_pre * gate_sig
        hidden = (gate_act * up_pre).astype(jnp.bfloat16)
        mlp_part = jnp.einsum("blf,fd->bld", hidden, w_down, preferred_element_type=jnp.float32)
        branch_part = (attn_part + mlp_part).astype(jnp.bfloat16)
        branch_loc = lax.psum_scatter(branch_part, "tp", scatter_dimension=1, tiled=True)
        y_loc = (residual + branch_loc.astype(jnp.float32)).astype(jnp.bfloat16)

        grad_full = lax.all_gather(grad_y_loc, "tp", axis=1, tiled=True)
        grad_hidden = jnp.einsum("bld,fd->blf", grad_full, w_down, preferred_element_type=jnp.float32)
        grad_w_down = jnp.einsum("blf,bld->fd", hidden, grad_full, preferred_element_type=jnp.float32)
        grad_gate = (grad_hidden * up_pre * gate_sig * (1.0 + gate_pre * (1.0 - gate_sig))).astype(jnp.bfloat16)
        grad_up = (grad_hidden * gate_act).astype(jnp.bfloat16)
        grad_w_gate = jnp.einsum("bld,blf->df", normed, grad_gate, preferred_element_type=jnp.float32)
        grad_w_up = jnp.einsum("bld,blf->df", normed, grad_up, preferred_element_type=jnp.float32)

        grad_heads = jnp.einsum("bld,nkd->blnk", grad_full, w_out, preferred_element_type=jnp.float32).astype(jnp.bfloat16)
        grad_w_out = jnp.einsum("blnk,bld->nkd", attn_heads, grad_full, preferred_element_type=jnp.float32)
        grad_probs = jnp.einsum("bqnk,bsk->bnqs", grad_heads, values, preferred_element_type=jnp.float32)
        grad_values = jnp.einsum("bnqs,bqnk->bsk", probs_low, grad_heads, preferred_element_type=jnp.float32).astype(jnp.bfloat16)
        row_dot = jnp.sum(attn_probs * grad_probs, axis=-1, keepdims=True)
        grad_scores = (attn_probs * (grad_probs - row_dot) * score_scale).astype(jnp.bfloat16)
        grad_q_rot = jnp.einsum("bnqs,bsk->bqnk", grad_scores, k_rot, preferred_element_type=jnp.float32)
        grad_k_rot = jnp.einsum("bnqs,bqnk->bsk", grad_scores, q_rot, preferred_element_type=jnp.float32)
        grad_query = rotate_half(grad_q_rot, cos_head, -sin_head).astype(jnp.bfloat16)
        grad_key = rotate_half(grad_k_rot, cos_tab, -sin_tab).astype(jnp.bfloat16)
        grad_w_query = jnp.einsum("bld,blnk->dnk", normed, grad_query, preferred_element_type=jnp.float32)
        grad_w_key = lax.psum(jnp.einsum("bld,blk->dk", normed, grad_key, preferred_element_type=jnp.float32), "tp")
        grad_w_value = lax.psum(jnp.einsum("bld,blk->dk", normed, grad_values, preferred_element_type=jnp.float32), "tp")

        grad_normed = (
            jnp.einsum("blf,df->bld", grad_gate, w_gate, preferred_element_type=jnp.float32)
            + jnp.einsum("blf,df->bld", grad_up, w_up, preferred_element_type=jnp.float32)
            + jnp.einsum("blnk,dnk->bld", grad_query, w_query, preferred_element_type=jnp.float32)
            + jnp.einsum("blk,dk->bld", grad_key, w_key, preferred_element_type=jnp.float32)
            + jnp.einsum("blk,dk->bld", grad_values, w_value, preferred_element_type=jnp.float32)
        ).astype(jnp.bfloat16)
        grad_normed_loc = lax.psum_scatter(grad_normed, "tp", scatter_dimension=1, tiled=True).astype(jnp.float32)
        grad_gain = lax.psum(jnp.sum(grad_normed_loc * x_hat, axis=(0, 1)), "tp")
        grad_hat = grad_normed_loc * ln_gain
        grad_x = inv_std * (grad_hat - jnp.mean(grad_hat, axis=-1, keepdims=True) - x_hat * jnp.mean(grad_hat * x_hat, axis=-1, keepdims=True)) + grad_y_loc.astype(jnp.float32)
        return (
            y_loc,
            grad_x.astype(jnp.bfloat16),
            grad_gain,
            grad_w_query.astype(jnp.bfloat16),
            grad_w_key.astype(jnp.bfloat16),
            grad_w_value.astype(jnp.bfloat16),
            grad_w_out.astype(jnp.bfloat16),
            grad_w_gate.astype(jnp.bfloat16),
            grad_w_up.astype(jnp.bfloat16),
            grad_w_down.astype(jnp.bfloat16),
        )

    act_spec = P(None, "tp", None)
    weight_specs = (P(), P(None, "tp", None), P(), P(), P("tp", None, None), P(None, "tp"), P(None, "tp"), P("tp", None))
    return jax.shard_map(layer_shard, mesh=mesh, in_specs=(act_spec, act_spec) + weight_specs, out_specs=(act_spec, act_spec) + weight_specs, check_vma=False)
```

profile of v0, /device:TPU:0, one launch (start us, length us, event | category | flops | bytes accessed | tf_op | source)
XLA Modules:
  0.0 1580.4 jit_solution(16406349906226989756)
XLA Ops:
  7.3 1.6 convert_reduce_fusion
  8.8 1.7 fusion.36
  10.5 0.6 copy-done.24
  11.1 2.6 fusion.31
  13.8 0.7 all-gather.5.cloned.1.call-update
  14.9 194.7 %all-gather.3.cloned.1.call-done = bf16[16,256,4096]{2,1,0:T(8,128)(2,1)} async-done(((bf16[16,8,4096]{2,1,0:T(8,128)(2,1)}), bf16[16,256,4096]{2,1,0:T(8,128)(2,1)}) %all-gather.3.cloned.1.call-update) | async-done | bytes 33554448 | tf_op jit(solution)/shard_map/all_gather | solution.py:36
  209.6 15.6 convolution_bitcast_fusion.5
  225.6 15.6 fusion.62
  241.6 0.9 fusion.23
  242.5 2.0 copy-done.3
  244.5 0.9 fusion.22
  245.4 159.4 %all-gather.5.cloned.1.call-done = bf16[16,256,4096]{2,1,0:T(8,128)(2,1)} async-done(((bf16[16,8,4096]{2,1,0:T(8,128)(2,1)}), bf16[16,256,4096]{2,1,0:T(8,128)(2,1)}) %all-gather.5.cloned.1.call-update) | async-done | bytes 33554448 | tf_op jit(solution)/shard_map/all_gather | solution.py:63
  404.8 15.6 convolution_convert_fusion
  420.4 2.2 fusion.49
  422.6 15.4 convolution_convert_fusion.1
  438.0 1.4 fusion.5
  439.4 1.5 fusion.40
  441.0 0.8 fusion.66
  442.2 1.3 fusion.70
  443.6 1.3 subtract_convert_fusion
  444.9 25.0 %fusion.15 = f32[16,256,512]{2,1,0:T(8,128)} fusion(bf16[16,256,4096]{2,1,0:T(8,128)(2,1)} %all-gather.3.cloned.1.call-done, bf16[4096,512]{1,0:T(8,128)(2,1)S(1)} %copy-done.31), kind=kOutput, calls=%fused_computation.31 | convolution fusion | flops 17179869184 | bytes 46137344 | tf_op jit(solution)/shard_map/bld,df->blf/dot_general | solution.py:54
  469.9 24.5 %fusion.19 = f32[16,256,512]{2,1,0:T(8,128)} fusion(bf16[16,256,4096]{2,1,0:T(8,128)(2,1)} %all-gather.3.cloned.1.call-done, bf16[4096,512]{1,0:T(8,128)(2,1)S(1)} %copy-done.30), kind=kOutput, calls=%fused_computation.35 | convolution fusion | flops 17179869184 | bytes 46137344 | tf_op jit(solution)/shard_map/bld,df->blf/dot_general | solution.py:53
  494.4 29.6 %multiply_convert_fusion = (bf16[16,256,512]{2,1,0:T(8,128)(2,1)}, bf16[16,256,512]{2,1,0:T(8,128)(2,1)}, bf16[16,256,512]{2,1,0:T(8,128)(2,1)}) fusion(f32[16,256,512]{2,1,0:T(8,128)} %fusion.19, f32[16,256,512]{2,1,0:T(8,128)} %fusion.15, bf16[16,256,4096]{2,1,0:T(8,128)(2,1)} %all-gather.5.cloned.1.call-done, bf16[512,4096]{1,0:T(8,128)(2,1)} %param.19), kind=kOutput, calls=%fused_computation.5 | convolution fusion | flops 17211326464 | bytes 67108864 | tf_op jit(solution)/shard_map/bld,fd->blf/dot_general | solution.py:64
  524.0 30.2 %fusion.17 = f32[16,256,4096]{2,1,0:T(8,128)} fusion(bf16[16,256,512]{2,1,0:T(8,128)(2,1)} %get-tuple-element.17, bf16[4096,512]{1,0:T(8,128)(2,1)} %param.17), kind=kOutput, calls=%fused_computation.33 | convolution fusion | flops 17179869184 | bytes 75497472 | tf_op jit(solution)/shard_map/blf,df->bld/dot_general | solution.py:86
  554.2 30.5 %fusion.13 = f32[16,256,4096]{2,1,0:T(8,128)} fusion(bf16[16,256,512]{2,1,0:T(8,128)(2,1)} %get-tuple-element.16, bf16[4096,512]{1,0:T(8,128)(2,1)} %param.18), kind=kOutput, calls=%fused_computation.29 | convolution fusion | flops 17179869184 | bytes 75497472 | tf_op jit(solution)/shard_map/blf,df->bld/dot_general | solution.py:87
  584.7 23.1 %fusion.60 = f32[16,256,4096]{2,1,0:T(8,128)} fusion(bf16[4096,128]{1,0:T(8,128)(2,1)S(1)} %copy-done, bf16[16,256,64]{1,2,0:T(8,128)(2,1)S(1)} %copy-done.13, bf16[16,256,64]{1,2,0:T(8,128)(2,1)S(1)} %copy-done.11), kind=kOutput, calls=%fused_computation.86 | convolution fusion | flops 4297064448 | bytes 69206016 | tf_op jit(solution)/shard_map/blk,dk->bld/dot_general | solution.py:89
  607.8 23.1 %fusion.55 = f32[16,256,4096]{2,1,0:T(8,128)} fusion(bf16[4096,1,128]{2,0,1:T(8,128)(2,1)S(1)} %copy-done.6, bf16[16,256,64]{1,2,0:T(8,128)(2,1)S(1)} %copy-done.9, bf16[16,256,64]{1,2,0:T(8,128)(2,1)S(1)} %copy-done.7), kind=kOutput, calls=%fused_computation.81 | convolution fusion | flops 4297064448 | bytes 69206016 | tf_op jit(solution)/shard_map/blnk,dnk->bld/dot_general | solution.py:88
  630.9 92.1 %fusion.87 = bf16[32,8,16,4096]{3,1,0,2:T(8,128)(2,1)} fusion(bf16[16,256,128]{2,1,0:T(8,128)(2,1)S(1)} %copy-done.18, bf16[4096,128]{1,0:T(8,128)(2,1)S(1)} %copy-done.16, f32[16,256,4096]{2,1,0:T(8,128)} %fusion.60, f32[16,256,4096]{2,1,0:T(8,128)} %fusion.55, f32[16,256,4096]{2,1,0:T(8,128)} %fusion.17, f32[16,256,4096]{2,1,0:T(8,128)} %fusion.13), kind=kOutput, calls=%fused_computation.124 | convolution fusion | flops 4378853376 | bytes 304087040 | tf_op jit(solution)/shard_map/blk,dk->bld/dot_general | solution.py:90
  723.0 22.9 %copy.70 = bf16[32,8,16,4096]{3,1,2,0:T(8,128)(2,1)} copy(bf16[32,8,16,4096]{3,1,0,2:T(8,128)(2,1)} %fusion.87) | data formatting | bytes 67108864
  746.1 0.7 copy-done.20
  746.8 3.8 fusion.52
  750.7 30.6 %fusion.11 = f32[16,256,4096]{2,1,0:T(8,128)} fusion(bf16[16,256,512]{2,1,0:T(8,128)(2,1)} %get-tuple-element.18, bf16[512,4096]{1,0:T(8,128)(2,1)} %param.19), kind=kOutput, calls=%fused_computation.27 | convolution fusion | flops 17179869184 | bytes 75497472 | tf_op jit(solution)/shard_map/blf,fd->bld/dot_general | solution.py:58
  781.2 32.6 %fusion.84 = bf16[32,8,16,4096]{3,1,0,2:T(8,128)(2,1)} fusion(f32[16,256,4096]{2,1,0:T(8,128)} %fusion.11, bf16[16,256,128]{1,2,0:T(8,128)(2,1)S(1)} %fusion.52, bf16[1,128,4096]{2,1,0:T(8,128)(2,1)S(1)} %copy-done.17), kind=kOutput, calls=%fused_computation.123 | convolution fusion | flops 4328521728 | bytes 102760448 | tf_op jit(solution)/shard_map/crol,ole->cre/dot_general | solution.py:52
  813.8 22.7 %copy.68 = bf16[32,8,16,4096]{3,1,2,0:T(8,128)(2,1)} copy(bf16[32,8,16,4096]{3,1,0,2:T(8,128)(2,1)} %fusion.84) | data formatting | bytes 67108864
  836.6 16.6 %convolution_bitcast_fusion.1 = f32[4096,128]{1,0:T(8,128)} fusion(bf16[16,256,4096]{2,1,0:T(8,128)(2,1)} %all-gather.3.cloned.1.call-done, bf16[16,256,128]{2,1,0:T(8,128)(2,1)S(1)} %copy-done.18), kind=kOutput, calls=%fused_computation.11 | convolution fusion | flops 4294967296 | bytes 36700160 | tf_op jit(solution)/shard_map/bld,blk->dk/dot_general | solution.py:83
  853.2 16.6 %convolution_bitcast_fusion.2 = f32[4096,128]{1,0:T(8,128)} fusion(bf16[16,256,4096]{2,1,0:T(8,128)(2,1)} %all-gather.3.cloned.1.call-done, bf16[16,256,64]{1,2,0:T(8,128)(2,1)S(1)} %copy-done.14, bf16[16,256,64]{1,2,0:T(8,128)(2,1)S(1)} %copy-done.12), kind=kOutput, calls=%fused_computation.12 | convolution fusion | flops 4297064448 | bytes 36700160 | tf_op jit(solution)/shard_map/bld,blk->dk/dot_general | solution.py:82
  869.8 14.1 fusion.4
  883.9 16.6 %fusion.3 = bf16[4096,1,128]{2,0,1:T(8,128)(2,1)} fusion(bf16[16,256,4096]{2,1,0:T(8,128)(2,1)} %all-gather.3.cloned.1.call-done, bf16[16,256,64]{1,2,0:T(8,128)(2,1)S(1)} %copy-done.10, bf16[16,256,64]{1,2,0:T(8,128)(2,1)S(1)} %copy-done.8), kind=kOutput, calls=%fused_computation.16 | convolution fusion | flops 4297588736 | bytes 35651584 | tf_op jit(solution)/shard_map/bld,blnk->dnk/dot_general | solution.py:81
  900.5 23.2 %bitcast_convert_fusion = bf16[512,4096]{1,0:T(8,128)(2,1)} fusion(bf16[16,256,512]{2,1,0:T(8,128)(2,1)S(1)} %copy-done.33, bf16[16,256,4096]{2,1,0:T(8,128)(2,1)} %all-gather.5.cloned.1.call-done), kind=kOutput, calls=%fused_computation.2 | convolution fusion | flops 17181966336 | bytes 41943040 | tf_op jit(solution)/shard_map/blf,bld->fd/dot_general | solution.py:65
  923.8 24.3 %bitcast_convert_fusion.1 = bf16[4096,512]{1,0:T(8,128)(2,1)} fusion(bf16[16,256,4096]{2,1,0:T(8,128)(2,1)} %all-gather.3.cloned.1.call-done, bf16[16,256,512]{2,1,0:T(8,128)(2,1)S(1)} %copy-done.35), kind=kOutput, calls=%fused_computation.3 | convolution fusion | flops 17181966336 | bytes 41943040 | tf_op jit(solution)/shard_map/bld,blf->df/dot_general | solution.py:69
  948.0 24.2 %bitcast_convert_fusion.2 = bf16[4096,512]{1,0:T(8,128)(2,1)} fusion(bf16[16,256,4096]{2,1,0:T(8,128)(2,1)} %all-gather.3.cloned.1.call-done, bf16[16,256,512]{2,1,0:T(8,128)(2,1)S(1)} %copy-done.34), kind=kOutput, calls=%fused_computation.4 | convolution fusion | flops 17181966336 | bytes 41943040 | tf_op jit(solution)/shard_map/bld,blf->df/dot_general | solution.py:68
  972.3 127.5 %reduce-scatter.9.cloned.1.call-done = bf16[8,65536]{1,0:T(8,128)(2,1)} async-done(((bf16[256,65536]{1,0:T(8,128)(2,1)}), bf16[8,65536]{1,0:T(8,128)(2,1)}) %reduce-scatter.9.cloned.1.call-update) | async-done | bytes 1048592
  1099.8 1.8 copy.81
  1101.6 1.9 fusion.38
  1103.5 360.3 %reduce-scatter.7.cloned.1.call-done = bf16[8,65536]{1,0:T(8,128)(2,1)} async-done(((bf16[256,65536]{1,0:T(8,128)(2,1)}), bf16[8,65536]{1,0:T(8,128)(2,1)}) %reduce-scatter.7.cloned.1.call-update) | async-done | bytes 1048592
  1463.9 2.8 copy.82
  1466.7 101.8 %all-reduce.2 = (f32[4096]{0:T(1024)}, bf16[4096,128]{1,0:T(8,128)(2,1)}, bf16[4096,128]{1,0:T(8,128)(2,1)}) all-reduce(f32[4096]{0:T(1024)S(1)} %get-tuple-element.10, f32[4096,128]{1,0:T(8,128)} %convolution_bitcast_fusion.2, f32[4096,128]{1,0:T(8,128)} %convolution_bitcast_fusion.1), channel_id=1, replica_groups=mesh['tp'=32] {'tp'}, use_global_device_ids=true, to_apply=%region_10.11 | all-reduce | flops 1052672 | bytes 6324224 | tf_op jit(solution)/shard_map/psum | solution.py:93
  1568.5 4.8 fusion.35
  (85 shorter events, 1.9 us)
Async XLA Ops:
  7.2 218.4 %copy-start = (bf16[4096,128]{1,0:T(8,128)(2,1)S(1)}, bf16[4096,128]{1,0:T(8,128)(2,1)}, u32[]{:S(2)}) copy-start(bf16[4096,128]{1,0:T(8,128)(2,1)} %param.14) | copy-start | bytes 3145732
  7.2 202.4 %copy-start.5 = (bf16[4096,1,128]{2,0,1:T(8,128)(2,1)S(1)}, bf16[4096,1,128]{2,0,1:T(8,128)(2,1)}, u32[]{:S(2)}) copy-start(bf16[4096,1,128]{2,0,1:T(8,128)(2,1)} %param.13) | copy-start | bytes 3145732
  7.2 202.4 %all-gather.3.cloned.1.call-start = ((), (), s32[]{:S(2)}) async-start(), calls=%async_computation.2 | async-start | bytes 34603008 | tf_op jit(solution)/shard_map/all_gather | solution.py:36
  8.8 1.7 copy-start.21
  10.5 0.6 copy-start.24
  13.7 391.1 %all-gather.5.cloned.1.call-start = ((), (), s32[]{:S(2)}) async-start(), calls=%async_computation.3 | async-start | bytes 34603008 | tf_op jit(solution)/shard_map/all_gather | solution.py:63
  14.5 1085.3 %reduce-scatter.9.cloned.1.call-start = ((), (), s32[]{:S(2)}) async-start(), calls=%async_computation.5 | async-start | bytes 34603008
  14.6 424.8 %copy-start.19 = (pred[256,256]{0,1:T(8,128)(4,1)}, pred[256,256]{0,1:T(8,128)(4,1)S(1)}, u32[]{:S(2)}) copy-start(pred[256,256]{0,1:T(8,128)(4,1)S(1)} %iota_compare_fusion) | copy-start | bytes 196612
  242.5 2.0 copy-start.3
  242.5 196.9 %copy-start.26 = (f32[16,256]{1,0:T(8,128)}, f32[16,256]{1,0:T(8,128)S(1)}, u32[]{:S(2)}) copy-start(f32[16,256]{1,0:T(8,128)S(1)} %get-tuple-element.32) | copy-start | bytes 49156
  245.4 194.0 %copy-start.28 = (f32[16,256]{1,0:T(8,128)}, f32[16,256]{1,0:T(8,128)S(1)}, u32[]{:S(2)}) copy-start(f32[16,256]{1,0:T(8,128)S(1)} %fusion.22) | copy-start | bytes 49156
  404.8 15.6 copy-start.4
  420.4 2.2 copy-start.15
  438.0 1.4 copy-start.32
  442.2 2.6 copy-start.31
  444.9 25.0 %copy-start.30 = (bf16[4096,512]{1,0:T(8,128)(2,1)S(1)}, bf16[4096,512]{1,0:T(8,128)(2,1)}, u32[]{:S(2)}) copy-start(bf16[4096,512]{1,0:T(8,128)(2,1)} %param.17) | copy-start | bytes 12582916
  554.1 30.5 %copy-start.11 = (bf16[16,256,64]{1,2,0:T(8,128)(2,1)S(1)}, bf16[16,256,64]{1,2,0:T(8,128)(2,1)}, u32[]{:S(2)}) copy-start(bf16[16,256,64]{1,2,0:T(8,128)(2,1)} %get-tuple-element.21) | copy-start | bytes 1572868
  554.1 30.5 %copy-start.13 = (bf16[16,256,64]{1,2,0:T(8,128)(2,1)S(1)}, bf16[16,256,64]{1,2,0:T(8,128)(2,1)}, u32[]{:S(2)}) copy-start(bf16[16,256,64]{1,2,0:T(8,128)(2,1)} %get-tuple-element.22) | copy-start | bytes 1572868
  584.6 23.1 %copy-start.6 = (bf16[4096,1,128]{2,0,1:T(8,128)(2,1)S(1)}, bf16[4096,1,128]{2,0,1:T(8,128)(2,1)}, u32[]{:S(2)}) copy-start(bf16[4096,1,128]{2,0,1:T(8,128)(2,1)} %param.13) | copy-start | bytes 3145732
  584.6 23.1 %copy-start.7 = (bf16[16,256,64]{1,2,0:T(8,128)(2,1)S(1)}, bf16[16,256,64]{1,2,0:T(8,128)(2,1)}, u32[]{:S(2)}) copy-start(bf16[16,256,64]{1,2,0:T(8,128)(2,1)} %get-tuple-element.19) | copy-start | bytes 1572868
  584.6 23.1 %copy-start.9 = (bf16[16,256,64]{1,2,0:T(8,128)(2,1)S(1)}, bf16[16,256,64]{1,2,0:T(8,128)(2,1)}, u32[]{:S(2)}) copy-start(bf16[16,256,64]{1,2,0:T(8,128)(2,1)} %get-tuple-element.20) | copy-start | bytes 1572868
  607.8 23.2 %copy-start.16 = (bf16[4096,128]{1,0:T(8,128)(2,1)S(1)}, bf16[4096,128]{1,0:T(8,128)(2,1)}, u32[]{:S(2)}) copy-start(bf16[4096,128]{1,0:T(8,128)(2,1)} %param.15) | copy-start | bytes 3145732
  607.8 23.1 %copy-start.18 = (bf16[16,256,128]{2,1,0:T(8,128)(2,1)S(1)}, bf16[16,256,128]{2,1,0:T(8,128)(2,1)}, u32[]{:S(2)}) copy-start(bf16[16,256,128]{2,1,0:T(8,128)(2,1)} %fusion.49) | copy-start | bytes 3145732
  746.0 0.8 copy-start.20
  746.0 0.8 copy-start.27
  746.0 0.8 copy-start.29
  746.0 717.9 %reduce-scatter.7.cloned.1.call-start = ((), (), s32[]{:S(2)}) async-start(), calls=%async_computation.4 | async-start | bytes 34603008
  750.6 30.6 %copy-start.17 = (bf16[1,128,4096]{2,1,0:T(8,128)(2,1)S(1)}, bf16[1,128,4096]{2,1,0:T(8,128)(2,1)}, u32[]{:S(2)}) copy-start(bf16[1,128,4096]{2,1,0:T(8,128)(2,1)} %param.16) | copy-start | bytes 3145732
  836.6 16.6 %copy-start.12 = (bf16[16,256,64]{1,2,0:T(8,128)(2,1)S(1)}, bf16[16,256,64]{1,2,0:T(8,128)(2,1)}, u32[]{:S(2)}) copy-start(bf16[16,256,64]{1,2,0:T(8,128)(2,1)} %get-tuple-element.21) | copy-start | bytes 1572868
  836.6 16.6 %copy-start.14 = (bf16[16,256,64]{1,2,0:T(8,128)(2,1)S(1)}, bf16[16,256,64]{1,2,0:T(8,128)(2,1)}, u32[]{:S(2)}) copy-start(bf16[16,256,64]{1,2,0:T(8,128)(2,1)} %get-tuple-element.22) | copy-start | bytes 1572868
  869.8 14.1 copy-start.8
  869.8 14.1 copy-start.10
  883.9 16.6 %copy-start.33 = (bf16[16,256,512]{2,1,0:T(8,128)(2,1)S(1)}, bf16[16,256,512]{2,1,0:T(8,128)(2,1)}, u32[]{:S(2)}) copy-start(bf16[16,256,512]{2,1,0:T(8,128)(2,1)} %get-tuple-element.18) | copy-start | bytes 12582916
  900.5 23.2 %copy-start.35 = (bf16[16,256,512]{2,1,0:T(8,128)(2,1)S(1)}, bf16[16,256,512]{2,1,0:T(8,128)(2,1)}, u32[]{:S(2)}) copy-start(bf16[16,256,512]{2,1,0:T(8,128)(2,1)} %get-tuple-element.16) | copy-start | bytes 12582916
  923.8 24.3 %copy-start.34 = (bf16[16,256,512]{2,1,0:T(8,128)(2,1)S(1)}, bf16[16,256,512]{2,1,0:T(8,128)(2,1)}, u32[]{:S(2)}) copy-start(bf16[16,256,512]{2,1,0:T(8,128)(2,1)} %get-tuple-element.17) | copy-start | bytes 12582916
  948.0 153.6 %copy-start.2 = (bf16[16,8,4096]{2,1,0:T(8,128)(2,1)S(1)}, bf16[16,8,4096]{2,1,0:T(8,128)(2,1)}, u32[]{:S(2)}) copy-start(bf16[16,8,4096]{2,1,0:T(8,128)(2,1)} %param.10) | copy-start | bytes 3145732
  948.0 153.6 %copy-start.22 = (f32[16,8]{1,0:T(8,128)S(1)}, f32[16,8]{1,0:T(8,128)}, u32[]{:S(2)}) copy-start(f32[16,8]{1,0:T(8,128)} %copy-done.21) | copy-start | bytes 1540
  948.0 153.6 %copy-start.23 = (f32[4096]{0:T(1024)S(1)}, f32[4096]{0:T(1024)}, u32[]{:S(2)}) copy-start(f32[4096]{0:T(1024)} %param.12) | copy-start | bytes 49156
  948.0 153.6 %copy-start.25 = (f32[16,8]{1,0:T(8,128)S(1)}, f32[16,8]{1,0:T(8,128)}, u32[]{:S(2)}) copy-start(f32[16,8]{1,0:T(8,128)} %copy-done.24) | copy-start | bytes 1540
  1466.7 106.6 %copy-start.1 = (bf16[4096,128]{1,0:T(8,128)(2,1)S(1)}, bf16[4096,128]{1,0:T(8,128)(2,1)}, u32[]{:S(2)}) copy-start(bf16[4096,128]{1,0:T(8,128)(2,1)} %param.14) | copy-start | bytes 3145732
Sparse Core Ops, SparseCore 0:
  13.9 195.7 all-gather.2
  212.5 192.2 all-gather.4
  746.1 353.6 reduce-scatter.8
  1101.9 361.8 reduce-scatter.6
where the time goes:
time: 1590 us; the launch traced here: 1580 us
  waiting for transfers between devices  843 us (53%)
  matrix products  549 us (35%)
  blocking collectives  102 us (6%)
  local copies, waits for them, and re-layouts  53.8 us (3%)
  other arithmetic  18.7 us (1%)
    unnamed x6, waiting for transfers between devices  489 us
    all_gather x1, waiting for transfers between devices, layer_shard(): normed = lax.all_gather(normed_loc, 'tp', axis=1, tiled=True)  195 us
    all_gather x1, waiting for transfers between devices, layer_shard(): grad_full = lax.all_gather(grad_y_loc, 'tp', axis=1, tiled=True)  159 us
    psum x1, blocking collectives, layer_shard(): grad_gain = lax.psum(jnp.sum(grad_normed_loc * x_hat, axis=(0, 1)), 'tp')  102 us
    dot_general x1, matrix products, layer_shard(): jnp.einsum('blk,dk->bld', grad_values, w_value, preferred_element_type=jn...  92.1 us
    unnamed x76, local copies, waits for them, and re-layouts  53.8 us
    dot_general x1, matrix products, layer_shard(): jnp.einsum('crol,ole->cre', attn_heads, w_out, preferred_element_type=jnp...  32.6 us
  transfers between devices with their start and end apart: 4, of which 4 were waited for; matrix products, arithmetic and copies ran while one was open for 17% of the time, Pallas kernels for 0%

commit v1 on v0

v1 whole, which is shorter than its diff:
```python
import functools

import jax
import jax.numpy as jnp
from jax import lax
from jax.experimental import pallas as pl
from jax.experimental.pallas import tpu as pltpu
from jax.sharding import PartitionSpec as P

LN_EPS = 1e-6
ROPE_BASE = 10000.0
MESH = pl.DeviceIdType.MESH
F32 = jnp.float32
BF16 = jnp.bfloat16

GROUP = 8
SEQ = 256
DIM = 4096
HALF = DIM // 2
HEAD = 128
FFN = 512
OWN = 2 * FFN + HEAD
KEY = 2 * OWN
NCAT = 2 * OWN + 2 * HEAD
NZO = 2 * (FFN + HEAD)
QCOL = (2 * FFN, OWN + 2 * FFN)
OCOL = (2 * FFN, 2 * FFN + HEAD)


def dims():
    i = lax.axis_index("tp")
    return lax.div(i, 8), lax.rem(lax.div(i, 4), 2), lax.rem(lax.div(i, 2), 2), lax.rem(i, 2)


def index(z, y, x, core):
    return ((z * 2 + y) * 2 + x) * 2 + core


def rows8(start, size):
    return pl.ds(pl.multiple_of(start, 8), size)


def rows16(start, size):
    return pl.ds(pl.multiple_of(start, 16), size)


def lanes(start, size):
    return pl.ds(pl.multiple_of(start, 128), size)


def remote(src, dst, send, recv, target):
    return pltpu.make_async_remote_copy(src, dst, send, recv, device_id=(target,), device_id_type=MESH)


def entry_barrier(partners):
    barrier = pltpu.get_barrier_semaphore()
    for partner in partners:
        pl.semaphore_signal(barrier, inc=1, device_id=(partner,), device_id_type=MESH)
    pl.semaphore_wait(barrier, len(partners))


def dot_nt(a, b):
    return lax.dot_general(a, b, (((1,), (1,)), ((), ())), preferred_element_type=F32)


def dot_tn(a, b):
    return lax.dot_general(a, b, (((0,), (0,)), ((), ())), preferred_element_type=F32)


def dot_nn(a, b):
    return jnp.dot(a, b, preferred_element_type=F32)


def row_position(r):
    return ((r // 16) % 4) * 64 + (r // 128) * 32 + ((r // 64) % 2) * 16 + r % 16


def gather_kernel(
    h_loc, dy_loc, w1, w3, wq, wk, wv, w2, wo, cos_t, sin_t,
    h_all, dy_all, h_sib, dy_sib, y_part, dh_part, g_all, zo_all, g_sib, zo_sib,
    wcat, w2o, hv, dyv, proj, zo, g, yo, dho, probs, qs, stage,
    s1, r1, s2, r2, s3, r3, sx, rx, sw, rw, ss, rs, sg, rg, lsem, wsem, osem, gsem,
):
    z, y, x, core = dims()
    sib = index(z, y, x, 1 - core)
    xn = index(z, y, 1 - x, core)
    yn = index(z, 1 - y, x, core)
    zn = [index(lax.rem(z + k, 4), y, x, core) for k in (1, 2, 3)]
    entry_barrier([sib, xn, yn] + zn)
    row0 = (y * 2 + x) * 64 + z * 16
    full = ((h_loc, h_all, h_sib), (dy_loc, dy_all, dy_sib))

    swaps = []
    for s, (loc, out, _) in enumerate(full):
        swaps.append(remote(loc.at[rows8(8 * (1 - core), 8)], out.at[:, rows8(row0 + 8 * core, 8), :], sx.at[s], rx.at[s], sib))
    for c in swaps:
        c.start()
    takes = [pltpu.make_async_copy(loc.at[rows8(8 * core, 8)], stage.at[s], lsem.at[s]) for s, (loc, _, _) in enumerate(full)]
    for c in takes:
        c.start()
    puts = []
    for s, (_, out, _) in enumerate(full):
        takes[s].wait()
        c = pltpu.make_async_copy(stage.at[s], out.at[:, rows8(row0 + 8 * core, 8), :], lsem.at[s])
        c.start()
        puts.append(c)
    for c in puts:
        c.wait()
    for c in swaps:
        c.wait_recv()

    def p1(b, s):
        out = full[s][1]
        block = out.at[b, rows16(row0, 16), :]
        return [remote(block, block, s1.at[b, s, k], r1.at[b, s, k], zn[k]) for k in range(3)]

    def p2(b, s):
        out = full[s][1]
        rows = rows16((y * 2 + x) * 64, 64)
        left = out.at[b, rows, 0:HALF]
        right = out.at[b, rows, HALF:DIM]
        return [remote(left, left, s2.at[b, s, 0], r2.at[b, s, 0], yn), remote(right, right, s2.at[b, s, 1], r2.at[b, s, 1], xn)]

    def p3(b, s):
        out = full[s][1]
        copies = []
        for k in range(2):
            left = out.at[b, rows16((k * 2 + x) * 64, 64), 0:HALF]
            copies.append(remote(left, left, s3.at[b, s, k], r3.at[b, s, k], xn))
        right = out.at[b, rows16(y * 128, 128), HALF:DIM]
        copies.append(remote(right, right, s3.at[b, s, 2], r3.at[b, s, 2], yn))
        return copies

    def start(copies):
        for c in copies:
            c.start()

    def wait_recv(copies):
        for c in copies:
            c.wait_recv()

    def step2(b, s):
        wait_recv(p1(b, s))
        start(p2(b, s))

    def step3(b, s):
        wait_recv(p2(b, s))
        start(p3(b, s))

    for b in range(2):
        for s in range(2):
            start(p1(b, s))

    pieces = ((w1, 0, FFN), (w3, FFN, FFN), (wq, 2 * FFN, HEAD))
    local = []
    for k, (w, col, width) in enumerate(pieces):
        local.append(pltpu.make_async_copy(w, wcat.at[:, col : col + width], wsem.at[k]))
    local.append(pltpu.make_async_copy(wk, wcat.at[:, KEY : KEY + HEAD], wsem.at[3]))
    local.append(pltpu.make_async_copy(wv, wcat.at[:, KEY + HEAD : NCAT], wsem.at[4]))
    local.append(pltpu.make_async_copy(w2, w2o.at[0:FFN], wsem.at[5]))
    local.append(pltpu.make_async_copy(wo, w2o.at[2 * FFN : 2 * FFN + HEAD], wsem.at[6]))
    far = []
    for k, (w, col, width) in enumerate(pieces):
        far.append(remote(w, wcat.at[:, OWN + col : OWN + col + width], sw.at[k], rw.at[k], sib))
    far.append(remote(w2, w2o.at[FFN : 2 * FFN], sw.at[3], rw.at[3], sib))
    far.append(remote(wo, w2o.at[2 * FFN + HEAD : NZO], sw.at[4], rw.at[4], sib))
    start(local)
    start(far)

    for b in range(2):
        for s in range(2):
            start(p1(b + 2, s))
            step2(b, s)
            if b == 0:
                step3(b, s)
    for c in local:
        c.wait()
    wait_recv(far)

    def sib_copies(b):
        copies = [remote(out.at[b], far_out.at[b], ss.at[b, s], rs.at[b, s], sib) for s, (_, out, far_out) in enumerate(full)]
        return copies

    def gz_copies(b):
        return [
            remote(g.at[:, OWN : 2 * OWN], g_sib.at[b], sg.at[b, 0], rg.at[b, 0], sib),
            remote(zo.at[:, FFN : 2 * FFN], zo_sib.at[b, :, 0:FFN], sg.at[b, 1], rg.at[b, 1], sib),
            remote(zo.at[:, OCOL[1] : NZO], zo_sib.at[b, :, FFN : FFN + HEAD], sg.at[b, 2], rg.at[b, 2], sib),
        ]

    def gz_local(b):
        return [pltpu.make_async_copy(g, g_all.at[b], gsem.at[0]), pltpu.make_async_copy(zo, zo_all.at[b], gsem.at[1])]

    y_out = lambda b: pltpu.make_async_copy(yo, y_part.at[b], osem.at[0])
    dh_out = lambda b: pltpu.make_async_copy(dho, dh_part.at[b], osem.at[1])
    scale = HEAD ** -0.5

    def rotate(v, sign):
        return v * cos_t[...] + sign * (pltpu.roll(v, HEAD // 2, 1) * sin_t[...])

    def batch_step(b, carry):
        wait_recv(p3(b, 0))
        load_h = pltpu.make_async_copy(h_all.at[b], hv, lsem.at[0])
        load_h.start()

        @pl.when(b < GROUP - 1)
        def _():
            step3(b + 1, 0)

        @pl.when(b < GROUP - 2)
        def _():
            step2(b + 2, 0)

        wait_recv(p3(b, 1))
        load_dy = pltpu.make_async_copy(dy_all.at[b], dyv, lsem.at[1])
        load_dy.start()
        start(sib_copies(b))
        load_h.wait()

        def proj_tile(t, c):
            proj[:, lanes(t * 512, 512)] = dot_nn(hv[...], wcat[:, lanes(t * 512, 512)])
            return c

        lax.fori_loop(0, NCAT // 512, proj_tile, 0)

        @pl.when(b < GROUP - 1)
        def _():
            step3(b + 1, 1)

        @pl.when(b < GROUP - 2)
        def _():
            step2(b + 2, 1)

        @pl.when(b < GROUP - 4)
        def _():
            for s in range(2):
                start(p1(b + 4, s))

        @pl.when(b > 0)
        def _():
            for c in gz_local(b - 1):
                c.wait()
            for c in gz_copies(b - 1):
                c.wait_send()
            y_out(b - 1).wait()
            dh_out(b - 1).wait()

        def hidden_tile(t, c):
            at = t * 256 + lax.div(t, 2) * (OWN - FFN)
            gate = proj[:, lanes(at, 256)]
            up = proj[:, lanes(at + FFN, 256)]
            zo[:, lanes(t * 256, 256)] = (gate * jax.nn.sigmoid(gate) * up).astype(BF16)
            return c

        lax.fori_loop(0, 4, hidden_tile, 0)

        keys = rotate(proj[:, KEY : KEY + HEAD], 1.0).astype(BF16)
        vals = proj[:, KEY + HEAD : NCAT].astype(BF16)
        qs[2] = keys
        qs[3] = vals
        q_pos = row_position(lax.broadcasted_iota(jnp.int32, (SEQ, SEQ), 0))
        k_pos = row_position(lax.broadcasted_iota(jnp.int32, (SEQ, SEQ), 1))
        causal = q_pos >= k_pos
        for hd in range(2):
            query = rotate(proj[:, QCOL[hd] : QCOL[hd] + HEAD], 1.0).astype(BF16)
            qs[hd] = query
            scores = jnp.where(causal, dot_nt(query, keys) * scale, -1e30)
            e = jnp.exp(scores - jnp.max(scores, axis=-1, keepdims=True))
            p = e / jnp.sum(e, axis=-1, keepdims=True)
            probs[hd] = p
            zo[:, OCOL[hd] : OCOL[hd] + HEAD] = dot_nn(p.astype(BF16), vals).astype(BF16)

        def y_tile(n, c):
            yo[:, lanes(n * 512, 512)] = dot_nn(zo[...], w2o[:, lanes(n * 512, 512)]).astype(BF16)
            return c

        lax.fori_loop(0, DIM // 512, y_tile, 0)
        y_out(b).start()
        load_dy.wait()

        def dz_tile(t, c):
            dz = dot_nt(dyv[...], w2o[rows16(t * 256, 256), :])
            at = t * 256 + lax.div(t, 2) * (OWN - FFN)
            gate = proj[:, lanes(at, 256)]
            up = proj[:, lanes(at + FFN, 256)]
            sig = jax.nn.sigmoid(gate)
            g[:, lanes(at, 256)] = (dz * up * sig * (1.0 + gate * (1.0 - sig))).astype(BF16)
            g[:, lanes(at + FFN, 256)] = (dz * (gate * sig)).astype(BF16)
            return c

        lax.fori_loop(0, 4, dz_tile, 0)
        d_heads = dot_nt(dyv[...], w2o[2 * FFN : NZO, :]).astype(BF16)
        d_keys = jnp.zeros((SEQ, HEAD), F32)
        d_vals = jnp.zeros((SEQ, HEAD), F32)
        for hd in range(2):
            d_out = d_heads[:, hd * HEAD : (hd + 1) * HEAD]
            p = probs[hd]
            d_probs = dot_nt(d_out, qs[3])
            d_vals = d_vals + dot_tn(p.astype(BF16), d_out)
            row_dot = jnp.sum(p * d_probs, axis=-1, keepdims=True)
            d_scores = (p * (d_probs - row_dot) * scale).astype(BF16)
            g[:, QCOL[hd] : QCOL[hd] + HEAD] = rotate(dot_nn(d_scores, qs[2]), -1.0).astype(BF16)
            d_keys = d_keys + dot_tn(d_scores, qs[hd])
        g[:, KEY : KEY + HEAD] = rotate(d_keys, -1.0).astype(BF16)
        g[:, KEY + HEAD : NCAT] = d_vals.astype(BF16)

        def dh_tile(n, c):
            dho[:, lanes(n * 512, 512)] = dot_nt(g[...], wcat[rows16(n * 512, 512), :]).astype(BF16)
            return c

        lax.fori_loop(0, DIM // 512, dh_tile, 0)
        dh_out(b).start()
        start(gz_local(b))
        start(gz_copies(b))
        return carry

    lax.fori_loop(0, GROUP, batch_step, 0)

    last = GROUP - 1
    for c in gz_local(last):
        c.wait()
    y_out(last).wait()
    dh_out(last).wait()
    for c in gz_copies(last):
        c.wait_send()

    def finish(b, carry):
        for s in range(2):
            for c in p1(b, s) + p2(b, s) + p3(b, s):
                c.wait_send()
        for c in sib_copies(b):
            c.wait()
        wait_recv(gz_copies(b))
        return carry

    lax.fori_loop(0, GROUP, finish, 0)
    for c in swaps:
        c.wait_send()
    for c in far:
        c.wait_send()


def gather_call(h_loc, dy_loc, w1, w3, wq, wk, wv, w2, wo, cos_t, sin_t):
    any_spec = pl.BlockSpec(memory_space=pl.ANY)
    vmem_spec = pl.BlockSpec(memory_space=pltpu.VMEM)
    dma = pltpu.SemaphoreType.DMA
    shapes = [(GROUP, SEQ, DIM)] * 6 + [(GROUP, SEQ, NCAT), (GROUP, SEQ, NZO), (GROUP, SEQ, OWN), (GROUP, SEQ, FFN + HEAD)]
    return pl.pallas_call(
        gather_kernel,
        out_shape=[jax.ShapeDtypeStruct(s, BF16) for s in shapes],
        in_specs=[any_spec] * 9 + [vmem_spec] * 2,
        out_specs=[any_spec] * len(shapes),
        scratch_shapes=[
            pltpu.VMEM((DIM, NCAT), BF16),
            pltpu.VMEM((NZO, DIM), BF16),
            pltpu.VMEM((SEQ, DIM), BF16),
            pltpu.VMEM((SEQ, DIM), BF16),
            pltpu.VMEM((SEQ, NCAT), F32),
            pltpu.VMEM((SEQ, NZO), BF16),
            pltpu.VMEM((SEQ, NCAT), BF16),
            pltpu.VMEM((SEQ, DIM), BF16),
            pltpu.VMEM((SEQ, DIM), BF16),
            pltpu.VMEM((2, SEQ, SEQ), F32),
            pltpu.VMEM((4, SEQ, HEAD), BF16),
            pltpu.VMEM((2, 8, 8, DIM), BF16),
            dma((GROUP, 2, 3)), dma((GROUP, 2, 3)),
            dma((GROUP, 2, 2)), dma((GROUP, 2, 2)),
            dma((GROUP, 2, 3)), dma((GROUP, 2, 3)),
            dma((2,)), dma((2,)),
            dma((5,)), dma((5,)),
            dma((GROUP, 2)), dma((GROUP, 2)),
            dma((GROUP, 3)), dma((GROUP, 3)),
            dma((2,)), dma((7,)), dma((2,)), dma((2,)),
        ],
        compiler_params=pltpu.CompilerParams(collective_id=0, has_side_effects=True, vmem_limit_bytes=60 * 1024 * 1024),
        name="gather_layer",
    )(h_loc, dy_loc, w1, w3, wq, wk, wv, w2, wo, cos_t, sin_t)


ITEMS = 2 * GROUP


def scatter_kernel(y_part, dh_part, y_sum, dh_sum, b1, b2, b3, own, fin, s1, r1, s2, r2, s3, r3, osem, fsem, ssem, rsem):
    z, y, x, core = dims()
    sib = index(z, y, x, 1 - core)
    xn = index(z, y, 1 - x, core)
    yn = index(z, 1 - y, x, core)
    zn = [index(lax.rem(z + k, 4), y, x, core) for k in (1, 2, 3)]
    entry_barrier([sib, xn, yn] + zn)
    parts = (y_part, dh_part)
    sums = (y_sum, dh_sum)

    def q1(b, s):
        n = 2 * b + s
        copies = []
        for k in range(2):
            src = parts[s].at[b, rows16((k * 2 + 1 - x) * 64, 64), 0:HALF]
            copies.append(remote(src, b1.at[n, 0, k * 64 : k * 64 + 64], s1.at[n, k], r1.at[n, k], xn))
        src = parts[s].at[b, rows16((1 - y) * 128, 128), HALF:DIM]
        copies.append(remote(src, b1.at[n, 1], s1.at[n, 2], r1.at[n, 2], yn))
        return copies

    def load(b, s):
        copies = []
        for k in range(2):
            src = parts[s].at[b, rows16((k * 2 + x) * 64, 64), 0:HALF]
            copies.append(pltpu.make_async_copy(src, own.at[s, 0, k * 64 : k * 64 + 64], osem.at[s, k]))
        src = parts[s].at[b, rows16(y * 128, 128), HALF:DIM]
        copies.append(pltpu.make_async_copy(src, own.at[s, 1], osem.at[s, 2]))
        return copies

    def q2(n):
        return [
            remote(b1.at[n, 0, rows16((1 - y) * 64, 64)], b2.at[n, 0], s2.at[n, 0], r2.at[n, 0], yn),
            remote(b1.at[n, 1, rows16((1 - x) * 64, 64)], b2.at[n, 1], s2.at[n, 1], r2.at[n, 1], xn),
        ]

    def q3(n):
        copies = []
        for k in range(3):
            rows = rows16(lax.rem(z + k + 1, 4) * 16, 16)
            copies.append(remote(b2.at[n, :, rows, :], b3.at[n, k], s3.at[n, k], r3.at[n, k], zn[k]))
        return copies

    def store(b, s):
        n = 2 * b + s
        far = remote(fin.at[n, 1 - core], sums[s].at[8 * core + b], ssem.at[n], rsem.at[n], sib)
        near = pltpu.make_async_copy(fin.at[n, core], sums[s].at[8 * core + b], fsem.at[n])
        return far, near

    def start(copies):
        for c in copies:
            c.start()

    def wait_recv(copies):
        for c in copies:
            c.wait_recv()

    def add1(b, s):
        n = 2 * b + s
        wait_recv(q1(b, s))
        for c in load(b, s):
            c.wait()

        def tile(t, c):
            cols = lanes(t * 256, 256)
            for k in range(2):
                b1[n, k, :, cols] = (b1[n, k, :, cols].astype(F32) + own[s, k, :, cols].astype(F32)).astype(BF16)
            return c

        lax.fori_loop(0, HALF // 256, tile, 0)
        start(q2(n))

    def add2(n):
        wait_recv(q2(n))

        def tile(t, c):
            cols = lanes(t * 256, 256)
            mine = (rows16(y * 64, 64), rows16(x * 64, 64))
            for k in range(2):
                b2[n, k, :, cols] = (b2[n, k, :, cols].astype(F32) + b1[n, k, mine[k], cols].astype(F32)).astype(BF16)
            return c

        lax.fori_loop(0, HALF // 256, tile, 0)
        start(q3(n))

    def add3(b, s):
        n = 2 * b + s
        wait_recv(q3(n))

        def tile(t, c):
            cols = lanes(t * 256, 256)
            for k in range(2):
                total = b2[n, k, rows16(z * 16, 16), cols].astype(F32)
                for j in range(3):
                    total = total + b3[n, j, k, :, cols].astype(F32)
                fin[n, 0, :, lanes(k * HALF + t * 256, 256)] = total[0:8].astype(BF16)
                fin[n, 1, :, lanes(k * HALF + t * 256, 256)] = total[8:16].astype(BF16)
            return c

        lax.fori_loop(0, HALF // 256, tile, 0)
        start(store(b, s))

    for s in range(2):
        start(load(0, s))
    for b in range(2):
        for s in range(2):
            start(q1(b, s))

    def step(b, carry):
        for s in range(2):
            n = 2 * b + s

            @pl.when(b < GROUP)
            def _():
                add1(b, s)

            @pl.when(b < GROUP - 1)
            def _():
                start(load(b + 1, s))

            @pl.when(b < GROUP - 2)
            def _():
                start(q1(b + 2, s))

            @pl.when((n >= 1) & (n < ITEMS + 1))
            def _():
                add2(n - 1)

            @pl.when((n >= 2) & (n < ITEMS + 2))
            def _():
                add3(b - 1, s)

        return carry

    lax.fori_loop(0, GROUP + 1, step, 0)

    def finish(b, carry):
        for s in range(2):
            n = 2 * b + s
            for c in q1(b, s) + q2(n) + q3(n):
                c.wait_send()
            far, near = store(b, s)
            near.wait()
            far.wait()
        return carry

    lax.fori_loop(0, GROUP, finish, 0)


def scatter_call(y_part, dh_part):
    any_spec = pl.BlockSpec(memory_space=pl.ANY)
    dma = pltpu.SemaphoreType.DMA
    return pl.pallas_call(
        scatter_kernel,
        out_shape=[jax.ShapeDtypeStruct((2 * GROUP, 8, DIM), BF16)] * 2,
        in_specs=[any_spec] * 2,
        out_specs=[any_spec] * 2,
        scratch_shapes=[
            pltpu.VMEM((ITEMS, 2, 128, HALF), BF16),
            pltpu.VMEM((ITEMS, 2, 64, HALF), BF16),
            pltpu.VMEM((ITEMS, 3, 2, 16, HALF), BF16),
            pltpu.VMEM((2, 2, 128, HALF), BF16),
            pltpu.VMEM((ITEMS, 2, 8, DIM), BF16),
            dma((ITEMS, 3)), dma((ITEMS, 3)),
            dma((ITEMS, 2)), dma((ITEMS, 2)),
            dma((ITEMS, 3)), dma((ITEMS, 3)),
            dma((2, 3)), dma((ITEMS,)), dma((ITEMS,)), dma((ITEMS,)),
        ],
        compiler_params=pltpu.CompilerParams(collective_id=1, has_side_effects=True, vmem_limit_bytes=48 * 1024 * 1024),
        name="scatter_sums",
    )(y_part, dh_part)


def rope_tables():
    half = HEAD // 2
    inv_freq = ROPE_BASE ** (-jnp.arange(half, dtype=F32) * 2.0 / HEAD)
    pos = row_position(jnp.arange(SEQ, dtype=jnp.int32)).astype(F32)
    angles = pos[:, None] * inv_freq[None, :]
    cos, sin = jnp.cos(angles), jnp.sin(angles)
    return jnp.concatenate([cos, cos], axis=1), jnp.concatenate([-sin, sin], axis=1)


def solution(mesh):
    def layer_shard(x_loc, dy_loc, ln_gain, w_query, w_key, w_value, w_out, w_gate, w_up, w_down):
        residual = x_loc.astype(F32)
        centered = residual - jnp.mean(residual, axis=-1, keepdims=True)
        inv_std = lax.rsqrt(jnp.mean(centered * centered, axis=-1, keepdims=True) + LN_EPS)
        x_hat = centered * inv_std
        h_loc = (ln_gain * x_hat).astype(BF16)
        cos_t, sin_t = rope_tables()
        wq = w_query.reshape(DIM, HEAD)
        wo = w_out.reshape(HEAD, DIM)
        h_all, dy_all, h_sib, dy_sib, y_part, dh_part, g_all, zo_all, g_sib, zo_sib = gather_call(
            h_loc, dy_loc, w_gate, w_up, wq, w_key, w_value, w_down, wo, cos_t, sin_t
        )

        def grad_in(lo, hi):
            near = jnp.einsum("bld,blf->df", h_all, g_all[:, :, lo:hi], preferred_element_type=F32)
            return (near + jnp.einsum("bld,blf->df", h_sib, g_sib[:, :, lo:hi], preferred_element_type=F32)).astype(BF16)

        def grad_out(lo, hi, sib_lo, sib_hi):
            near = jnp.einsum("blf,bld->fd", zo_all[:, :, lo:hi], dy_all, preferred_element_type=F32)
            return (near + jnp.einsum("blf,bld->fd", zo_sib[:, :, sib_lo:sib_hi], dy_sib, preferred_element_type=F32)).astype(BF16)

        grad_w_gate = grad_in(0, FFN)
        grad_w_up = grad_in(FFN, 2 * FFN)
        grad_w_query = grad_in(2 * FFN, OWN).reshape(DIM, 1, HEAD)
        grad_w_down = grad_out(0, FFN, 0, FFN)
        grad_w_out = grad_out(OCOL[0], OCOL[0] + HEAD, FFN, FFN + HEAD).reshape(1, HEAD, DIM)
        grad_kv = lax.psum(jnp.einsum("bld,blk->dk", h_all, g_all[:, :, KEY:NCAT], preferred_element_type=F32), "tp")

        y_sum, dh_sum = scatter_call(y_part, dh_part)
        y_loc = (residual + y_sum.astype(F32)).astype(BF16)
        grad_normed = dh_sum.astype(F32)
        grad_gain = lax.psum(jnp.sum(grad_normed * x_hat, axis=(0, 1)), "tp")
        grad_hat = grad_normed * ln_gain
        grad_x = (
            inv_std * (grad_hat - jnp.mean(grad_hat, axis=-1, keepdims=True) - x_hat * jnp.mean(grad_hat * x_hat, axis=-1, keepdims=True))
            + dy_loc.astype(F32)
        )
        return (
            y_loc,
            grad_x.astype(BF16),
            grad_gain,
            grad_w_query,
            grad_kv[:, 0:HEAD].astype(BF16),
            grad_kv[:, HEAD:].astype(BF16),
            grad_w_out,
            grad_w_gate,
            grad_w_up,
            grad_w_down,
        )

    act_spec = P(None, "tp", None)
    weight_specs = (P(), P(None, "tp", None), P(), P(), P("tp", None, None), P(None, "tp"), P(None, "tp"), P("tp", None))
    return jax.shard_map(layer_shard, mesh=mesh, in_specs=(act_spec, act_spec) + weight_specs, out_specs=(act_spec, act_spec) + weight_specs, check_vma=False)
```

time: 1590 us -> 898 us (0.56)
  waiting for transfers between devices: 843 us -> 0 us
  Pallas kernels: 0 us -> 646 us
  matrix products: 549 us -> 134 us
  local copies, waits for them, and re-layouts: 53.8 us -> 1.53 us
    pallas_call x0 -> x2, Pallas kernels: none -> 646 us  [the longest x1 331 us: gather_call(): pl.pallas_call(gather_kernel, out_shape=[jax.ShapeDtypeStruct(s, BF16) fo...]
    unnamed x6 -> x0, waiting for transfers between devices: 489 us -> none
    dot_general x27 -> x11, matrix products: 549 us -> 134 us  [the longest x3 46.7 us: grad_in(): jnp.einsum('bld,blf->df', h_sib, g_sib[:, :, lo:hi], preferred_element_ty...]
    all_gather x2 -> x0, waiting for transfers between devices: 354 us -> none  [the longest x1 195 us: layer_shard(): normed = lax.all_gather(normed_loc, 'tp', axis=1, tiled=True)]
    unnamed x76 -> x34, local copies, waits for them, and re-layouts: 53.8 us -> 0.07 us
  transfers between devices with their start and end apart: 4 -> 0, of which waited for: 4 -> 0; matrix products, arithmetic and copies ran while one was open for 17% -> 0% of each run, Pallas kernels for 0% -> 0%
where the time goes in v1:
time: 898 us; the launch traced here: 892 us
  Pallas kernels  646 us (72%)
  matrix products  134 us (15%)
  blocking collectives  97.1 us (11%)
  other arithmetic  12 us (1%)
    pallas_call x1, Pallas kernels, gather_call(): pl.pallas_call(gather_kernel, out_shape=[jax.ShapeDtypeStruct(s, BF16) fo...  331 us
    pallas_call x1, Pallas kernels, scatter_call(): pl.pallas_call(scatter_kernel, out_shape=[jax.ShapeDtypeStruct((2 * GROUP...  315 us
    psum x1, blocking collectives, layer_shard(): grad_gain = lax.psum(jnp.sum(grad_normed * x_hat, axis=(0, 1)), 'tp')  97.1 us
    dot_general x3, matrix products, grad_in(): jnp.einsum('bld,blf->df', h_sib, g_sib[:, :, lo:hi], preferred_element_ty...  46.7 us
    dot_general x3, matrix products, grad_in(): jnp.einsum('bld,blf->df', h_all, g_all[:, :, lo:hi], preferred_element_ty...  35.8 us
    dot_general x2, matrix products, grad_out(): jnp.einsum('blf,bld->fd', zo_sib[:, :, sib_lo:sib_hi], dy_sib, preferred_...  25.8 us

profile of v1, /device:TPU:0, one launch (start us, length us, event | category | flops | bytes accessed | tf_op | source)
XLA Modules:
  0.0 891.8 jit_solution(4380531532841122517)
XLA Ops:
  0.7 1.5 convert_reduce_fusion
  2.1 1.6 fusion.21
  3.8 0.5 fusion.39
  4.3 0.8 pad_maximum_fusion
  5.2 2.6 fusion.16.h_loc
  7.8 331.1 %gather_layer.1 = (bf16[8,256,4096]{2,1,0:T(8,128)(2,1)}, bf16[8,256,4096]{2,1,0:T(8,128)(2,1)}, bf16[8,256,4096]{2,1,0:T(8,128)(2,1)}, bf16[8,256,4096]{2,1,0:T...) custom-call(bf16[16,8,4096]{2,1,0:T(8,128)(2,1)} %fusion.16.h_loc, ...), custom_call_target="tpu_custom_call" | custom-call | tf_op jit(solution)/shard_map/gather_layer/pallas_call | solution.py:348
  338.9 0.0 copy-start
  338.9 0.0 copy-start.1
  338.9 0.0 slice-start
  338.9 0.0 slice-start.1
  338.9 0.0 slice-start.2
  338.9 314.9 %scatter_sums.1 = (bf16[16,8,4096]{2,1,0:T(8,128)(2,1)S(1)}, bf16[16,8,4096]{2,1,0:T(8,128)(2,1)S(1)}) custom-call(bf16[8,256,4096]{2,1,0:T(8,128)(2,1)} %get-tuple-element.22.y_part, bf16[8,256,4096]{2,1,0:T(8,128)(2,1)} %get-tuple-element.23.dh_part), custom_call_target="tpu_custom_call" | custom-call | tf_op jit(solution)/shard_map/scatter_sums/pallas_call | solution.py:534
  653.9 0.0 copy-done
  653.9 0.0 copy-done.1
  653.9 1.2 fusion.23
  655.0 3.7 fusion.20
  658.8 0.0 slice-start.3
  658.8 8.5 convolution_bitcast_fusion.1
  667.2 0.0 slice-done
  667.3 0.0 slice-done.1
  667.3 0.0 slice-done.2
  667.3 0.0 slice-done.3
  667.3 4.4 fusion.7
  671.7 13.2 %fusion.26 = f32[512,4096,1]{1,0,2:T(8,128)} fusion(bf16[8,256,4096]{2,1,0:T(8,128)(2,1)S(1)} %bitcast.58, bf16[8,256,1280]{2,1,0:T(8,128)(2,1)} %get-tuple-element.30), kind=kOutput, calls=%fused_computation.39 | convolution fusion | flops 8589934592 | bytes 27262976 | tf_op jit(solution)/shard_map/blf,bld->fd/dot_general | solution.py:583
  684.9 0.0 copy-done.2
  684.9 0.0 slice-start.6
  684.9 17.4 %fusion = bf16[512,4096]{1,0:T(8,128)(2,1)} fusion(f32[512,4096,1]{1,0,2:T(8,128)} %fusion.26, bf16[8,256,4096]{2,1,0:T(8,128)(2,1)} %get-tuple-element.33, bf16[8,256,640]{2,1,0:T(8,128)(2,1)S(1)} %copy-done.2), kind=kOutput, calls=%fused_computation.1 | convolution fusion | flops 8594128896 | bytes 31457280 | tf_op jit(solution)/shard_map/blf,bld->fd/dot_general | solution.py:584
  702.3 8.7 convolution_bitcast_fusion.3
  711.0 0.0 slice-done.4
  711.0 0.0 slice-done.5
  711.0 0.0 slice-done.6
  711.0 0.0 slice-done.7
  711.0 6.8 fusion.8
  717.8 7.8 convolution_bitcast_fusion
  725.6 97.1 %all-reduce.2 = (f32[4096]{0:T(1024)}, bf16[4096,256]{1,0:T(8,128)(2,1)S(1)}) all-reduce(f32[4096]{0:T(1024)S(1)} %get-tuple-element.34, f32[4096,256]{1,0:T(8,128)} %convolution_bitcast_fusion), channel_id=1, replica_groups=mesh['tp'=32] {'tp'}, use_global_device_ids=true, to_apply=%region_5.6 | all-reduce | flops 1052672 | bytes 6324224 | tf_op jit(solution)/shard_map/psum | solution.py:596
  822.7 0.0 slice-start.8
  822.7 1.5 fusion.52
  824.2 15.7 %fusion.29 = f32[4096,512,1]{1,0,2:T(8,128)} fusion(bf16[8,256,4096]{2,1,0:T(8,128)(2,1)} %get-tuple-element.26, bf16[8,256,2560]{2,1,0:T(8,128)(2,1)} %get-tuple-element.27), kind=kOutput, calls=%fused_computation.42 | convolution fusion | flops 8589934592 | bytes 27262976 | tf_op jit(solution)/shard_map/bld,blf->df/dot_general | solution.py:579
  839.9 0.0 slice-done.8
  839.9 0.0 slice-done.9
  839.9 0.0 slice-done.10
  839.9 0.0 slice-done.11
  839.9 0.0 slice-start.13
  839.9 13.4 %fusion.32 = f32[4096,512,1]{1,0,2:T(8,128)} fusion(bf16[8,256,4096]{2,1,0:T(8,128)(2,1)S(1)} %bitcast.62, bf16[8,256,2560]{2,1,0:T(8,128)(2,1)} %get-tuple-element.27), kind=kOutput, calls=%fused_computation.45 | convolution fusion | flops 8589934592 | bytes 27262976 | tf_op jit(solution)/shard_map/bld,blf->df/dot_general | solution.py:579
  853.3 0.0 slice-done.12
  853.3 0.0 slice-done.13
  853.3 19.1 %fusion.2 = bf16[4096,512]{1,0:T(8,128)(2,1)} fusion(f32[4096,512,1]{1,0,2:T(8,128)} %fusion.32, bf16[8,256,4096]{2,1,0:T(8,128)(2,1)} %get-tuple-element.28, bf16[8,256,1152]{2,1,0:T(8,128)(2,1)S(1)} %bitcast.66), kind=kOutput, calls=%fused_computation.5 | convolution fusion | flops 8594128896 | bytes 31457280 | tf_op jit(solution)/shard_map/bld,blf->df/dot_general | solution.py:580
  872.4 18.9 %fusion.1 = bf16[4096,512]{1,0:T(8,128)(2,1)} fusion(f32[4096,512,1]{1,0,2:T(8,128)} %fusion.29, bf16[8,256,4096]{2,1,0:T(8,128)(2,1)} %get-tuple-element.28, bf16[8,256,1152]{2,1,0:T(8,128)(2,1)S(1)} %bitcast.66), kind=kOutput, calls=%fused_computation.3 | convolution fusion | flops 8594128896 | bytes 31457280 | tf_op jit(solution)/shard_map/bld,blf->df/dot_general | solution.py:580
  (18 shorter events, 0.1 us)
Async XLA Ops:
  338.9 315.0 %copy-start = (bf16[16,8,4096]{2,1,0:T(8,128)(2,1)S(1)}, bf16[16,8,4096]{2,1,0:T(8,128)(2,1)}, u32[]{:S(2)}) copy-start(bf16[16,8,4096]{2,1,0:T(8,128)(2,1)} %param.10) | copy-start | bytes 3145732
  338.9 315.0 %copy-start.1 = (f32[4096]{0:T(1024)S(1)}, f32[4096]{0:T(1024)}, u32[]{:S(2)}) copy-start(f32[4096]{0:T(1024)} %param.12) | copy-start | bytes 49156
  338.9 328.4 %slice-start = ((s8[16777216]{0:T(1024)(128)(4,1)}), s8[4194304]{0:T(1024)(128)(4,1)S(1)}, s32[]{:S(2)}) async-start(s8[16777216]{0:T(1024)(128)(4,1)} %bitcast.57), calls=%async_computation | async-start | bytes 8388608
  338.9 328.4 %slice-start.1 = ((s8[16777216]{0:T(1024)(128)(4,1)}), s8[4194304]{0:T(1024)(128)(4,1)S(1)}, s32[]{:S(2)}) async-start(s8[16777216]{0:T(1024)(128)(4,1)} %bitcast.57), calls=%async_computation.1 | async-start | bytes 8388608
  338.9 328.4 %slice-start.2 = ((s8[16777216]{0:T(1024)(128)(4,1)}), s8[4194304]{0:T(1024)(128)(4,1)S(1)}, s32[]{:S(2)}) async-start(s8[16777216]{0:T(1024)(128)(4,1)} %bitcast.57), calls=%async_computation.2 | async-start | bytes 8388608
  658.8 8.5 slice-start.3
  671.7 13.2 %copy-start.2 = (bf16[8,256,640]{2,1,0:T(8,128)(2,1)S(1)}, bf16[8,256,640]{2,1,0:T(8,128)(2,1)}, u32[]{:S(2)}) copy-start(bf16[8,256,640]{2,1,0:T(8,128)(2,1)} %get-tuple-element.32) | copy-start | bytes 7864324
  684.9 26.1 %slice-start.4 = ((s8[16777216]{0:T(1024)(128)(4,1)}), s8[4194304]{0:T(1024)(128)(4,1)S(1)}, s32[]{:S(2)}) async-start(s8[16777216]{0:T(1024)(128)(4,1)} %bitcast.59), calls=%async_computation.4 | async-start | bytes 8388608
  684.9 26.1 %slice-start.5 = ((s8[16777216]{0:T(1024)(128)(4,1)}), s8[4194304]{0:T(1024)(128)(4,1)S(1)}, s32[]{:S(2)}) async-start(s8[16777216]{0:T(1024)(128)(4,1)} %bitcast.59), calls=%async_computation.5 | async-start | bytes 8388608
  684.9 26.1 %slice-start.6 = ((s8[16777216]{0:T(1024)(128)(4,1)}), s8[4194304]{0:T(1024)(128)(4,1)S(1)}, s32[]{:S(2)}) async-start(s8[16777216]{0:T(1024)(128)(4,1)} %bitcast.59), calls=%async_computation.6 | async-start | bytes 8388608
  702.3 8.7 slice-start.7
  822.7 17.2 %slice-start.8 = ((s8[16777216]{0:T(1024)(128)(4,1)}), s8[4194304]{0:T(1024)(128)(4,1)S(1)}, s32[]{:S(2)}) async-start(s8[16777216]{0:T(1024)(128)(4,1)} %bitcast.61), calls=%async_computation.8 | async-start | bytes 8388608
  824.2 15.7 %slice-start.9 = ((s8[16777216]{0:T(1024)(128)(4,1)}), s8[4194304]{0:T(1024)(128)(4,1)S(1)}, s32[]{:S(2)}) async-start(s8[16777216]{0:T(1024)(128)(4,1)} %bitcast.61), calls=%async_computation.9 | async-start | bytes 8388608
  824.2 15.7 %slice-start.10 = ((s8[16777216]{0:T(1024)(128)(4,1)}), s8[4194304]{0:T(1024)(128)(4,1)S(1)}, s32[]{:S(2)}) async-start(s8[16777216]{0:T(1024)(128)(4,1)} %bitcast.61), calls=%async_computation.10 | async-start | bytes 8388608
  824.2 15.7 %slice-start.11 = ((s8[16777216]{0:T(1024)(128)(4,1)}), s8[4194304]{0:T(1024)(128)(4,1)S(1)}, s32[]{:S(2)}) async-start(s8[16777216]{0:T(1024)(128)(4,1)} %bitcast.61), calls=%async_computation.11 | async-start | bytes 8388608
  824.2 29.1 %slice-start.12 = ((s8[4718592]{0:T(1024)(128)(4,1)}), s8[4194304]{0:T(1024)(128)(4,1)S(1)}, s32[]{:S(2)}) async-start(s8[4718592]{0:T(1024)(128)(4,1)} %bitcast.65), calls=%async_computation.12 | async-start | bytes 8388608
  839.9 13.4 %slice-start.13 = ((s8[4718592]{0:T(1024)(128)(4,1)}), s8[524288]{0:T(1024)(128)(4,1)S(1)}, s32[]{:S(2)}) async-start(s8[4718592]{0:T(1024)(128)(4,1)} %bitcast.65), calls=%async_computation.13 | async-start | bytes 1048576

commit v2 on v0

v2 whole, which is shorter than its diff:
```python
import jax
import jax.numpy as jnp
from jax import lax
from jax.experimental import pallas as pl
from jax.experimental.pallas import tpu as pltpu
from jax.sharding import PartitionSpec as P

LN_EPS = 1e-6
ROPE_BASE = 10000.0
MESH = pl.DeviceIdType.MESH
F32 = jnp.float32
BF16 = jnp.bfloat16
ALL = slice(None)
PAIR = range(2)
LANES = 128
W = 256
VMEM_BYTES = 67043328

GROUP = 8
ITEMS = 2 * GROUP
ROWS = 8
BLOCK = 2 * ROWS
LINE = 4 * BLOCK
SEQ = 4 * LINE
TALL = (2, 2, LINE)
DIM = 4096
HEAD = 128
FFN = 512
OUT = FFN + HEAD
OWN = 2 * FFN + HEAD
KEY = 2 * OWN
VAL = KEY + HEAD
NCAT = VAL + HEAD
NZO = 2 * OUT
QCOL = (2 * FFN, OWN + 2 * FFN)
OCOL = (2 * FFN, 2 * FFN + HEAD)
NEAR = GROUP * SEQ

EARLY = 5
DEPTH = 5
COPIES = 14


class Columns:
    def __init__(self, a):
        self.a, self.c = a, DIM // 2 - a
        self.left = (slice(0, a), slice(a, 2 * a))
        self.both_left = slice(0, 2 * a)
        self.right = (slice(2 * a, 2 * a + self.c), slice(2 * a + self.c, DIM))
        self.both_right = slice(2 * a, DIM)
        self.halves = (slice(0, self.c), slice(self.c, 2 * self.c))


GCOL = Columns(1280)
SCOL = Columns(1536)


def place():
    i = lax.axis_index("tp")
    return lax.div(i, 8), lax.rem(lax.div(i, 4), 2), lax.rem(lax.div(i, 2), 2), lax.rem(i, 2)


def index(z, y, x, core):
    return ((z * 2 + y) * 2 + x) * 2 + core


def rows8(start, size):
    return pl.ds(pl.multiple_of(start, ROWS), size)


def rows16(start, size):
    return pl.ds(pl.multiple_of(start, BLOCK), size)


def lanes(start, size):
    return pl.ds(pl.multiple_of(start, LANES), size)


def step_of(t, size):
    return lanes(t * size, size)


def loop(count, body):
    lo, hi = count if isinstance(count, tuple) else (0, count)

    def run(i, carry):
        body(i)
        return carry

    lax.fori_loop(lo, hi, run, 0)


def remote(src, dst, sems, target):
    return pltpu.make_async_remote_copy(src, dst, *sems, device_id=(target,), device_id_type=MESH)


def start(copies):
    for c in copies:
        c.start()


def wait(copies):
    for c in copies:
        c.wait()


def wait_recv(copies):
    for c in copies:
        c.wait_recv()


def wait_send(copies):
    for c in copies:
        c.wait_send()


def partners_of(z, y, x, core):
    chips = [index(lax.rem(z + k, 4), y, x, core) for k in (1, 2, 3)]
    return [index(z, y, x, 1 - core), index(z, y, 1 - x, core), index(z, 1 - y, x, core)] + chips


def entry_barrier(partners):
    barrier = pltpu.get_barrier_semaphore()
    for partner in partners:
        pl.semaphore_signal(barrier, inc=1, device_id=(partner,), device_id_type=MESH)
    pl.semaphore_wait(barrier, len(partners))


def dot_nt(a, b):
    return lax.dot_general(a, b, (((1,), (1,)), ((), ())), preferred_element_type=F32)


def dot_tn(a, b):
    return lax.dot_general(a, b, (((0,), (0,)), ((), ())), preferred_element_type=F32)


def dot_nn(a, b):
    return jnp.dot(a, b, preferred_element_type=F32)


def add_into(dst, src, width):
    def tile(t):
        cols = step_of(t, W)
        dst[..., cols] = (dst[..., cols].astype(F32) + src[..., cols].astype(F32)).astype(BF16)

    loop(width // W, tile)


def row_position(r):
    return ((r // BLOCK) % 4) * LINE + (r // (2 * LINE)) * (2 * BLOCK) + ((r // LINE) % 2) * BLOCK + r % BLOCK


class Line:
    def __init__(self, z, y, x, core):
        low = lax.div(z, 2)
        odd = lax.rem(z, 2)
        self.mid = low != odd
        self.end = low == odd
        side = index(z + 1 - 2 * odd, y, x, core)
        across = index(3 - z, y, x, core)
        self.three = rows16(BLOCK - BLOCK * low, 3 * BLOCK)
        self.half = rows16(2 * BLOCK * low, 2 * BLOCK)
        self.other = rows16(2 * BLOCK - 2 * BLOCK * low, 2 * BLOCK)
        self.tip = rows16(3 * BLOCK * low, BLOCK)
        self.own = rows16(BLOCK * z, BLOCK)
        self.spread = ((self.own, side), (self.half, across), (self.three, side))
        self.merge = ((self.three, side), (self.other, across), (self.tip, side))


class Transfer:
    def __init__(self, spot, send, recv, lo, hi):
        self.z, self.y, self.x, self.core = spot
        self.lo, self.hi = lo, hi
        self.line = Line(*spot)
        self.sib, self.xn, self.yn, *self.zn = partners_of(*spot)
        self.send, self.recv, self.keys = send, recv, {}

    def sems(self, slot, key):
        k = self.keys.setdefault(key, len(self.keys))
        return self.send.at[slot, k], self.recv.at[slot, k]

    def on_end(self, body):
        pl.when(self.line.end)(body)

    def on_mid(self, body):
        pl.when(self.line.mid)(body)

    def tick(self, m):
        for k, stage in reversed(list(enumerate(self.stages))):
            n = m - k

            @pl.when((n >= self.lo) & (n < self.hi))
            def _(stage=stage, n=n):
                stage(n)


class Gather(Transfer):
    def __init__(self, spot, buf, send, recv):
        super().__init__(spot, send, recv, 0, ITEMS)
        self.buf = buf
        self.stages = (self.stage0, self.stage1, self.stage2, self.stage3, self.stage4, self.stage5)

    def copy(self, n, key, ys, xs, rows, cols, target):
        view = self.buf.at[lax.div(n, 2), lax.rem(n, 2), ys, xs, rows, cols]
        return remote(view, view, self.sems(n, key), target)

    def za(self, n, step):
        rows, target = self.line.spread[step]
        return self.copy(n, ("za", step), self.y, self.x, rows, GCOL.both_left, target)

    def zc(self, n, step):
        rows, target = self.line.spread[step]
        return self.copy(n, ("zc", step), ALL, ALL, rows, GCOL.both_right, target)

    def c1(self, n):
        cols, own = GCOL.right, self.line.own
        return [self.copy(n, "c1x", self.y, self.x, own, cols[0], self.xn), self.copy(n, "c1y", self.y, self.x, own, cols[1], self.yn)]

    def c2(self, n):
        cols, own = GCOL.right, self.line.own
        return [self.copy(n, "c2y", self.y, ALL, own, cols[0], self.yn), self.copy(n, "c2x", ALL, self.x, own, cols[1], self.xn)]

    def a1(self, n):
        cols = GCOL.left
        return [self.copy(n, "a1y", self.y, self.x, ALL, cols[0], self.yn), self.copy(n, "a1x", self.y, self.x, ALL, cols[1], self.xn)]

    def a2(self, n):
        cols = GCOL.left
        return [self.copy(n, "a2x", ALL, self.x, ALL, cols[0], self.xn), self.copy(n, "a2y", self.y, ALL, ALL, cols[1], self.yn)]

    def pass_on(self, chain, n, step):
        def body():
            chain(n, step - 1).wait_recv()
            chain(n, step).start()

        self.on_mid(body)

    def stage0(self, n):
        self.on_end(lambda: self.za(n, 0).start())
        start(self.c1(n))

    def stage1(self, n):
        self.pass_on(self.za, n, 1)
        wait_recv(self.c1(n))
        start(self.c2(n))

    def stage2(self, n):
        self.pass_on(self.za, n, 2)
        wait_recv(self.c2(n))
        self.on_end(lambda: self.zc(n, 0).start())

    def stage3(self, n):
        self.on_end(lambda: self.za(n, 2).wait_recv())
        start(self.a1(n))
        self.pass_on(self.zc, n, 1)

    def stage4(self, n):
        wait_recv(self.a1(n))
        start(self.a2(n))
        self.pass_on(self.zc, n, 2)

    def stage5(self, n):
        wait_recv(self.a2(n))
        self.on_end(lambda: self.zc(n, 2).wait_recv())

    def finish(self, n):
        wait_send(self.c1(n) + self.c2(n) + self.a1(n) + self.a2(n))
        self.on_end(lambda: wait_send([self.za(n, 0), self.zc(n, 0)]))
        self.on_mid(lambda: wait_send([chain(n, step) for chain in (self.za, self.zc) for step in (1, 2)]))


def scatter_shapes():
    a, c = SCOL.a, SCOL.c
    return dict(
        b1=(4, 2, 2, LINE, a), b2=(6, 2, LINE, a), za0=(3, 2, 3 * BLOCK, a), za1=(3, 2, 2 * BLOCK, a), za2=(4, 2, BLOCK, a),
        own_a=(2, 2, 2, LINE, a), own_c=(4, *TALL, 2 * c), zc0=(4, 2, 2, 3 * BLOCK, 2 * c), zc1=(3, 2, 2, 2 * BLOCK, 2 * c),
        zc2=(5, 2, 2, BLOCK, 2 * c), h1=(3, 2, 2, BLOCK, c), h2=(3, 2, BLOCK, c), fin=(3, 2, ROWS, DIM),
    )


SLOTS = 6


def scatter_scratch():
    dma = pltpu.SemaphoreType.DMA
    buffers = [pltpu.VMEM(s, BF16) for s in scatter_shapes().values()]
    return buffers + [dma((SLOTS, COPIES)), dma((SLOTS, COPIES)), dma((SLOTS, 3)), dma((ITEMS,)), dma((ITEMS,)), dma((ITEMS,))]


class Scatter(Transfer):
    def __init__(self, spot, parts, sums, lo, hi, refs):
        shapes = scatter_shapes()
        self.depth = {name: s[0] for name, s in shapes.items()}
        self.ring = dict(zip(shapes, refs))
        send, recv, self.lsem, *self.store_sems = refs[len(shapes) :]
        super().__init__(spot, send, recv, lo, hi)
        self.parts, self.sums = parts, sums
        self.stages = (self.stage0, self.stage1, self.stage2, self.stage3, self.stage4, self.stage5)

    def slot(self, name, n, *at):
        return self.ring[name].at[(lax.rem(n, self.depth[name]), *at)]

    def copy(self, n, key, src, dst, target):
        return remote(src, dst, self.sems(lax.rem(n, SLOTS), key), target)

    def a1(self, n):
        cols = SCOL.left
        return [
            self.copy(n, "a1x", self.parts.at[n, :, 1 - self.x, :, cols[0]], self.slot("b1", n, 0), self.xn),
            self.copy(n, "a1y", self.parts.at[n, 1 - self.y, :, :, cols[1]], self.slot("b1", n, 1), self.yn),
        ]

    def a2(self, n):
        return [
            self.copy(n, "a2y", self.slot("b1", n, 0, 1 - self.y), self.slot("b2", n, 0), self.yn),
            self.copy(n, "a2x", self.slot("b1", n, 1, 1 - self.x), self.slot("b2", n, 1), self.xn),
        ]

    def za(self, n, step):
        rows, target = self.line.merge[step]
        key = f"za{step}"
        return self.copy(n, key, self.slot("b2", n, ALL, rows, ALL), self.slot(key, n), target)

    def zc(self, n, step):
        rows, target = self.line.merge[step]
        key = f"zc{step}"
        src = self.slot("own_c", n, ALL, ALL, rows, ALL) if step else self.parts.at[n, :, :, rows, SCOL.both_right]
        return self.copy(n, key, src, self.slot(key, n), target)

    def h1(self, n):
        cols = SCOL.halves
        return [
            self.copy(n, "h1y", self.slot("zc2", n, 1 - self.y, ALL, ALL, cols[0]), self.slot("h1", n, 0), self.yn),
            self.copy(n, "h1x", self.slot("zc2", n, ALL, 1 - self.x, ALL, cols[1]), self.slot("h1", n, 1), self.xn),
        ]

    def h2(self, n):
        cols = SCOL.halves
        return [
            self.copy(n, "h2x", self.slot("zc2", n, self.y, 1 - self.x, ALL, cols[0]), self.slot("h2", n, 0), self.xn),
            self.copy(n, "h2y", self.slot("zc2", n, 1 - self.y, self.x, ALL, cols[1]), self.slot("h2", n, 1), self.yn),
        ]

    def loads(self, n):
        sem = self.lsem.at[lax.rem(n, SLOTS)]
        views = (
            (self.parts.at[n, :, self.x, :, SCOL.left[0]], self.slot("own_a", n, 0)),
            (self.parts.at[n, self.y, :, :, SCOL.left[1]], self.slot("own_a", n, 1)),
            (self.parts.at[n, :, :, :, SCOL.both_right], self.slot("own_c", n)),
        )
        return [pltpu.make_async_copy(src, dst, sem.at[k]) for k, (src, dst) in enumerate(views)]

    def store(self, n):
        to = self.sums.at[lax.rem(n, 2), self.core, lax.div(n, 2) - self.lo // 2]
        near, send, recv = self.store_sems
        far = remote(self.slot("fin", n, 1 - self.core), to, (send.at[n], recv.at[n]), self.sib)
        return pltpu.make_async_copy(self.slot("fin", n, self.core), to, near.at[n]), far

    def stored(self, n):
        near, far = self.store(n)
        near.wait()
        far.wait_send()

    def stage0(self, n):
        start(self.a1(n))
        self.on_end(lambda: self.zc(n, 0).start())
        start(self.loads(n))

    def stage1(self, n):
        wait(self.loads(n))
        wait_recv(self.a1(n))
        for c in PAIR:
            add_into(self.slot("b1", n, c), self.slot("own_a", n, c), SCOL.a)
        start(self.a2(n))

        def middle():
            self.zc(n, 0).wait_recv()
            add_into(self.slot("own_c", n, ALL, ALL, self.line.three), self.slot("zc0", n), 2 * SCOL.c)
            self.zc(n, 1).start()

        self.on_mid(middle)
        wait_send(self.a1(n))
        self.on_end(lambda: self.zc(n, 0).wait_send())

    def stage2(self, n):
        wait_recv(self.a2(n))
        for c, mine in enumerate((self.y, self.x)):
            add_into(self.slot("b2", n, c), self.slot("b1", n, c, mine), SCOL.a)
        self.on_end(lambda: self.za(n, 0).start())

        def middle():
            self.zc(n, 1).wait_recv()
            add_into(self.slot("own_c", n, ALL, ALL, self.line.half), self.slot("zc1", n), 2 * SCOL.c)
            self.zc(n, 2).start()
            self.zc(n, 1).wait_send()

        self.on_mid(middle)
        wait_send(self.a2(n))

    def stage3(self, n):
        own_c = self.slot("own_c", n, ALL, ALL, self.line.own)

        def middle():
            self.za(n, 0).wait_recv()
            add_into(self.slot("b2", n, ALL, self.line.three), self.slot("za0", n), SCOL.a)
            self.za(n, 1).start()
            self.slot("zc2", n)[...] = own_c[...]

        def tip():
            self.zc(n, 2).wait_recv()
            add_into(self.slot("zc2", n), own_c, 2 * SCOL.c)

        self.on_mid(middle)
        self.on_end(tip)
        start(self.h1(n))
        self.on_mid(lambda: self.zc(n, 2).wait_send())
        self.on_end(lambda: self.za(n, 0).wait_send())

    def stage4(self, n):
        def middle():
            self.za(n, 1).wait_recv()
            add_into(self.slot("b2", n, ALL, self.line.half), self.slot("za1", n), SCOL.a)
            self.za(n, 2).start()
            self.za(n, 1).wait_send()

        self.on_mid(middle)
        wait_recv(self.h1(n))
        cols = SCOL.halves
        add_into(self.slot("zc2", n, self.y, ALL, ALL, cols[0]), self.slot("h1", n, 0), SCOL.c)
        add_into(self.slot("zc2", n, ALL, self.x, ALL, cols[1]), self.slot("h1", n, 1), SCOL.c)
        start(self.h2(n))
        wait_send(self.h1(n))

    def stage5(self, n):
        pl.when(n >= self.lo + self.depth["fin"])(lambda: self.stored(n - self.depth["fin"]))

        def tip():
            self.za(n, 2).wait_recv()
            add_into(self.slot("b2", n, ALL, self.line.own), self.slot("za2", n), SCOL.a)

        self.on_end(tip)
        self.on_mid(lambda: self.za(n, 2).wait_send())
        wait_recv(self.h2(n))
        fin = self.slot("fin", n)

        def put(total, col):
            for core in PAIR:
                fin[core, :, lanes(col, W)] = total[core * ROWS : (core + 1) * ROWS].astype(BF16)

        def left(t):
            for c in PAIR:
                put(self.slot("b2", n, c, self.line.own)[:, step_of(t, W)].astype(F32), c * SCOL.a + t * W)

        def right(t):
            for c in PAIR:
                mine = self.slot("zc2", n, self.y, self.x)[:, lanes(c * SCOL.c + t * W, W)].astype(F32)
                put(mine + self.slot("h2", n, c)[:, step_of(t, W)].astype(F32), 2 * SCOL.a + c * SCOL.c + t * W)

        loop(SCOL.a // W, left)
        loop(SCOL.c // W, right)
        start(self.store(n))
        wait_send(self.h2(n))

    def finish(self):
        for n in range(self.hi - self.depth["fin"], self.hi):
            self.stored(n)
        loop((self.lo, self.hi), lambda n: wait_recv(self.store(n)[1:]))


def gather_kernel(
    h_loc, dy_loc, w1, w3, wq, wk, wv, w2, wo, cos_t, sin_t,
    full, full_sib, parts, g_all, zo_all, g_sib, zo_sib, sums,
    wcat, w2o, hv, dyv, proj, zo, g, yo, dho, probs, qs, stage,
    gsend, grecv, sx, rx, sw, rw, ss, rs, sg, rg, lsem, wsem, osem, gsem, *scatter_refs,
):
    spot = place()
    z, y, x, core = spot
    partners = partners_of(*spot)
    sib = partners[0]
    entry_barrier(partners)
    gather = Gather(spot, full, gsend, grecv)
    scatter = Scatter(spot, parts, sums, 0, 2 * EARLY, scatter_refs)

    mine = rows8(BLOCK * z + ROWS * core, ROWS)
    locs = (h_loc, dy_loc)
    to = [full.at[:, s, y, x, mine, :] for s in PAIR]
    swaps = [remote(locs[s].at[rows8(GROUP * (1 - core), GROUP)], to[s], (sx.at[s], rx.at[s]), sib) for s in PAIR]
    takes = [pltpu.make_async_copy(locs[s].at[rows8(GROUP * core, GROUP)], stage.at[s], lsem.at[s]) for s in PAIR]
    puts = [pltpu.make_async_copy(stage.at[s], to[s], lsem.at[s]) for s in PAIR]
    start(swaps + takes)
    for s in PAIR:
        takes[s].wait()
        puts[s].start()
    wait(puts)
    wait_recv(swaps)
    loop(2, gather.tick)

    spots = (
        (w1, wcat.at[:, 0:FFN], wcat.at[:, OWN : OWN + FFN]),
        (w3, wcat.at[:, FFN : 2 * FFN], wcat.at[:, OWN + FFN : OWN + 2 * FFN]),
        (wq, wcat.at[:, 2 * FFN : OWN], wcat.at[:, OWN + 2 * FFN : KEY]),
        (w2, w2o.at[0:FFN], w2o.at[FFN : 2 * FFN]),
        (wo, w2o.at[OCOL[0] : OCOL[1]], w2o.at[OCOL[1] : NZO]),
    )
    shared = ((wk, wcat.at[:, KEY:VAL]), (wv, wcat.at[:, VAL:NCAT]))
    weights = [(w, near) for w, near, _ in spots] + list(shared)
    local = [pltpu.make_async_copy(w, near, wsem.at[k]) for k, (w, near) in enumerate(weights)]
    far = [remote(w, there, (sw.at[k], rw.at[k]), sib) for k, (w, _, there) in enumerate(spots)]
    start(local + far)
    loop((2, DEPTH + 1), gather.tick)

    def load(b, s):
        return pltpu.make_async_copy(full.at[b, s], (hv, dyv)[s], lsem.at[s])

    def sib_copy(b, s):
        return remote(full.at[b, s], full_sib.at[b, s], (ss.at[b, s], rs.at[b, s]), sib)

    def arrived(b, s):
        load(b, s).start()
        sib_copy(b, s).start()

    arrived(0, 0)
    wait(local)
    wait_recv(far)

    def gz_copies(b):
        rows = rows16(b * SEQ, SEQ)
        views = (
            (g.at[:, OWN:KEY], g_sib.at[rows]),
            (zo.at[:, FFN : 2 * FFN], zo_sib.at[rows, 0:FFN]),
            (zo.at[:, OCOL[1] : NZO], zo_sib.at[rows, FFN:OUT]),
        )
        return [remote(src, dst, (sg.at[b, k], rg.at[b, k]), sib) for k, (src, dst) in enumerate(views)]

    def gz_local(b):
        rows = rows16(b * SEQ, SEQ)
        return [pltpu.make_async_copy(g, g_all.at[rows], gsem.at[0]), pltpu.make_async_copy(zo, zo_all.at[rows], gsem.at[1])]

    def out(b, s):
        return pltpu.make_async_copy((yo, dho)[s], parts.at[2 * b + s], osem.at[s])

    def drained(b):
        wait(gz_local(b) + [out(b, s) for s in PAIR])
        wait_send(gz_copies(b))

    scale = HEAD ** -0.5

    def rotate(v, back=False):
        turn = pltpu.roll(v, HEAD // 2, 1) * sin_t[...]
        return v * cos_t[...] + (-turn if back else turn)

    def flat(ref):
        return ref[...].reshape(SEQ, DIM)

    def gate_up(t):
        at = t * W + lax.div(t, 2) * (OWN - FFN)
        return lanes(at, W), lanes(at + FFN, W)

    wide = lambda t: step_of(t, FFN)

    def batch_step(b):
        gather.tick(2 * b + DEPTH + 1)
        arrived(b, 1)
        load(b, 0).wait()

        def proj_tile(t):
            proj[:, wide(t)] = dot_nn(flat(hv), wcat[:, wide(t)])

        loop(NCAT // FFN, proj_tile)
        pl.when(b > 0)(lambda: drained(b - 1))
        scatter.tick(2 * b - 2)

        def hidden_tile(t):
            gate_at, up_at = gate_up(t)
            gate = proj[:, gate_at]
            zo[:, step_of(t, W)] = (gate * jax.nn.sigmoid(gate) * proj[:, up_at]).astype(BF16)

        loop(2 * FFN // W, hidden_tile)
        keys = rotate(proj[:, KEY:VAL]).astype(BF16)
        vals = proj[:, VAL:NCAT].astype(BF16)
        qs[2] = keys
        qs[3] = vals
        causal = row_position(lax.broadcasted_iota(jnp.int32, (SEQ, SEQ), 0)) >= row_position(lax.broadcasted_iota(jnp.int32, (SEQ, SEQ), 1))
        for hd in PAIR:
            query = rotate(proj[:, QCOL[hd] : QCOL[hd] + HEAD]).astype(BF16)
            qs[hd] = query
            scores = jnp.where(causal, dot_nt(query, keys) * scale, -1e30)
            e = jnp.exp(scores - jnp.max(scores, axis=-1, keepdims=True))
            p = e / jnp.sum(e, axis=-1, keepdims=True)
            probs[hd] = p
            zo[:, OCOL[hd] : OCOL[hd] + HEAD] = dot_nn(p.astype(BF16), vals).astype(BF16)

        gather.tick(2 * b + DEPTH + 2)
        pl.when(b < GROUP - 1)(lambda: arrived(b + 1, 0))

        def y_tile(t):
            yo[:, :, :, wide(t)] = dot_nn(zo[...], w2o[:, wide(t)]).astype(BF16).reshape(*TALL, FFN)

        loop(DIM // FFN, y_tile)
        out(b, 0).start()
        load(b, 1).wait()

        def dz_tile(t):
            dz = dot_nt(flat(dyv), w2o[rows16(t * W, W), :])
            gate_at, up_at = gate_up(t)
            gate = proj[:, gate_at]
            sig = jax.nn.sigmoid(gate)
            g[:, gate_at] = (dz * proj[:, up_at] * sig * (1.0 + gate * (1.0 - sig))).astype(BF16)
            g[:, up_at] = (dz * (gate * sig)).astype(BF16)

        loop(2 * FFN // W, dz_tile)
        scatter.tick(2 * b - 1)
        d_heads = dot_nt(flat(dyv), w2o[2 * FFN : NZO, :]).astype(BF16)
        d_keys = d_vals = jnp.zeros((SEQ, HEAD), F32)
        for hd in PAIR:
            d_out = d_heads[:, hd * HEAD : (hd + 1) * HEAD]
            p = probs[hd]
            d_probs = dot_nt(d_out, qs[3])
            d_vals = d_vals + dot_tn(p.astype(BF16), d_out)
            row_dot = jnp.sum(p * d_probs, axis=-1, keepdims=True)
            d_scores = (p * (d_probs - row_dot) * scale).astype(BF16)
            g[:, QCOL[hd] : QCOL[hd] + HEAD] = rotate(dot_nn(d_scores, qs[2]), True).astype(BF16)
            d_keys = d_keys + dot_tn(d_scores, qs[hd])
        g[:, KEY:VAL] = rotate(d_keys, True).astype(BF16)
        g[:, VAL:NCAT] = d_vals.astype(BF16)

        def dh_tile(t):
            dho[:, :, :, wide(t)] = dot_nt(g[...], wcat[rows16(t * FFN, FFN), :]).astype(BF16).reshape(*TALL, FFN)

        loop(DIM // FFN, dh_tile)
        out(b, 1).start()
        start(gz_local(b) + gz_copies(b))

    loop(GROUP, batch_step)
    drained(GROUP - 1)
    loop((ITEMS - 2, 2 * EARLY + DEPTH), scatter.tick)
    scatter.finish()

    def finish(b):
        for s in PAIR:
            gather.finish(2 * b + s)
            sib_copy(b, s).wait()
        wait_recv(gz_copies(b))

    loop(GROUP, finish)
    wait_send(swaps + far)


def gather_call(*args):
    any_spec = pl.BlockSpec(memory_space=pl.ANY)
    vmem_spec = pl.BlockSpec(memory_space=pltpu.VMEM)
    dma = pltpu.SemaphoreType.DMA
    tall = (*TALL, DIM)
    shapes = [(GROUP, 2, *tall)] * 2 + [(ITEMS, *tall), (NEAR, NCAT), (NEAR, NZO), (NEAR, OWN), (NEAR, OUT), (2, 2, EARLY, ROWS, DIM)]
    vmem = [(DIM, NCAT), (NZO, DIM), tall, tall, (SEQ, NCAT), (SEQ, NZO), (SEQ, NCAT), tall, tall, (2, SEQ, SEQ), (4, SEQ, HEAD), (2, GROUP, ROWS, DIM)]
    types = [BF16] * 4 + [F32] + [BF16] * 4 + [F32] + [BF16] * 2
    pairs = [(ITEMS, COPIES), (2,), (5,), (GROUP, 2), (GROUP, 3)]
    return pl.pallas_call(
        gather_kernel,
        out_shape=[jax.ShapeDtypeStruct(s, BF16) for s in shapes],
        in_specs=[any_spec] * (len(args) - 2) + [vmem_spec] * 2,
        out_specs=[any_spec] * len(shapes),
        scratch_shapes=[
            *[pltpu.VMEM(s, t) for s, t in zip(vmem, types)],
            *[dma(s) for s in pairs for _ in PAIR],
            *[dma((k,)) for k in (2, 7, 2, 2)],
            *scatter_scratch(),
        ],
        compiler_params=pltpu.CompilerParams(collective_id=0, has_side_effects=True, vmem_limit_bytes=VMEM_BYTES),
        name="gather_layer",
    )(*args)


TILE = 512
STEPS = DIM // TILE
KV = 2 * HEAD
KCOL = OWN + OUT
NBIG = KCOL + KV
QUARTER = DIM // 4
EIGHTH = DIM // 8
KROWS = KV // 4


def scatter_kernel(
    full, full_sib, parts, g_all, zo_all, g_sib, zo_sib,
    sums, dw1, dw3, dwq, dw2, dwo, dwk, dwv,
    big, tiles, out1, outq, out2, kvp, k1, k2, k3, kc, k4, kvo,
    lsem, tsem, o1sem, o2sem, ksend, krecv, kosem, *scatter_refs,
):
    spot = place()
    z, y, x, core = spot
    partners = partners_of(*spot)
    sib, xn, yn, *zn = partners
    entry_barrier(partners)
    scatter = Scatter(spot, parts, sums, 2 * EARLY, ITEMS, scatter_refs)
    scatter.tick(2 * EARLY)

    near, away = slice(0, NEAR), slice(NEAR, 2 * NEAR)
    views = (
        (g_all.at[:, KEY:NCAT], big.at[near, KCOL:NBIG]),
        (g_all.at[:, 0:OWN], big.at[near, 0:OWN]),
        (g_sib, big.at[away, 0:OWN]),
        (zo_all.at[:, 0:FFN], big.at[near, OWN : OWN + FFN]),
        (zo_all.at[:, OCOL[0] : OCOL[1]], big.at[near, OWN + FFN : KCOL]),
        (zo_sib, big.at[away, OWN:KCOL]),
    )
    loads = [pltpu.make_async_copy(src, dst, lsem.at[k]) for k, (src, dst) in enumerate(views)]
    start(loads)

    def tile_load(u, s):
        slot = lax.rem(u, 2)
        sources = (full, full_sib)
        return [pltpu.make_async_copy(sources[k].at[:, s, :, :, :, step_of(u, TILE)], tiles.at[slot, k], tsem.at[slot, k]) for k in PAIR]

    tile_load(0, 0)[0].start()
    loads[0].wait()

    def kv_tile(u):
        pl.when(u < STEPS - 1)(lambda: tile_load(u + 1, 0)[0].start())
        tile_load(u, 0)[0].wait()
        kvp[:, step_of(u, TILE)] = dot_tn(big[near, KCOL:NBIG], tiles[lax.rem(u, 2), 0].reshape(NEAR, TILE))

    loop(STEPS, kv_tile)
    start(tile_load(0, 0))

    half = core * (DIM // 2)
    quarter = (half, half + QUARTER)
    ring = ((x, y, xn, yn), (y, x, yn, xn))
    first = [quarter[c] + ring[c][0] * EIGHTH for c in PAIR]
    second = [first[c] + ring[c][1] * W for c in PAIR]
    mine = rows16(z * KROWS, KROWS)
    hops = {}

    def hop(step, src, dst, target):
        group = hops.setdefault(step, [])
        group.append(remote(src, dst, (ksend.at[step, len(group)], krecv.at[step, len(group)]), target))

    hop(0, kvp.at[:, lanes(DIM // 2 - half, DIM // 2)], k1, sib)
    for c in PAIR:
        a, b, an, bn = ring[c]
        hop(1, kvp.at[:, lanes(quarter[c] + (1 - a) * EIGHTH, EIGHTH)], k2.at[c], an)
        hop(2, kvp.at[:, lanes(first[c] + (1 - b) * W, W)], k3.at[c], bn)
        same = kvo.at[:, lanes(second[c], W)]
        hop(5, same, same, bn)
        same = kvo.at[:, lanes(first[c], EIGHTH)]
        hop(6, same, same, an)
    for k, there in enumerate(zn):
        hop(3, kc.at[rows16(lax.rem(z + k + 1, 4) * KROWS, KROWS)], k4.at[k], there)
        for c in PAIR:
            same = kvo.at[mine, lanes(second[c], W)]
            hop(4, same, same, there)
    same = kvo.at[:, lanes(half, DIM // 2)]
    hop(7, same, same, sib)
    kv_out = [pltpu.make_async_copy(kvo.at[s * HEAD : (s + 1) * HEAD], (dwk, dwv)[s], kosem.at[s]) for s in PAIR]

    def kv_add(src, at, width):
        def tile(t):
            cols = lanes(at + t * W, W)
            kvp[:, cols] = kvp[:, cols] + src[:, step_of(t, W)]

        loop(width // W, tile)

    def kv_first():
        kv_add(k1, half, DIM // 2)

    def kv_second():
        for c in PAIR:
            kv_add(k2.at[c], first[c], EIGHTH)

    def kv_third():
        for c in PAIR:
            kc[:, c * W : (c + 1) * W] = kvp[:, lanes(second[c], W)] + k3[c]

    def kv_round():
        total = kc[mine, :] + k4[0] + k4[1] + k4[2]
        for c in PAIR:
            kvo[mine, lanes(second[c], W)] = total[:, c * W : (c + 1) * W].astype(BF16)

    works = (kv_first, kv_second, kv_third, kv_round)

    def kv_step(j):
        for step in range(len(hops)):

            @pl.when(j == step)
            def _(step=step):
                wait_recv(hops[step])
                if step < len(works):
                    works[step]()
                start(hops.get(step + 1, kv_out))

    start(hops[0])
    wait(loads[1:])

    def out_copies(u):
        slot = lax.rem(u, 2)
        rows, cols = step_of(u, TILE), step_of(u, TILE)
        sem = o1sem.at[slot]
        return [
            pltpu.make_async_copy(out1.at[slot, :, 0:FFN], dw1.at[rows], sem.at[0]),
            pltpu.make_async_copy(out1.at[slot, :, FFN : 2 * FFN], dw3.at[rows], sem.at[1]),
            pltpu.make_async_copy(outq.at[slot], dwq.at[:, cols], sem.at[2]),
        ]

    def out2_copies(u):
        slot, cols = lax.rem(u, 2), step_of(u, TILE)
        sem = o2sem.at[slot]
        return [
            pltpu.make_async_copy(out2.at[slot, 0:FFN], dw2.at[:, cols], sem.at[0]),
            pltpu.make_async_copy(out2.at[slot, FFN:OUT], dwo.at[:, cols], sem.at[1]),
        ]

    def tokens(u):
        return tiles[lax.rem(u, 2)].reshape(2 * NEAR, TILE)

    def grad_in(u):
        wait(tile_load(u, 0))
        pl.when(u < STEPS - 1)(lambda: start(tile_load(u + 1, 0)))
        pl.when(u == STEPS - 1)(lambda: start(tile_load(0, 1)))
        pl.when(u > 1)(lambda: wait(out_copies(u - 2)))
        slot = lax.rem(u, 2)
        for s in PAIR:
            out1[slot, :, s * FFN : (s + 1) * FFN] = dot_tn(tokens(u), big[:, s * FFN : (s + 1) * FFN]).astype(BF16)
        outq[slot] = dot_tn(big[:, 2 * FFN : OWN], tokens(u)).astype(BF16)
        start(out_copies(u))

    def grad_out(u):
        wait(tile_load(u, 1))
        pl.when(u < STEPS - 1)(lambda: start(tile_load(u + 1, 1)))
        pl.when(u > 1)(lambda: wait(out2_copies(u - 2)))
        out2[lax.rem(u, 2)] = dot_tn(big[:, OWN:KCOL], tokens(u)).astype(BF16)
        start(out2_copies(u))

    ticks = 2 * EARLY + 1

    def first_half(u):
        scatter.tick(ticks + u)
        grad_in(u)
        kv_step(u)

    def second_half(u):
        pl.when(lax.rem(u, 2) == 0)(lambda: scatter.tick(ticks + STEPS + lax.div(u, 2)))
        grad_out(u)

    loop(STEPS, first_half)
    loop(STEPS, second_half)
    for u in (STEPS - 2, STEPS - 1):
        wait(out_copies(u) + out2_copies(u))
    wait(kv_out)
    for group in hops.values():
        wait_send(group)
    scatter.finish()


def scatter_call(*args):
    any_spec = pl.BlockSpec(memory_space=pl.ANY)
    dma = pltpu.SemaphoreType.DMA
    shapes = [(2, 2, GROUP - EARLY, ROWS, DIM), (DIM, FFN), (DIM, FFN), (HEAD, DIM), (FFN, DIM), (HEAD, DIM), (HEAD, DIM), (HEAD, DIM)]
    half = DIM // 2
    assert STEPS + STEPS // 2 >= 2 * (GROUP - EARLY) + DEPTH - 1
    narrow = [(2 * NEAR, NBIG), (2, 2, GROUP, *TALL, TILE), (2, TILE, 2 * FFN), (2, HEAD, TILE), (2, OUT, TILE)]
    sums = [(KV, DIM), (KV, half), (2, KV, EIGHTH), (2, KV, W), (KV, 2 * W), (3, KROWS, 2 * W)]
    return pl.pallas_call(
        scatter_kernel,
        out_shape=[jax.ShapeDtypeStruct(s, BF16) for s in shapes],
        in_specs=[any_spec] * len(args),
        out_specs=[any_spec] * len(shapes),
        scratch_shapes=[
            *[pltpu.VMEM(s, BF16) for s in narrow],
            *[pltpu.VMEM(s, F32) for s in sums],
            pltpu.VMEM((KV, DIM), BF16),
            *[dma(s) for s in ((6,), (2, 2), (2, 3), (2, 2), (8, 6), (8, 6), (2,))],
            *scatter_scratch(),
        ],
        compiler_params=pltpu.CompilerParams(collective_id=1, has_side_effects=True, vmem_limit_bytes=VMEM_BYTES),
        name="scatter_grads",
    )(*args)


def total_kernel(part, out, acc, got, send, recv):
    spot = place()
    z = spot[0]
    partners = partners_of(*spot)
    entry_barrier(partners)
    near = partners[: len(partners) - 3]
    acc[0] = part[...]
    for k, there in enumerate(near):
        hop = remote(acc.at[k], got.at[k], (send.at[k], recv.at[k]), there)
        hop.start()
        hop.wait_recv()
        acc[k + 1] = acc[k] + got[k]
        hop.wait_send()
    last = len(near)
    hops = [remote(acc.at[last], out.at[z], (send.at[last + k], recv.at[last + k]), there) for k, there in enumerate(partners[last:])]
    start(hops)
    out[z] = acc[last]
    wait(hops)


def total_call(part):
    shape = (DIM // LANES, LANES)
    spec = pl.BlockSpec(memory_space=pltpu.VMEM)
    dma = pltpu.SemaphoreType.DMA
    chips = pl.pallas_call(
        total_kernel,
        out_shape=jax.ShapeDtypeStruct((4, *shape), F32),
        in_specs=[spec],
        out_specs=spec,
        scratch_shapes=[pltpu.VMEM((4, *shape), F32), pltpu.VMEM((3, *shape), F32), dma((6,)), dma((6,))],
        compiler_params=pltpu.CompilerParams(collective_id=2, has_side_effects=True),
        name="total_gain",
    )(part.reshape(shape))
    return jnp.sum(chips, axis=0).reshape(DIM)


def rope_tables():
    inv_freq = ROPE_BASE ** (-jnp.arange(HEAD // 2, dtype=F32) * 2.0 / HEAD)
    pos = row_position(jnp.arange(SEQ, dtype=jnp.int32)).astype(F32)
    angles = pos[:, None] * inv_freq[None, :]
    cos, sin = jnp.cos(angles), jnp.sin(angles)
    return jnp.concatenate([cos, cos], axis=1), jnp.concatenate([-sin, sin], axis=1)


def solution(mesh):
    def layer_shard(x_loc, dy_loc, ln_gain, w_query, w_key, w_value, w_out, w_gate, w_up, w_down):
        def mean(v):
            return jnp.mean(v, axis=-1, keepdims=True)

        residual = x_loc.astype(F32)
        centered = residual - mean(residual)
        inv_std = lax.rsqrt(mean(centered * centered) + LN_EPS)
        x_hat = centered * inv_std
        h_loc = (ln_gain * x_hat).astype(BF16)
        wq = w_query.reshape(DIM, HEAD)
        wo = w_out.reshape(HEAD, DIM)
        *kept, early = gather_call(h_loc, dy_loc, w_gate, w_up, wq, w_key, w_value, w_down, wo, *rope_tables())
        late, dw1, dw3, dwq, dw2, dwo, dwk, dwv = scatter_call(*kept)
        sums = jnp.concatenate([early, late], axis=2).reshape(2, ITEMS, ROWS, DIM).astype(F32)
        y_loc = (residual + sums[0]).astype(BF16)
        grad_normed = sums[1]
        grad_gain = total_call(jnp.sum(grad_normed * x_hat, axis=(0, 1)))
        grad_hat = grad_normed * ln_gain
        grad_x = inv_std * (grad_hat - mean(grad_hat) - x_hat * mean(grad_hat * x_hat)) + dy_loc.astype(F32)
        grad_query = dwq.T.reshape(DIM, 1, HEAD)
        return y_loc, grad_x.astype(BF16), grad_gain, grad_query, dwk.T, dwv.T, dwo.reshape(1, HEAD, DIM), dw1, dw3, dw2

    act = P(None, "tp", None)
    head, columns, lead, every = P(None, "tp", None), P(None, "tp"), P("tp"), P()
    specs = (act, act, every, head, every, every, lead, columns, columns, lead)
    return jax.shard_map(layer_shard, mesh=mesh, in_specs=specs, out_specs=specs, check_vma=False)
```

time: 1590 us -> 617 us (0.39)
  waiting for transfers between devices: 843 us -> 0 us
  Pallas kernels: 0 us -> 586 us
  matrix products: 549 us -> 0 us
  blocking collectives: 102 us -> 0 us
  local copies, waits for them, and re-layouts: 53.8 us -> 17.6 us
    pallas_call x0 -> x3, Pallas kernels: none -> 586 us  [the longest x1 417 us: gather_call(): pl.pallas_call(gather_kernel, out_shape=[jax.ShapeDtypeStruct(s, BF16) fo...]
    dot_general x27 -> x0, matrix products: 549 us -> none  [the longest x1 92.1 us: layer_shard(): jnp.einsum('blk,dk->bld', grad_values, w_value, preferred_element_type=jn...]
    unnamed x6 -> x0, waiting for transfers between devices: 489 us -> none
    all_gather x2 -> x0, waiting for transfers between devices: 354 us -> none  [the longest x1 195 us: layer_shard(): normed = lax.all_gather(normed_loc, 'tp', axis=1, tiled=True)]
    psum x1 -> x0, blocking collectives: 102 us -> none  [layer_shard(): grad_gain = lax.psum(jnp.sum(grad_normed_loc * x_hat, axis=(0, 1)), 'tp')]
    unnamed x76 -> x39, local copies, waits for them, and re-layouts: 53.8 us -> 17.1 us
  transfers between devices with their start and end apart: 4 -> 0, of which waited for: 4 -> 0; matrix products, arithmetic and copies ran while one was open for 17% -> 0% of each run, Pallas kernels for 0% -> 0%
where the time goes in v2:
time: 617 us; the launch traced here: 616 us
  Pallas kernels  586 us (95%)
  local copies, waits for them, and re-layouts  17.6 us (3%)
  other arithmetic  11.9 us (2%)
    pallas_call x1, Pallas kernels, gather_call(): pl.pallas_call(gather_kernel, out_shape=[jax.ShapeDtypeStruct(s, BF16) fo...  417 us
    pallas_call x1, Pallas kernels, scatter_call(): pl.pallas_call(scatter_kernel, out_shape=[jax.ShapeDtypeStruct(s, BF16) f...  156 us
    unnamed x39, local copies, waits for them, and re-layouts  17.1 us
    pallas_call x1, Pallas kernels, total_call(): pl.pallas_call(total_kernel, out_shape=jax.ShapeDtypeStruct((4, *shape),...  13.8 us

profile of v2, /device:TPU:0, one launch (start us, length us, event | category | flops | bytes accessed | tf_op | source)
XLA Modules:
  0.0 616.3 jit_solution(14779565441450596702)
XLA Ops:
  0.6 0.0 copy-start
  0.7 0.0 copy-start.12
  0.7 1.5 convert_reduce_fusion
  2.2 0.0 copy-start.10
  2.2 1.7 fusion.13
  3.9 0.0 copy-start.14
  3.9 0.5 fusion.15
  4.4 0.8 pad_maximum_fusion
  5.3 0.0 copy-done.10
  5.3 0.0 copy-done.14
  5.3 0.0 copy-done
  5.3 0.0 copy-done.12
  5.3 1.4 fusion.6.h_loc
  6.7 416.7 %gather_layer.1 = (bf16[8,2,2,2,64,4096]{5,4,3,2,1,0:T(8,128)(2,1)}, bf16[8,2,2,2,64,4096]{5,4,3,2,1,0:T(8,128)(2,1)}, bf16[16,2,2,64,4096]{4,3,2,1,0:T(8,128)(2...) custom-call(bf16[16,8,4096]{2,1,0:T(8,128)(2,1)} %fusion.6.h_loc, ...), custom_call_target="tpu_custom_call" | custom-call | tf_op jit(solution)/shard_map/gather_layer/pallas_call | solution.py:658
  423.4 155.6 %scatter_grads.1 = (bf16[2,2,3,8,4096]{4,3,2,1,0:T(8,128)(2,1)}, bf16[4096,512]{1,0:T(8,128)(2,1)}, bf16[4096,512]{1,0:T(8,128)(2,1)}, bf16[128,4096]{1,0:T(8,12...) custom-call(bf16[8,2,2,2,64,4096]{5,4,3,2,1,0:T(8,128)(2,1)} %get-tu, ...), custom_call_target="tpu_custom_call" | custom-call | tf_op jit(solution)/shard_map/scatter_grads/pallas_call | solution.py:862
  579.0 0.0 copy-start.8
  579.0 0.0 copy-start.7
  579.0 2.4 copy.20
  581.4 0.0 copy-done.8
  581.4 0.0 copy-start.5
  581.4 1.3 copy.21
  582.7 0.0 copy-done.7
  582.7 0.0 copy-start.9
  582.7 1.3 copy.22
  584.0 0.0 copy-done.5
  584.0 0.0 copy-done.9
  584.0 0.3 maximum_convert_fusion
  584.3 0.0 copy-start.1
  584.3 0.0 copy-start.11
  584.3 0.0 copy-start.13
  584.4 0.0 copy-start.15
  584.4 0.4 fusion.28
  584.8 0.7 copy-done.1
  585.5 0.0 copy-done.11
  585.5 0.0 copy-done.13
  585.5 0.0 copy-done.15
  585.6 1.6 multiply_reduce_fusion
  587.1 0.0 copy-done.4
  587.1 2.6 fusion.11
  589.7 13.8 %total_gain.1 = f32[4,32,128]{2,1,0:T(8,128)} custom-call(f32[32,128]{1,0:T(8,128)} %bitcast.22), custom_call_target="tpu_custom_call" | custom-call | tf_op jit(solution)/shard_map/total_gain/pallas_call | solution.py:903
  603.5 1.5 reduce_sum.59
  605.0 0.0 copy-done.6
  605.0 1.0 copy.27
  606.0 4.6 copy.28
  610.6 0.0 copy-done.3
  610.6 2.1 copy.29
  612.8 1.6 copy-done.2
  614.3 2.0 copy.30
  (10 shorter events, 0.0 us)
Async XLA Ops:
  0.6 4.7 copy-start
  0.7 4.6 copy-start.12
  2.2 3.1 copy-start.10
  3.9 1.4 copy-start.14
  579.0 2.4 copy-start.8
  579.0 3.7 copy-start.7
  581.4 2.6 copy-start.5
  582.7 1.3 copy-start.9
  584.3 1.2 copy-start.1
  584.3 1.2 copy-start.11
  584.3 1.2 copy-start.13
  584.4 1.2 copy-start.15
  585.6 1.6 copy-start.4
  587.1 17.9 %copy-start.6 = (bf16[128,4096]{1,0:T(8,128)(2,1)S(1)}, bf16[128,4096]{1,0:T(8,128)(2,1)}, u32[]{:S(2)}) copy-start(bf16[128,4096]{1,0:T(8,128)(2,1)} %get-tuple-element.38) | copy-start | bytes 3145732
  606.0 4.6 copy-start.3
  610.6 3.7 copy-start.2

commit v3 on v2

v3 whole, which is shorter than its diff:
```python
import jax
import jax.numpy as jnp
from jax import lax
from jax.experimental import pallas as pl
from jax.experimental.pallas import tpu as pltpu
from jax.sharding import PartitionSpec as P

LN_EPS = 1e-6
ROPE_BASE = 10000.0
MESH = pl.DeviceIdType.MESH
F32 = jnp.float32
BF16 = jnp.bfloat16
ALL = slice(None)
PAIR = range(2)
LANES = 128
W = 256
VMEM_BYTES = 67043328

GROUP = 8
ITEMS = 2 * GROUP
ROWS = 8
BLOCK = 2 * ROWS
LINE = 4 * BLOCK
SEQ = 4 * LINE
TALL = (2, 2, LINE)
DIM = 4096
HEAD = 128
FFN = 512
OUT = FFN + HEAD
OWN = 2 * FFN + HEAD
KEY = 2 * OWN
VAL = KEY + HEAD
NCAT = VAL + HEAD
NZO = 2 * OUT
QCOL = (2 * FFN, OWN + 2 * FFN)
OCOL = (2 * FFN, 2 * FFN + HEAD)
NEAR = GROUP * SEQ

SLOW = 3
DEPTH = 5
COPIES = 14


class Columns:
    def __init__(self, a):
        self.a, self.c = a, DIM // 2 - a
        self.left = (slice(0, a), slice(a, 2 * a))
        self.both_left = slice(0, 2 * a)
        self.right = (slice(2 * a, 2 * a + self.c), slice(2 * a + self.c, DIM))
        self.both_right = slice(2 * a, DIM)
        self.halves = (slice(0, self.c), slice(self.c, 2 * self.c))


GCOL = SCOL = Columns(1280)


def place():
    i = lax.axis_index("tp")
    return lax.div(i, 8), lax.rem(lax.div(i, 4), 2), lax.rem(lax.div(i, 2), 2), lax.rem(i, 2)


def index(z, y, x, core):
    return ((z * 2 + y) * 2 + x) * 2 + core


def rows8(start, size):
    return pl.ds(pl.multiple_of(start, ROWS), size)


def rows16(start, size):
    return pl.ds(pl.multiple_of(start, BLOCK), size)


def lanes(start, size):
    return pl.ds(pl.multiple_of(start, LANES), size)


def step_of(t, size):
    return lanes(t * size, size)


def loop(count, body):
    lo, hi = count if isinstance(count, tuple) else (0, count)

    def run(i, carry):
        body(i)
        return carry

    lax.fori_loop(lo, hi, run, 0)


def remote(src, dst, sems, target):
    return pltpu.make_async_remote_copy(src, dst, *sems, device_id=(target,), device_id_type=MESH)


def start(copies):
    for c in copies:
        c.start()


def wait(copies):
    for c in copies:
        c.wait()


def wait_recv(copies):
    for c in copies:
        c.wait_recv()


def wait_send(copies):
    for c in copies:
        c.wait_send()


def partners_of(z, y, x, core):
    chips = [index(lax.rem(z + k, 4), y, x, core) for k in (1, 2, 3)]
    return [index(z, y, x, 1 - core), index(z, y, 1 - x, core), index(z, 1 - y, x, core)] + chips


def entry_barrier(partners):
    barrier = pltpu.get_barrier_semaphore()
    for partner in partners:
        pl.semaphore_signal(barrier, inc=1, device_id=(partner,), device_id_type=MESH)
    pl.semaphore_wait(barrier, len(partners))


def dot_nt(a, b):
    return lax.dot_general(a, b, (((1,), (1,)), ((), ())), preferred_element_type=F32)


def dot_tn(a, b):
    return lax.dot_general(a, b, (((0,), (0,)), ((), ())), preferred_element_type=F32)


def dot_nn(a, b):
    return jnp.dot(a, b, preferred_element_type=F32)


def add_into(dst, src, width):
    def tile(t):
        cols = step_of(t, W)
        dst[..., cols] = (dst[..., cols].astype(F32) + src[..., cols].astype(F32)).astype(BF16)

    loop(width // W, tile)


def row_position(r):
    return ((r // BLOCK) % 4) * LINE + (r // (2 * LINE)) * (2 * BLOCK) + ((r // LINE) % 2) * BLOCK + r % BLOCK


class Line:
    def __init__(self, z, y, x, core):
        low = lax.div(z, 2)
        odd = lax.rem(z, 2)
        self.mid = low != odd
        self.end = low == odd
        side = index(z + 1 - 2 * odd, y, x, core)
        across = index(3 - z, y, x, core)
        self.three = rows16(BLOCK - BLOCK * low, 3 * BLOCK)
        self.half = rows16(2 * BLOCK * low, 2 * BLOCK)
        self.other = rows16(2 * BLOCK - 2 * BLOCK * low, 2 * BLOCK)
        self.tip = rows16(3 * BLOCK * low, BLOCK)
        self.own = rows16(BLOCK * z, BLOCK)
        self.spread = ((self.own, side), (self.half, across), (self.three, side))
        self.merge = ((self.three, side), (self.other, across), (self.tip, side))


class Transfer:
    def __init__(self, spot, send, recv):
        self.z, self.y, self.x, self.core = spot
        self.line = Line(*spot)
        self.sib, self.xn, self.yn, *self.zn = partners_of(*spot)
        self.send, self.recv, self.keys = send, recv, {}

    def sems(self, slot, key):
        k = self.keys.setdefault(key, len(self.keys))
        return self.send.at[slot, k], self.recv.at[slot, k]

    def on_end(self, body):
        pl.when(self.line.end)(body)

    def on_mid(self, body):
        pl.when(self.line.mid)(body)

    def tick(self, m):
        for k, stage in reversed(list(enumerate(self.stages))):
            n = m - k
            pl.when((n >= 0) & (n < ITEMS))(lambda stage=stage, n=n: stage(n))


class Gather(Transfer):
    def __init__(self, spot, buf, send, recv):
        super().__init__(spot, send, recv)
        self.buf = buf
        self.stages = (self.stage0, self.stage1, self.stage2, self.stage3, self.stage4, self.stage5)

    def copy(self, n, key, ys, xs, rows, cols, target):
        view = self.buf.at[lax.div(n, 2), lax.rem(n, 2), ys, xs, rows, cols]
        return remote(view, view, self.sems(n, key), target)

    def za(self, n, step):
        rows, target = self.line.spread[step]
        return self.copy(n, ("za", step), self.y, self.x, rows, GCOL.both_left, target)

    def zc(self, n, step):
        rows, target = self.line.spread[step]
        return self.copy(n, ("zc", step), ALL, ALL, rows, GCOL.both_right, target)

    def c1(self, n):
        cols, own = GCOL.right, self.line.own
        return [self.copy(n, "c1x", self.y, self.x, own, cols[0], self.xn), self.copy(n, "c1y", self.y, self.x, own, cols[1], self.yn)]

    def c2(self, n):
        cols, own = GCOL.right, self.line.own
        return [self.copy(n, "c2y", self.y, ALL, own, cols[0], self.yn), self.copy(n, "c2x", ALL, self.x, own, cols[1], self.xn)]

    def a1(self, n):
        cols = GCOL.left
        return [self.copy(n, "a1y", self.y, self.x, ALL, cols[0], self.yn), self.copy(n, "a1x", self.y, self.x, ALL, cols[1], self.xn)]

    def a2(self, n):
        cols = GCOL.left
        return [self.copy(n, "a2x", ALL, self.x, ALL, cols[0], self.xn), self.copy(n, "a2y", self.y, ALL, ALL, cols[1], self.yn)]

    def pass_on(self, chain, n, step):
        def body():
            chain(n, step - 1).wait_recv()
            chain(n, step).start()

        self.on_mid(body)

    def stage0(self, n):
        self.on_end(lambda: self.za(n, 0).start())
        start(self.c1(n))

    def stage1(self, n):
        self.pass_on(self.za, n, 1)
        wait_recv(self.c1(n))
        start(self.c2(n))

    def stage2(self, n):
        self.pass_on(self.za, n, 2)
        wait_recv(self.c2(n))
        self.on_end(lambda: self.zc(n, 0).start())

    def stage3(self, n):
        self.on_end(lambda: self.za(n, 2).wait_recv())
        start(self.a1(n))
        self.pass_on(self.zc, n, 1)

    def stage4(self, n):
        wait_recv(self.a1(n))
        start(self.a2(n))
        self.pass_on(self.zc, n, 2)

    def stage5(self, n):
        wait_recv(self.a2(n))
        self.on_end(lambda: self.zc(n, 2).wait_recv())

    def finish(self, n):
        wait_send(self.c1(n) + self.c2(n) + self.a1(n) + self.a2(n))
        self.on_end(lambda: wait_send([self.za(n, 0), self.zc(n, 0)]))
        self.on_mid(lambda: wait_send([chain(n, step) for chain in (self.za, self.zc) for step in (1, 2)]))


def scatter_shapes():
    a, c = SCOL.a, SCOL.c
    return dict(
        b1=(3, 2, 2, LINE, a), b2=(5, 2, LINE, a), za0=(3, 2, 3 * BLOCK, a), za1=(3, 2, 2 * BLOCK, a), za2=(4, 2, BLOCK, a),
        own_a=(2, 2, 2, LINE, a), own_c=(4, *TALL, 2 * c), zc0=(3, 2, 2, 3 * BLOCK, 2 * c), zc1=(3, 2, 2, 2 * BLOCK, 2 * c),
        zc2=(4, 2, 2, BLOCK, 2 * c), h1=(3, 2, 2, BLOCK, c), h2=(3, 2, BLOCK, c), fin=(3, 2, ROWS, DIM),
    )


SLOTS = 6


def scatter_scratch():
    dma = pltpu.SemaphoreType.DMA
    buffers = [pltpu.VMEM(s, BF16) for s in scatter_shapes().values()]
    return buffers + [dma((SLOTS, COPIES)), dma((SLOTS, COPIES)), dma((SLOTS, 3)), dma((ITEMS,)), dma((ITEMS,))]


class Scatter(Transfer):
    def __init__(self, spot, parts, sums, refs):
        shapes = scatter_shapes()
        self.depth = {name: s[0] for name, s in shapes.items()}
        self.ring = dict(zip(shapes, refs))
        send, recv, self.lsem, *self.store_sems = refs[len(shapes) :]
        super().__init__(spot, send, recv)
        self.parts, self.sums = parts, sums
        self.stages = (self.stage0, self.stage1, self.stage2, self.stage3, self.stage4, self.stage5)

    def slot(self, name, n, *at):
        return self.ring[name].at[(lax.rem(n, self.depth[name]), *at)]

    def copy(self, n, key, src, dst, target):
        return remote(src, dst, self.sems(lax.rem(n, SLOTS), key), target)

    def a1(self, n):
        cols = SCOL.left
        return [
            self.copy(n, "a1x", self.parts.at[n, :, 1 - self.x, :, cols[0]], self.slot("b1", n, 0), self.xn),
            self.copy(n, "a1y", self.parts.at[n, 1 - self.y, :, :, cols[1]], self.slot("b1", n, 1), self.yn),
        ]

    def a2(self, n):
        return [
            self.copy(n, "a2y", self.slot("b1", n, 0, 1 - self.y), self.slot("b2", n, 0), self.yn),
            self.copy(n, "a2x", self.slot("b1", n, 1, 1 - self.x), self.slot("b2", n, 1), self.xn),
        ]

    def za(self, n, step):
        rows, target = self.line.merge[step]
        key = f"za{step}"
        return self.copy(n, key, self.slot("b2", n, ALL, rows, ALL), self.slot(key, n), target)

    def zc(self, n, step):
        rows, target = self.line.merge[step]
        key = f"zc{step}"
        src = self.slot("own_c", n, ALL, ALL, rows, ALL) if step else self.parts.at[n, :, :, rows, SCOL.both_right]
        return self.copy(n, key, src, self.slot(key, n), target)

    def h1(self, n):
        cols = SCOL.halves
        return [
            self.copy(n, "h1y", self.slot("zc2", n, 1 - self.y, ALL, ALL, cols[0]), self.slot("h1", n, 0), self.yn),
            self.copy(n, "h1x", self.slot("zc2", n, ALL, 1 - self.x, ALL, cols[1]), self.slot("h1", n, 1), self.xn),
        ]

    def h2(self, n):
        cols = SCOL.halves
        return [
            self.copy(n, "h2x", self.slot("zc2", n, self.y, 1 - self.x, ALL, cols[0]), self.slot("h2", n, 0), self.xn),
            self.copy(n, "h2y", self.slot("zc2", n, 1 - self.y, self.x, ALL, cols[1]), self.slot("h2", n, 1), self.yn),
        ]

    def loads(self, n):
        sem = self.lsem.at[lax.rem(n, SLOTS)]
        views = (
            (self.parts.at[n, :, self.x, :, SCOL.left[0]], self.slot("own_a", n, 0)),
            (self.parts.at[n, self.y, :, :, SCOL.left[1]], self.slot("own_a", n, 1)),
            (self.parts.at[n, :, :, :, SCOL.both_right], self.slot("own_c", n)),
        )
        return [pltpu.make_async_copy(src, dst, sem.at[k]) for k, (src, dst) in enumerate(views)]

    def kept(self, n):
        return self.sums.at[lax.rem(n, 2), self.core, lax.div(n, 2)]

    def store(self, n):
        send, recv = self.store_sems
        return remote(self.slot("fin", n, 1 - self.core), self.kept(n), (send.at[n], recv.at[n]), self.sib)

    def stage0(self, n):
        start(self.a1(n))
        self.on_end(lambda: self.zc(n, 0).start())
        start(self.loads(n))

    def stage1(self, n):
        wait(self.loads(n))
        wait_recv(self.a1(n))
        for c in PAIR:
            add_into(self.slot("b1", n, c), self.slot("own_a", n, c), SCOL.a)
        start(self.a2(n))

        def middle():
            self.zc(n, 0).wait_recv()
            add_into(self.slot("own_c", n, ALL, ALL, self.line.three), self.slot("zc0", n), 2 * SCOL.c)
            self.zc(n, 1).start()

        self.on_mid(middle)
        wait_send(self.a1(n))
        self.on_end(lambda: self.zc(n, 0).wait_send())

    def stage2(self, n):
        wait_recv(self.a2(n))
        for c, mine in enumerate((self.y, self.x)):
            add_into(self.slot("b2", n, c), self.slot("b1", n, c, mine), SCOL.a)
        self.on_end(lambda: self.za(n, 0).start())

        def middle():
            self.zc(n, 1).wait_recv()
            add_into(self.slot("own_c", n, ALL, ALL, self.line.half), self.slot("zc1", n), 2 * SCOL.c)
            self.zc(n, 2).start()
            self.zc(n, 1).wait_send()

        self.on_mid(middle)
        wait_send(self.a2(n))

    def stage3(self, n):
        own_c = self.slot("own_c", n, ALL, ALL, self.line.own)

        def middle():
            self.za(n, 0).wait_recv()
            add_into(self.slot("b2", n, ALL, self.line.three), self.slot("za0", n), SCOL.a)
            self.za(n, 1).start()
            self.slot("zc2", n)[...] = own_c[...]

        def tip():
            self.zc(n, 2).wait_recv()
            add_into(self.slot("zc2", n), own_c, 2 * SCOL.c)

        self.on_mid(middle)
        self.on_end(tip)
        start(self.h1(n))
        self.on_mid(lambda: self.zc(n, 2).wait_send())
        self.on_end(lambda: self.za(n, 0).wait_send())

    def stage4(self, n):
        def middle():
            self.za(n, 1).wait_recv()
            add_into(self.slot("b2", n, ALL, self.line.half), self.slot("za1", n), SCOL.a)
            self.za(n, 2).start()
            self.za(n, 1).wait_send()

        self.on_mid(middle)
        wait_recv(self.h1(n))
        cols = SCOL.halves
        add_into(self.slot("zc2", n, self.y, ALL, ALL, cols[0]), self.slot("h1", n, 0), SCOL.c)
        add_into(self.slot("zc2", n, ALL, self.x, ALL, cols[1]), self.slot("h1", n, 1), SCOL.c)
        start(self.h2(n))
        wait_send(self.h1(n))

    def stage5(self, n):
        pl.when(n >= self.depth["fin"])(lambda: self.store(n - self.depth["fin"]).wait_send())

        def tip():
            self.za(n, 2).wait_recv()
            add_into(self.slot("b2", n, ALL, self.line.own), self.slot("za2", n), SCOL.a)

        self.on_end(tip)
        self.on_mid(lambda: self.za(n, 2).wait_send())
        wait_recv(self.h2(n))
        fin = self.slot("fin", n)

        def put(total, col):
            for core in PAIR:
                fin[core, :, lanes(col, W)] = total[core * ROWS : (core + 1) * ROWS].astype(BF16)

        def left(t):
            for c in PAIR:
                put(self.slot("b2", n, c, self.line.own)[:, step_of(t, W)].astype(F32), c * SCOL.a + t * W)

        def right(t):
            for c in PAIR:
                mine = self.slot("zc2", n, self.y, self.x)[:, lanes(c * SCOL.c + t * W, W)].astype(F32)
                put(mine + self.slot("h2", n, c)[:, step_of(t, W)].astype(F32), 2 * SCOL.a + c * SCOL.c + t * W)

        loop(SCOL.a // W, left)
        loop(SCOL.c // W, right)
        self.store(n).start()
        self.kept(n)[...] = fin[self.core]
        wait_send(self.h2(n))

    def finish(self):
        loop((ITEMS - self.depth["fin"], ITEMS), lambda n: self.store(n).wait_send())
        loop(ITEMS, lambda n: self.store(n).wait_recv())


TILE = 512
STEPS = DIM // TILE
KV = 2 * HEAD
KCOL = OWN + OUT
NBIG = KCOL + KV
QUARTER = DIM // 4
EIGHTH = DIM // 8
KROWS = KV // 4


def layer_kernel(
    h_loc, dy_tok, x_loc, dy_loc, w1, w3, wq, wk, wv, w2, wo, gain, cos_t, sin_t,
    full, full_sib, parts, g_all, zo_all, g_sib, zo_sib, y_out, dx_out, dgain, dw1, dw3, dwq, dw2, dwo, dwk, dwv,
    gsend, grecv, sx, rx, sw, rw, ss, rs, sg, rg, ksend, krecv, lsem, wsem, osem, gsem,
    tsem, o1sem, o2sem, hsend, hrecv, ready, sums, *scatter_refs,
):
    spot = place()
    z, y, x, core = spot
    partners = partners_of(*spot)
    sib, xn, yn, *zn = partners
    entry_barrier(partners)
    gather = Gather(spot, full, gsend, grecv)
    scatter = Scatter(spot, parts, sums, scatter_refs)

    def meet(others):
        for there in others:
            pl.semaphore_signal(ready, inc=1, device_id=(there,), device_id_type=MESH)
        pl.semaphore_wait(ready, len(others))

    def activations(wcat, w2o, hv, dyv, proj, zo, g, yo, dho, probs, qs, stage):
        mine = rows8(BLOCK * z + ROWS * core, ROWS)
        locs = (h_loc, dy_tok)
        to = [full.at[:, s, y, x, mine, :] for s in PAIR]
        swaps = [remote(locs[s].at[rows8(GROUP * (1 - core), GROUP)], to[s], (sx.at[s], rx.at[s]), sib) for s in PAIR]
        takes = [pltpu.make_async_copy(locs[s].at[rows8(GROUP * core, GROUP)], stage.at[s], lsem.at[s]) for s in PAIR]
        puts = [pltpu.make_async_copy(stage.at[s], to[s], lsem.at[s]) for s in PAIR]
        start(swaps + takes)
        for s in PAIR:
            takes[s].wait()
            puts[s].start()
        wait(puts)
        wait_recv(swaps)
        loop(2, gather.tick)

        spots = (
            (w1, wcat.at[:, 0:FFN], wcat.at[:, OWN : OWN + FFN]),
            (w3, wcat.at[:, FFN : 2 * FFN], wcat.at[:, OWN + FFN : OWN + 2 * FFN]),
            (wq, wcat.at[:, 2 * FFN : OWN], wcat.at[:, OWN + 2 * FFN : KEY]),
            (w2, w2o.at[0:FFN], w2o.at[FFN : 2 * FFN]),
            (wo, w2o.at[OCOL[0] : OCOL[1]], w2o.at[OCOL[1] : NZO]),
        )
        shared = ((wk, wcat.at[:, KEY:VAL]), (wv, wcat.at[:, VAL:NCAT]))
        weights = [(w, near) for w, near, _ in spots] + list(shared)
        local = [pltpu.make_async_copy(w, near, wsem.at[k]) for k, (w, near) in enumerate(weights)]
        far = [remote(w, there, (sw.at[k], rw.at[k]), sib) for k, (w, _, there) in enumerate(spots)]
        start(local)
        meet([sib])
        start(far)
        loop((2, DEPTH + 1), gather.tick)

        def load(b, s):
            return pltpu.make_async_copy(full.at[b, s], (hv, dyv)[s], lsem.at[s])

        def sib_copy(b, s):
            return remote(full.at[b, s], full_sib.at[b, s], (ss.at[b, s], rs.at[b, s]), sib)

        def arrived(b, s):
            load(b, s).start()
            sib_copy(b, s).start()

        arrived(0, 0)
        wait(local)
        wait_recv(far)

        def gz_copies(b):
            rows = rows16(b * SEQ, SEQ)
            views = (
                (g.at[:, OWN:KEY], g_sib.at[rows]),
                (zo.at[:, FFN : 2 * FFN], zo_sib.at[rows, 0:FFN]),
                (zo.at[:, OCOL[1] : NZO], zo_sib.at[rows, FFN:OUT]),
            )
            return [remote(src, dst, (sg.at[b, k], rg.at[b, k]), sib) for k, (src, dst) in enumerate(views)]

        def gz_local(b):
            rows = rows16(b * SEQ, SEQ)
            return [pltpu.make_async_copy(g, g_all.at[rows], gsem.at[0]), pltpu.make_async_copy(zo, zo_all.at[rows], gsem.at[1])]

        def out(b, s):
            return pltpu.make_async_copy((yo, dho)[s], parts.at[2 * b + s], osem.at[s])

        def drained(b):
            wait([*gz_local(b), out(b, 1)])
            wait_send(gz_copies(b))

        scale = HEAD ** -0.5

        def rotate(v, back=False):
            turn = pltpu.roll(v, HEAD // 2, 1) * sin_t[...]
            return v * cos_t[...] + (-turn if back else turn)

        def flat(ref):
            return ref[...].reshape(SEQ, DIM)

        def gate_up(t):
            at = t * W + lax.div(t, 2) * (OWN - FFN)
            return lanes(at, W), lanes(at + FFN, W)

        wide = lambda t: step_of(t, FFN)

        def batch_step(b):
            ahead = 2 * b + DEPTH + 1
            behind = b - 1 + lax.max(b - SLOW, 0)
            pl.when(b > 0)(lambda: out(b - 1, 0).wait())
            scatter.tick(behind)
            load(b, 0).wait()

            def proj_tile(t):
                proj[:, wide(t)] = dot_nn(flat(hv), wcat[:, wide(t)])

            loop(NCAT // FFN, proj_tile)
            pl.when(b > 0)(lambda: drained(b - 1))

            def hidden_tile(t):
                gate_at, up_at = gate_up(t)
                gate = proj[:, gate_at]
                zo[:, step_of(t, W)] = (gate * jax.nn.sigmoid(gate) * proj[:, up_at]).astype(BF16)

            loop(2 * FFN // W, hidden_tile)
            keys = rotate(proj[:, KEY:VAL]).astype(BF16)
            vals = proj[:, VAL:NCAT].astype(BF16)
            qs[2] = keys
            qs[3] = vals
            causal = row_position(lax.broadcasted_iota(jnp.int32, (SEQ, SEQ), 0)) >= row_position(lax.broadcasted_iota(jnp.int32, (SEQ, SEQ), 1))
            for hd in PAIR:
                query = rotate(proj[:, QCOL[hd] : QCOL[hd] + HEAD]).astype(BF16)
                qs[hd] = query
                scores = jnp.where(causal, dot_nt(query, keys) * scale, -1e30)
                e = jnp.exp(scores - jnp.max(scores, axis=-1, keepdims=True))
                p = e / jnp.sum(e, axis=-1, keepdims=True)
                probs[hd] = p
                zo[:, OCOL[hd] : OCOL[hd] + HEAD] = dot_nn(p.astype(BF16), vals).astype(BF16)

            gather.tick(ahead)
            arrived(b, 1)

            def y_tile(t):
                yo[:, :, :, wide(t)] = dot_nn(zo[...], w2o[:, wide(t)]).astype(BF16).reshape(*TALL, FFN)

            loop(DIM // FFN, y_tile)
            out(b, 0).start()
            load(b, 1).wait()

            def dz_tile(t):
                dz = dot_nt(flat(dyv), w2o[rows16(t * W, W), :])
                gate_at, up_at = gate_up(t)
                gate = proj[:, gate_at]
                sig = jax.nn.sigmoid(gate)
                g[:, gate_at] = (dz * proj[:, up_at] * sig * (1.0 + gate * (1.0 - sig))).astype(BF16)
                g[:, up_at] = (dz * (gate * sig)).astype(BF16)

            loop(2 * FFN // W, dz_tile)
            pl.when(b >= SLOW)(lambda: scatter.tick(behind + 1))
            d_heads = dot_nt(flat(dyv), w2o[2 * FFN : NZO, :]).astype(BF16)
            d_keys = d_vals = jnp.zeros((SEQ, HEAD), F32)
            for hd in PAIR:
                d_out = d_heads[:, hd * HEAD : (hd + 1) * HEAD]
                p = probs[hd]
                d_probs = dot_nt(d_out, qs[3])
                d_vals = d_vals + dot_tn(p.astype(BF16), d_out)
                row_dot = jnp.sum(p * d_probs, axis=-1, keepdims=True)
                d_scores = (p * (d_probs - row_dot) * scale).astype(BF16)
                g[:, QCOL[hd] : QCOL[hd] + HEAD] = rotate(dot_nn(d_scores, qs[2]), True).astype(BF16)
                d_keys = d_keys + dot_tn(d_scores, qs[hd])
            g[:, KEY:VAL] = rotate(d_keys, True).astype(BF16)
            g[:, VAL:NCAT] = d_vals.astype(BF16)
            gather.tick(ahead + 1)
            pl.when(b < GROUP - 1)(lambda: arrived(b + 1, 0))

            def dh_tile(t):
                dho[:, :, :, wide(t)] = dot_nt(g[...], wcat[rows16(t * FFN, FFN), :]).astype(BF16).reshape(*TALL, FFN)

            loop(DIM // FFN, dh_tile)
            out(b, 1).start()
            start(gz_local(b) + gz_copies(b))

        loop(GROUP, batch_step)
        out(GROUP - 1, 0).wait()
        drained(GROUP - 1)

        def finish(b):
            for s in PAIR:
                gather.finish(2 * b + s)
                sib_copy(b, s).wait()
            wait_recv(gz_copies(b))

        loop(GROUP, finish)
        wait_send(swaps + far)


    def gradients(big, tiles, out1, outq, out2, kvo, kvt, kvp, k1, k2, k3, kc, k4, gacc, gpart, ggot, gz):
        near, away = slice(0, NEAR), slice(NEAR, 2 * NEAR)
        views = (
            (g_all.at[:, KEY:NCAT], big.at[near, KCOL:NBIG]),
            (g_all.at[:, 0:OWN], big.at[near, 0:OWN]),
            (g_sib, big.at[away, 0:OWN]),
            (zo_all.at[:, 0:FFN], big.at[near, OWN : OWN + FFN]),
            (zo_all.at[:, OCOL[0] : OCOL[1]], big.at[near, OWN + FFN : KCOL]),
            (zo_sib, big.at[away, OWN:KCOL]),
        )
        loads = [pltpu.make_async_copy(src, dst, lsem.at[k]) for k, (src, dst) in enumerate(views)]
        start(loads)

        def tile_load(u, s):
            slot = lax.rem(u, 2)
            sources = (full, full_sib)
            return [pltpu.make_async_copy(sources[k].at[:, s, :, :, :, step_of(u, TILE)], tiles.at[slot, k], tsem.at[slot, k]) for k in PAIR]

        tile_load(0, 0)[0].start()
        loads[0].wait()

        def kv_tile(u):
            pl.when(u < STEPS - 1)(lambda: tile_load(u + 1, 0)[0].start())
            tile_load(u, 0)[0].wait()
            kvp[:, step_of(u, TILE)] = dot_tn(big[near, KCOL:NBIG], tiles[lax.rem(u, 2), 0].reshape(NEAR, TILE))

        loop(STEPS, kv_tile)
        start(tile_load(0, 0))

        half = core * (DIM // 2)
        quarter = (half, half + QUARTER)
        ring = ((x, y, xn, yn), (y, x, yn, xn))
        first = [quarter[c] + ring[c][0] * EIGHTH for c in PAIR]
        second = [first[c] + ring[c][1] * W for c in PAIR]
        mine = rows16(z * KROWS, KROWS)
        hops = {}

        def hop(step, src, dst, target):
            group = hops.setdefault(step, [])
            group.append(remote(src, dst, (ksend.at[step, len(group)], krecv.at[step, len(group)]), target))

        hop(0, kvp.at[:, lanes(DIM // 2 - half, DIM // 2)], k1, sib)
        for c in PAIR:
            a, b, an, bn = ring[c]
            hop(1, kvp.at[:, lanes(quarter[c] + (1 - a) * EIGHTH, EIGHTH)], k2.at[c], an)
            hop(2, kvp.at[:, lanes(first[c] + (1 - b) * W, W)], k3.at[c], bn)
            same = kvo.at[:, lanes(second[c], W)]
            hop(5, same, same, bn)
            same = kvo.at[:, lanes(first[c], EIGHTH)]
            hop(6, same, same, an)
        for k, there in enumerate(zn):
            hop(3, kc.at[rows16(lax.rem(z + k + 1, 4) * KROWS, KROWS)], k4.at[k], there)
            for c in PAIR:
                same = kvo.at[mine, lanes(second[c], W)]
                hop(4, same, same, there)
        same = kvo.at[:, lanes(half, DIM // 2)]
        hop(7, same, same, sib)

        def kv_add(src, at, width):
            def tile(t):
                cols = lanes(at + t * W, W)
                kvp[:, cols] = kvp[:, cols] + src[:, step_of(t, W)]

            loop(width // W, tile)

        def kv_first():
            kv_add(k1, half, DIM // 2)

        def kv_second():
            for c in PAIR:
                kv_add(k2.at[c], first[c], EIGHTH)

        def kv_third():
            for c in PAIR:
                kc[:, c * W : (c + 1) * W] = kvp[:, lanes(second[c], W)] + k3[c]

        def kv_round():
            total = kc[mine, :] + k4[0] + k4[1] + k4[2]
            for c in PAIR:
                kvo[mine, lanes(second[c], W)] = total[:, c * W : (c + 1) * W].astype(BF16)

        def kv_turn(t):
            rows = step_of(t, TILE)
            for s in PAIR:
                kvt[s] = kvo[s * HEAD : (s + 1) * HEAD, rows].astype(F32).T.astype(BF16)
            copies = [pltpu.make_async_copy(kvt.at[s], (dwk, dwv)[s].at[rows], osem.at[s]) for s in PAIR]
            start(copies)
            wait(copies)

        works = (kv_first, kv_second, kv_third, kv_round)

        def kv_step(j):
            for step in range(len(hops)):

                @pl.when(j == step)
                def _(step=step):
                    wait_recv(hops[step])
                    if step < len(works):
                        works[step]()
                    elif step == len(hops) - 1:
                        loop(STEPS, kv_turn)
                    start(hops.get(step + 1, ()))

        meet(partners)
        start(hops[0])
        ticks = 2 * GROUP - 1 - SLOW
        scatter.tick(ticks)
        wait(loads[1:])

        def out_copies(u):
            slot = lax.rem(u, 2)
            rows = step_of(u, TILE)
            sem = o1sem.at[slot]
            return [
                pltpu.make_async_copy(out1.at[slot, :, 0:FFN], dw1.at[rows], sem.at[0]),
                pltpu.make_async_copy(out1.at[slot, :, FFN : 2 * FFN], dw3.at[rows], sem.at[1]),
                pltpu.make_async_copy(outq.at[slot], dwq.at[rows], sem.at[2]),
            ]

        def out2_copies(u):
            slot, cols = lax.rem(u, 2), step_of(u, TILE)
            sem = o2sem.at[slot]
            return [
                pltpu.make_async_copy(out2.at[slot, 0:FFN], dw2.at[:, cols], sem.at[0]),
                pltpu.make_async_copy(out2.at[slot, FFN:OUT], dwo.at[:, cols], sem.at[1]),
            ]

        def mean(v):
            return jnp.mean(v, axis=-1, keepdims=True)

        def token_step(i):
            first = i * 2
            spans = [rows16(k * ITEMS * ROWS + i * BLOCK, BLOCK) for k in range(4)]

            def total(s):
                return sums[s, lax.div(first, GROUP), pl.ds(lax.rem(first, GROUP), 2)].astype(F32).reshape(BLOCK, DIM)

            def both(k):
                return jnp.concatenate([big[spans[k], :], big[spans[k + 1], :]], axis=1).astype(F32)

            def keep(k, value):
                big[spans[k], :] = value[:, 0:NBIG].astype(BF16)
                big[spans[k + 1], :] = value[:, NBIG:DIM].astype(BF16)

            res = both(0)
            d_norm = total(1)
            centered = res - mean(res)
            inv_std = lax.rsqrt(mean(centered * centered) + LN_EPS)
            x_hat = centered * inv_std
            gacc[...] = gacc[...] + d_norm * x_hat
            d_hat = d_norm * gain[...]
            dx = inv_std * (d_hat - mean(d_hat) - x_hat * mean(d_hat * x_hat)) + both(2)
            keep(0, res + total(0))
            keep(2, dx)

        def tokens_of(arrays, inward):
            copies = []
            for k in range(4):
                here = big.at[k * ITEMS * ROWS : (k + 1) * ITEMS * ROWS]
                there = arrays[k // 2].at[:, k % 2 * NBIG : (k % 2 + 1) * NBIG]
                src, dst = (there, here) if inward else (here, there)
                copies.append(pltpu.make_async_copy(src, dst, lsem.at[k]))
            return copies

        tokens_in, results = tokens_of((x_loc, dy_loc), True), tokens_of((y_out, dx_out), False)
        gain_out = pltpu.make_async_copy(gpart.at[0], dgain, osem.at[0])

        def finalize():
            start(tokens_in)
            gacc[...] = jnp.zeros_like(gacc)
            wait(tokens_in)
            loop(GROUP, token_step)
            start(results)
            gpart[0] = jnp.sum(gacc[...], axis=0, keepdims=True)
            near = partners[:3]
            for k, there in enumerate(near):
                step = remote(gpart.at[k], ggot.at[k], (hsend.at[k], hrecv.at[k]), there)
                step.start()
                step.wait_recv()
                gpart[k + 1] = gpart[k] + ggot[k]
                step.wait_send()
            steps = [remote(gpart.at[3], gz.at[z], (hsend.at[3 + k], hrecv.at[3 + k]), there) for k, there in enumerate(zn)]
            start(steps)
            gz[z] = gpart[3]
            wait(steps)
            gpart[0] = gz[0] + gz[1] + gz[2] + gz[3]
            gain_out.start()
            gain_out.wait()

        def tokens(u):
            return tiles[lax.rem(u, 2)].reshape(2 * NEAR, TILE)

        def grad_in(u):
            wait(tile_load(u, 0))
            pl.when(u < STEPS - 1)(lambda: start(tile_load(u + 1, 0)))
            pl.when(u == STEPS - 1)(lambda: start(tile_load(0, 1)))
            pl.when(u > 1)(lambda: wait(out_copies(u - 2)))
            slot = lax.rem(u, 2)
            for s in PAIR:
                out1[slot, :, s * FFN : (s + 1) * FFN] = dot_tn(tokens(u), big[:, s * FFN : (s + 1) * FFN]).astype(BF16)
            outq[slot] = dot_tn(big[:, 2 * FFN : OWN], tokens(u)).T.astype(BF16)
            start(out_copies(u))

        def grad_out(u):
            wait(tile_load(u, 1))
            pl.when(u < STEPS - 1)(lambda: start(tile_load(u + 1, 1)))
            pl.when(u > 1)(lambda: wait(out2_copies(u - 2)))
            slot = lax.rem(u, 2)
            out2[slot, 0:FFN] = dot_tn(big[:, OWN : OWN + FFN], tokens(u)).astype(BF16)
            out2[slot, FFN:OUT] = dot_tn(big[:, OWN + FFN : KCOL], tokens(u)).astype(BF16)
            start(out2_copies(u))

        def pairs(first, grad):
            def body(j):
                scatter.tick(ticks + 1 + first + j)
                grad(2 * j)
                kv_step(first + j)
                grad(2 * j + 1)

            loop(STEPS // 2, body)

        pairs(0, grad_in)
        pairs(STEPS // 2, grad_out)
        scatter.finish()
        finalize()
        for u in (STEPS - 2, STEPS - 1):
            wait(out_copies(u) + out2_copies(u))
        wait(results)
        for group in hops.values():
            wait_send(group)


    tall = (*TALL, DIM)
    half = DIM // 2
    wide = [(DIM, NCAT), (NZO, DIM), tall, tall, (SEQ, NCAT), (SEQ, NZO), (SEQ, NCAT), tall, tall, (2, SEQ, SEQ), (4, SEQ, HEAD), (2, GROUP, ROWS, DIM)]
    types = [BF16] * 4 + [F32] + [BF16] * 4 + [F32] + [BF16] * 2
    pl.run_scoped(activations, *[pltpu.VMEM(s, t) for s, t in zip(wide, types)])
    narrow = [(2 * NEAR, NBIG), (2, 2, GROUP, *TALL, TILE), (2, TILE, 2 * FFN), (2, TILE, HEAD), (2, OUT, TILE), (KV, DIM), (2, TILE, HEAD)]
    totals = [(KV, DIM), (KV, half), (2, KV, EIGHTH), (2, KV, W), (KV, 2 * W), (3, KROWS, 2 * W), (BLOCK, DIM), (4, 1, DIM), (3, 1, DIM), (4, 1, DIM)]
    buffers = [pltpu.VMEM(s, BF16) for s in narrow] + [pltpu.VMEM(s, F32) for s in totals]
    pl.run_scoped(gradients, *buffers)


def layer_call(*args):
    any_spec = pl.BlockSpec(memory_space=pl.ANY)
    vmem_spec = pl.BlockSpec(memory_space=pltpu.VMEM)
    dma = pltpu.SemaphoreType.DMA
    tall = (*TALL, DIM)
    kept = [(GROUP, 2, *tall)] * 2 + [(ITEMS, *tall), (NEAR, NCAT), (NEAR, NZO), (NEAR, OWN), (NEAR, OUT)]
    shapes = kept + [(ITEMS * ROWS, DIM)] * 2 + [(1, DIM), (DIM, FFN), (DIM, FFN), (DIM, HEAD), (FFN, DIM), (HEAD, DIM), (DIM, HEAD), (DIM, HEAD)]
    types = [BF16] * len(shapes)
    types[len(kept) + 2] = F32
    pairs = [(ITEMS, COPIES), (2,), (5,), (GROUP, 2), (GROUP, 3), (8, 6)]
    results = pl.pallas_call(
        layer_kernel,
        out_shape=[jax.ShapeDtypeStruct(s, t) for s, t in zip(shapes, types)],
        in_specs=[any_spec] * (len(args) - 3) + [vmem_spec] * 3,
        out_specs=[any_spec] * len(shapes),
        scratch_shapes=[
            *[dma(s) for s in pairs for _ in PAIR],
            *[dma(s) for s in ((6,), (7,), (2,), (2,), (2, 2), (2, 3), (2, 2), (6,), (6,))],
            pltpu.SemaphoreType.REGULAR,
            pltpu.VMEM((2, 2, GROUP, ROWS, DIM), BF16),
            *scatter_scratch(),
        ],
        compiler_params=pltpu.CompilerParams(collective_id=0, has_side_effects=True, vmem_limit_bytes=VMEM_BYTES),
        name="layer",
    )(*args)
    return results[len(kept) :]


def rope_tables():
    inv_freq = ROPE_BASE ** (-jnp.arange(HEAD // 2, dtype=F32) * 2.0 / HEAD)
    pos = row_position(jnp.arange(SEQ, dtype=jnp.int32)).astype(F32)
    angles = pos[:, None] * inv_freq[None, :]
    cos, sin = jnp.cos(angles), jnp.sin(angles)
    return jnp.concatenate([cos, cos], axis=1), jnp.concatenate([-sin, sin], axis=1)


def solution(mesh):
    def layer_shard(x_loc, dy_loc, ln_gain, w_query, w_key, w_value, w_out, w_gate, w_up, w_down):
        def mean(v):
            return jnp.mean(v, axis=-1, keepdims=True)

        residual = x_loc.astype(F32)
        centered = residual - mean(residual)
        h_loc = (ln_gain * (centered * lax.rsqrt(mean(centered * centered) + LN_EPS))).astype(BF16)
        wq = w_query.reshape(DIM, HEAD)
        wo = w_out.reshape(HEAD, DIM)
        weights = (w_gate, w_up, wq, w_key, w_value, w_down, wo)
        flat = (ITEMS * ROWS, DIM)
        y_loc, grad_x, dgain, dw1, dw3, dwq, dw2, dwo, dwk, dwv = layer_call(
            h_loc, dy_loc, x_loc.reshape(flat), dy_loc.reshape(flat), *weights, ln_gain.reshape(1, DIM), *rope_tables()
        )
        y_loc, grad_x = (v.reshape(x_loc.shape) for v in (y_loc, grad_x))
        return y_loc, grad_x, dgain.reshape(DIM), dwq.reshape(DIM, 1, HEAD), dwk, dwv, dwo.reshape(1, HEAD, DIM), dw1, dw3, dw2

    act = P(None, "tp", None)
    head, columns, lead, every = P(None, "tp", None), P(None, "tp"), P("tp"), P()
    specs = (act, act, every, head, every, every, lead, columns, columns, lead)
    return jax.shard_map(layer_shard, mesh=mesh, in_specs=specs, out_specs=specs, check_vma=False)
```

time: 617 us -> 568 us (0.921)
  Pallas kernels: 586 us -> 541 us
    pallas_call x3 -> x1, Pallas kernels: 586 us -> 541 us  [layer_call(): pl.pallas_call(layer_kernel, out_shape=[jax.ShapeDtypeStruct(s, t) for s,...]
    unnamed x39 -> x26, local copies, waits for them, and re-layouts: 17.1 us -> 18.7 us
where the time goes in v3:
time: 568 us
  Pallas kernels  541 us (95%)
  local copies, waits for them, and re-layouts  18.7 us (3%)
  other arithmetic  7.11 us (1%)
    pallas_call x1, Pallas kernels, layer_call(): pl.pallas_call(layer_kernel, out_shape=[jax.ShapeDtypeStruct(s, t) for s,...  541 us
    unnamed x26, local copies, waits for them, and re-layouts  18.7 us

profile of v3, /device:TPU:0, one launch (start us, length us, event | category | flops | bytes accessed | tf_op | source)
XLA Modules:
  0.0 567.7 jit_solution(1201851754012313209)
XLA Ops:
  0.7 1.5 convert_reduce_fusion
  2.1 1.7 fusion.2
  3.8 0.5 fusion.5
  4.3 0.8 pad_maximum_fusion
  5.2 2.6 fusion.4.h_loc
  7.8 541.2 %layer.1 = (bf16[8,2,2,2,64,4096]{5,4,3,2,1,0:T(8,128)(2,1)}, bf16[8,2,2,2,64,4096]{5,4,3,2,1,0:T(8,128)(2,1)}, bf16[16,2,2,64,4096]{4,3,2,1,0:T(8,128)(2,1)}, b...) custom-call(bf16[16,8,4096]{2,1,0:T(8,128)(2,1)} %fusion.4.h_loc, ...), custom_call_target="tpu_custom_call" | custom-call | tf_op jit(solution)/shard_map/layer/pallas_call | solution.py:913
  549.0 0.0 copy-start.7
  549.0 0.0 copy-start.6
  549.0 0.0 copy-start.5
  549.0 0.0 copy-start.4
  549.0 2.4 copy.30
  551.4 0.0 copy-start.3
  551.4 2.4 copy.31
  553.8 0.0 copy-done.7
  553.8 0.6 copy.32
  554.4 0.0 copy-done.6
  554.4 0.0 copy-start.2
  554.4 1.0 copy.33
  555.4 0.0 copy-done.5
  555.4 1.0 copy.34
  556.4 0.0 copy-done.4
  556.4 1.0 copy.35
  557.4 0.0 copy-done.3
  557.4 1.0 copy.36
  558.3 0.0 copy-done.2
  558.3 0.0 copy-start.1
  558.3 2.1 copy.37
  560.5 1.6 copy-done.1
  562.0 0.0 copy-start
  562.0 2.1 copy.38
  564.2 1.6 copy-done
  565.7 2.0 copy.39
  (4 shorter events, 0.0 us)
Async XLA Ops:
  549.0 4.9 copy-start.7
  549.0 5.5 copy-start.6
  549.0 6.4 %copy-start.5 = (bf16[4096,128]{1,0:T(8,128)(2,1)S(1)}, bf16[4096,128]{1,0:T(8,128)(2,1)}, u32[]{:S(2)}) copy-start(bf16[4096,128]{1,0:T(8,128)(2,1)} %get-tuple-element.49) | copy-start | bytes 3145732
  549.0 7.4 %copy-start.4 = (bf16[4096,128]{1,0:T(8,128)(2,1)S(1)}, bf16[4096,128]{1,0:T(8,128)(2,1)}, u32[]{:S(2)}) copy-start(bf16[4096,128]{1,0:T(8,128)(2,1)} %get-tuple-element.50) | copy-start | bytes 3145732
  551.4 5.9 %copy-start.3 = (bf16[128,4096]{1,0:T(8,128)(2,1)S(1)}, bf16[128,4096]{1,0:T(8,128)(2,1)}, u32[]{:S(2)}) copy-start(bf16[128,4096]{1,0:T(8,128)(2,1)} %get-tuple-element.26) | copy-start | bytes 3145732
  554.4 3.9 copy-start.2
  558.3 3.7 copy-start.1
  562.0 3.7 copy-start

commit v4 on v3

--- a/solution.py
+++ b/solution.py
@@ -36,7 +36,6 @@
 OCOL = (2 * FFN, 2 * FFN + HEAD)
 NEAR = GROUP * SEQ
 
-SLOW = 3
 DEPTH = 5
 COPIES = 14
 
@@ -469,8 +468,8 @@
 
 
 def layer_kernel(
-    h_loc, dy_tok, x_loc, dy_loc, w1, w3, wq, wk, wv, w2, wo, gain, cos_t, sin_t,
-    full, full_sib, parts, g_all, zo_all, g_sib, zo_sib, y_out, dx_out, dgain, dw1, dw3, dwq, dw2, dwo, dwk, dwv,
+    h_loc, dy_loc, x_loc, w1, w3, wq, wk, wv, w2, wo, cos_t, sin_t,
+    full, full_sib, parts, g_all, zo_all, g_sib, zo_sib, sums_out, dgain, dw1, dw3, dwq, dw2, dwo, dwk, dwv,
     gsend, grecv, sx, rx, sw, rw, ss, rs, sg, rg, ksend, krecv, lsem, wsem, osem, gsem,
     tsem, o1sem, o2sem, hsend, hrecv, ready, sums, *scatter_refs,
 ):
@@ -489,7 +488,7 @@
 
     def activations(wcat, w2o, hv, dyv, proj, zo, g, yo, dho, probs, qs, stage):
         mine = rows8(BLOCK * z + ROWS * core, ROWS)
-        locs = (h_loc, dy_tok)
+        locs = (h_loc, dy_loc)
         to = [full.at[:, s, y, x, mine, :] for s in PAIR]
         swaps = [remote(locs[s].at[rows8(GROUP * (1 - core), GROUP)], to[s], (sx.at[s], rx.at[s]), sib) for s in PAIR]
         takes = [pltpu.make_async_copy(locs[s].at[rows8(GROUP * core, GROUP)], stage.at[s], lsem.at[s]) for s in PAIR]
@@ -569,9 +568,6 @@
 
         def batch_step(b):
             ahead = 2 * b + DEPTH + 1
-            behind = b - 1 + lax.max(b - SLOW, 0)
-            pl.when(b > 0)(lambda: out(b - 1, 0).wait())
-            scatter.tick(behind)
             load(b, 0).wait()
 
             def proj_tile(t):
@@ -579,6 +575,7 @@
 
             loop(NCAT // FFN, proj_tile)
             pl.when(b > 0)(lambda: drained(b - 1))
+            scatter.tick(2 * b - 1)
 
             def hidden_tile(t):
                 gate_at, up_at = gate_up(t)
@@ -619,7 +616,8 @@
                 g[:, up_at] = (dz * (gate * sig)).astype(BF16)
 
             loop(2 * FFN // W, dz_tile)
-            pl.when(b >= SLOW)(lambda: scatter.tick(behind + 1))
+            out(b, 0).wait()
+            scatter.tick(2 * b)
             d_heads = dot_nt(flat(dyv), w2o[2 * FFN : NZO, :]).astype(BF16)
             d_keys = d_vals = jnp.zeros((SEQ, HEAD), F32)
             for hd in PAIR:
@@ -644,7 +642,6 @@
             start(gz_local(b) + gz_copies(b))
 
         loop(GROUP, batch_step)
-        out(GROUP - 1, 0).wait()
         drained(GROUP - 1)
 
         def finish(b):
@@ -657,7 +654,9 @@
         wait_send(swaps + far)
 
 
-    def gradients(big, tiles, out1, outq, out2, kvo, kvt, kvp, k1, k2, k3, kc, k4, gacc, gpart, ggot, gz):
+    def gradients(big, tiles, out1, outq, out2, kvo, kvt, xb, kvp, k1, k2, k3, kc, k4, gacc, gpart, ggot, gz):
+        x_in = pltpu.make_async_copy(x_loc, xb, gsem.at[0])
+        x_in.start()
         near, away = slice(0, NEAR), slice(NEAR, 2 * NEAR)
         views = (
             (g_all.at[:, KEY:NCAT], big.at[near, KCOL:NBIG]),
@@ -762,7 +761,7 @@
 
         meet(partners)
         start(hops[0])
-        ticks = 2 * GROUP - 1 - SLOW
+        ticks = 2 * GROUP - 1
         scatter.tick(ticks)
         wait(loads[1:])
 
@@ -784,67 +783,42 @@
                 pltpu.make_async_copy(out2.at[slot, FFN:OUT], dwo.at[:, cols], sem.at[1]),
             ]
 
-        def mean(v):
-            return jnp.mean(v, axis=-1, keepdims=True)
-
-        def token_step(i):
+        def gain_step(i):
             first = i * 2
-            spans = [rows16(k * ITEMS * ROWS + i * BLOCK, BLOCK) for k in range(4)]
-
-            def total(s):
-                return sums[s, lax.div(first, GROUP), pl.ds(lax.rem(first, GROUP), 2)].astype(F32).reshape(BLOCK, DIM)
-
-            def both(k):
-                return jnp.concatenate([big[spans[k], :], big[spans[k + 1], :]], axis=1).astype(F32)
-
-            def keep(k, value):
-                big[spans[k], :] = value[:, 0:NBIG].astype(BF16)
-                big[spans[k + 1], :] = value[:, NBIG:DIM].astype(BF16)
-
-            res = both(0)
-            d_norm = total(1)
-            centered = res - mean(res)
-            inv_std = lax.rsqrt(mean(centered * centered) + LN_EPS)
-            x_hat = centered * inv_std
-            gacc[...] = gacc[...] + d_norm * x_hat
-            d_hat = d_norm * gain[...]
-            dx = inv_std * (d_hat - mean(d_hat) - x_hat * mean(d_hat * x_hat)) + both(2)
-            keep(0, res + total(0))
-            keep(2, dx)
-
-        def tokens_of(arrays, inward):
-            copies = []
-            for k in range(4):
-                here = big.at[k * ITEMS * ROWS : (k + 1) * ITEMS * ROWS]
-                there = arrays[k // 2].at[:, k % 2 * NBIG : (k % 2 + 1) * NBIG]
-                src, dst = (there, here) if inward else (here, there)
-                copies.append(pltpu.make_async_copy(src, dst, lsem.at[k]))
-            return copies
-
-        tokens_in, results = tokens_of((x_loc, dy_loc), True), tokens_of((y_out, dx_out), False)
-        gain_out = pltpu.make_async_copy(gpart.at[0], dgain, osem.at[0])
-
-        def finalize():
-            start(tokens_in)
+            two = pl.ds(lax.rem(first, GROUP), 2)
+            x_hat, _ = normalize(xb[pl.ds(first, 2)].astype(F32).reshape(BLOCK, DIM))
+            gacc[...] = gacc[...] + sums[1, lax.div(first, GROUP), two].astype(F32).reshape(BLOCK, DIM) * x_hat
+
+        near = partners[: len(partners) - len(zn)]
+        gain_hops = [remote(gpart.at[k], ggot.at[k], (hsend.at[k], hrecv.at[k]), there) for k, there in enumerate(near)]
+        last = len(near)
+        gain_last = [remote(gpart.at[last], gz.at[z], (hsend.at[last + k], hrecv.at[last + k]), there) for k, there in enumerate(zn)]
+        results = pltpu.make_async_copy(sums, sums_out, osem.at[0])
+        gain_out = pltpu.make_async_copy(gpart.at[0], dgain, osem.at[1])
+
+        def gain_start():
+            x_in.wait()
             gacc[...] = jnp.zeros_like(gacc)
-            wait(tokens_in)
-            loop(GROUP, token_step)
-            start(results)
+            loop(GROUP, gain_step)
             gpart[0] = jnp.sum(gacc[...], axis=0, keepdims=True)
-            near = partners[:3]
-            for k, there in enumerate(near):
-                step = remote(gpart.at[k], ggot.at[k], (hsend.at[k], hrecv.at[k]), there)
-                step.start()
-                step.wait_recv()
-                gpart[k + 1] = gpart[k] + ggot[k]
-                step.wait_send()
-            steps = [remote(gpart.at[3], gz.at[z], (hsend.at[3 + k], hrecv.at[3 + k]), there) for k, there in enumerate(zn)]
-            start(steps)
-            gz[z] = gpart[3]
-            wait(steps)
+            gain_hops[0].start()
+
+        def gain_hop(k):
+            gain_hops[k].wait_recv()
+            gpart[k + 1] = gpart[k] + ggot[k]
+            start(gain_hops[k + 1 : k + 2] or gain_last)
+
+        def gain_finish():
+            results.start()
+            for k in range(len(near)):
+                gain_hop(k)
+            gz[z] = gpart[last]
+            wait(gain_last)
+            wait_send(gain_hops)
             gpart[0] = gz[0] + gz[1] + gz[2] + gz[3]
             gain_out.start()
             gain_out.wait()
+            results.wait()
 
         def tokens(u):
             return tiles[lax.rem(u, 2)].reshape(2 * NEAR, TILE)
@@ -869,22 +843,27 @@
             out2[slot, FFN:OUT] = dot_tn(big[:, OWN + FFN : KCOL], tokens(u)).astype(BF16)
             start(out2_copies(u))
 
-        def pairs(first, grad):
-            def body(j):
-                scatter.tick(ticks + 1 + first + j)
-                grad(2 * j)
-                kv_step(first + j)
-                grad(2 * j + 1)
-
-            loop(STEPS // 2, body)
-
-        pairs(0, grad_in)
-        pairs(STEPS // 2, grad_out)
+        def first_half(j):
+            grad_in(2 * j)
+            pl.when(lax.rem(j, 2) == 1)(lambda: scatter.tick(ticks + 1 + lax.div(j, 2)))
+            grad_in(2 * j + 1)
+            kv_step(j)
+
+        def second_half(j):
+            grad_out(2 * j)
+            scatter.tick(ticks + 3 + j)
+            grad_out(2 * j + 1)
+            kv_step(STEPS // 2 + j)
+
+        loop(STEPS // 2, first_half)
+        loop(STEPS // 2 - 1, second_half)
         scatter.finish()
-        finalize()
+        gain_start()
+        loop((STEPS - 2, STEPS), grad_out)
+        kv_step(STEPS - 1)
+        gain_finish()
         for u in (STEPS - 2, STEPS - 1):
             wait(out_copies(u) + out2_copies(u))
-        wait(results)
         for group in hops.values():
             wait_send(group)
 
@@ -894,7 +873,7 @@
     wide = [(DIM, NCAT), (NZO, DIM), tall, tall, (SEQ, NCAT), (SEQ, NZO), (SEQ, NCAT), tall, tall, (2, SEQ, SEQ), (4, SEQ, HEAD), (2, GROUP, ROWS, DIM)]
     types = [BF16] * 4 + [F32] + [BF16] * 4 + [F32] + [BF16] * 2
     pl.run_scoped(activations, *[pltpu.VMEM(s, t) for s, t in zip(wide, types)])
-    narrow = [(2 * NEAR, NBIG), (2, 2, GROUP, *TALL, TILE), (2, TILE, 2 * FFN), (2, TILE, HEAD), (2, OUT, TILE), (KV, DIM), (2, TILE, HEAD)]
+    narrow = [(2 * NEAR, NBIG), (2, 2, GROUP, *TALL, TILE), (2, TILE, 2 * FFN), (2, TILE, HEAD), (2, OUT, TILE), (KV, DIM), (2, TILE, HEAD), (ITEMS, ROWS, DIM)]
     totals = [(KV, DIM), (KV, half), (2, KV, EIGHTH), (2, KV, W), (KV, 2 * W), (3, KROWS, 2 * W), (BLOCK, DIM), (4, 1, DIM), (3, 1, DIM), (4, 1, DIM)]
     buffers = [pltpu.VMEM(s, BF16) for s in narrow] + [pltpu.VMEM(s, F32) for s in totals]
     pl.run_scoped(gradients, *buffers)
@@ -906,14 +885,14 @@
     dma = pltpu.SemaphoreType.DMA
     tall = (*TALL, DIM)
     kept = [(GROUP, 2, *tall)] * 2 + [(ITEMS, *tall), (NEAR, NCAT), (NEAR, NZO), (NEAR, OWN), (NEAR, OUT)]
-    shapes = kept + [(ITEMS * ROWS, DIM)] * 2 + [(1, DIM), (DIM, FFN), (DIM, FFN), (DIM, HEAD), (FFN, DIM), (HEAD, DIM), (DIM, HEAD), (DIM, HEAD)]
+    shapes = kept + [(2, 2, GROUP, ROWS, DIM), (1, DIM), (DIM, FFN), (DIM, FFN), (DIM, HEAD), (FFN, DIM), (HEAD, DIM), (DIM, HEAD), (DIM, HEAD)]
     types = [BF16] * len(shapes)
-    types[len(kept) + 2] = F32
+    types[len(kept) + 1] = F32
     pairs = [(ITEMS, COPIES), (2,), (5,), (GROUP, 2), (GROUP, 3), (8, 6)]
     results = pl.pallas_call(
         layer_kernel,
         out_shape=[jax.ShapeDtypeStruct(s, t) for s, t in zip(shapes, types)],
-        in_specs=[any_spec] * (len(args) - 3) + [vmem_spec] * 3,
+        in_specs=[any_spec] * (len(args) - 2) + [vmem_spec] * 2,
         out_specs=[any_spec] * len(shapes),
         scratch_shapes=[
             *[dma(s) for s in pairs for _ in PAIR],
@@ -928,6 +907,65 @@
     return results[len(kept) :]
 
 
+def normalize(x):
+    centered = x - mean(x)
+    inv_std = lax.rsqrt(mean(centered * centered) + LN_EPS)
+    return centered * inv_std, inv_std
+
+
+def mean(v):
+    return jnp.mean(v, axis=-1, keepdims=True)
+
+
+def finish_kernel(sums, x_loc, dy_loc, gain, *refs):
+    *refs, sv, xv, dyv, sem = refs
+    count = len(refs) // 3
+    sources, (y_out, dx_out, *refs) = refs[:count], refs[count:]
+    places, buffers = refs[:count], refs[count:]
+    loads = [pltpu.make_async_copy(src, dst, sem.at[k]) for k, (src, dst) in enumerate(zip((sums, x_loc, dy_loc, *sources), (sv, xv, dyv, *buffers)))]
+    stores = [pltpu.make_async_copy(src, dst, sem.at[k]) for k, (src, dst) in enumerate(zip((xv, dyv), (y_out, dx_out)))]
+    moved = [pltpu.make_async_copy(src, dst, sem.at[3 + k]) for k, (src, dst) in enumerate(zip(buffers, places))]
+    start(loads)
+    wait(loads[:3])
+
+    def step(i):
+        rows = rows16(i * BLOCK, BLOCK)
+        res = xv[rows, :].astype(F32)
+        x_hat, inv_std = normalize(res)
+        d_hat = sv[1, rows, :].astype(F32) * gain[...]
+        dx = inv_std * (d_hat - mean(d_hat) - x_hat * mean(d_hat * x_hat)) + dyv[rows, :].astype(F32)
+        xv[rows, :] = (res + sv[0, rows, :].astype(F32)).astype(BF16)
+        dyv[rows, :] = dx.astype(BF16)
+
+    for k, c in enumerate(moved):
+        loop((k, k + 1), step)
+        loads[3 + k].wait()
+        c.start()
+    loop((len(moved), GROUP), step)
+    start(stores)
+    wait(stores + moved)
+
+
+def finish_call(sums, x, dy, gain, *grads):
+    any_spec = pl.BlockSpec(memory_space=pl.ANY)
+    shapes = [x.shape] * 2 + [v.shape for v in grads]
+    types = [BF16] * 2 + [v.dtype for v in grads]
+    tokens = [sums.shape, x.shape, x.shape]
+    return pl.pallas_call(
+        finish_kernel,
+        out_shape=[jax.ShapeDtypeStruct(s, t) for s, t in zip(shapes, types)],
+        in_specs=[any_spec] * 3 + [pl.BlockSpec(memory_space=pltpu.VMEM)] + [any_spec] * len(grads),
+        out_specs=[any_spec] * len(shapes),
+        scratch_shapes=[
+            *[pltpu.VMEM(v.shape, v.dtype) for v in grads],
+            *[pltpu.VMEM(s, BF16) for s in tokens],
+            pltpu.SemaphoreType.DMA((3 + len(grads),)),
+        ],
+        compiler_params=pltpu.CompilerParams(vmem_limit_bytes=VMEM_BYTES),
+        name="finish",
+    )(sums, x, dy, gain, *grads)
+
+
 def rope_tables():
     inv_freq = ROPE_BASE ** (-jnp.arange(HEAD // 2, dtype=F32) * 2.0 / HEAD)
     pos = row_position(jnp.arange(SEQ, dtype=jnp.int32)).astype(F32)
@@ -938,18 +976,12 @@
 
 def solution(mesh):
     def layer_shard(x_loc, dy_loc, ln_gain, w_query, w_key, w_value, w_out, w_gate, w_up, w_down):
-        def mean(v):
-            return jnp.mean(v, axis=-1, keepdims=True)
-
-        residual = x_loc.astype(F32)
-        centered = residual - mean(residual)
-        h_loc = (ln_gain * (centered * lax.rsqrt(mean(centered * centered) + LN_EPS))).astype(BF16)
-        wq = w_query.reshape(DIM, HEAD)
-        wo = w_out.reshape(HEAD, DIM)
-        weights = (w_gate, w_up, wq, w_key, w_value, w_down, wo)
+        h_loc = (ln_gain * normalize(x_loc.astype(F32))[0]).astype(BF16)
+        weights = (w_gate, w_up, w_query.reshape(DIM, HEAD), w_key, w_value, w_down, w_out.reshape(HEAD, DIM))
+        sums, *grads = layer_call(h_loc, dy_loc, x_loc, *weights, *rope_tables())
         flat = (ITEMS * ROWS, DIM)
-        y_loc, grad_x, dgain, dw1, dw3, dwq, dw2, dwo, dwk, dwv = layer_call(
-            h_loc, dy_loc, x_loc.reshape(flat), dy_loc.reshape(flat), *weights, ln_gain.reshape(1, DIM), *rope_tables()
+        y_loc, grad_x, dgain, dw1, dw3, dwq, dw2, dwo, dwk, dwv = finish_call(
+            sums.reshape(2, *flat), x_loc.reshape(flat), dy_loc.reshape(flat), ln_gain.reshape(1, DIM), *grads
         )
         y_loc, grad_x = (v.reshape(x_loc.shape) for v in (y_loc, grad_x))
         return y_loc, grad_x, dgain.reshape(DIM), dwq.reshape(DIM, 1, HEAD), dwk, dwv, dwo.reshape(1, HEAD, DIM), dw1, dw3, dw2

time: 568 us -> 553 us (0.974)
  local copies, waits for them, and re-layouts: 18.7 us -> 0 us
    unnamed x26 -> x0, local copies, waits for them, and re-layouts: 18.7 us -> none
    pallas_call x0 -> x1, Pallas kernels: none -> 13.9 us  [finish_call(): pl.pallas_call(finish_kernel, out_shape=[jax.ShapeDtypeStruct(s, t) for s...]
    pallas_call x1, Pallas kernels: 541 us -> 531 us  [layer_call(): pl.pallas_call(layer_kernel, out_shape=[jax.ShapeDtypeStruct(s, t) for s,...]
where the time goes in v4:
time: 553 us
  Pallas kernels  545 us (99%)
  other arithmetic  7.11 us (1%)
    pallas_call x1, Pallas kernels, layer_call(): pl.pallas_call(layer_kernel, out_shape=[jax.ShapeDtypeStruct(s, t) for s,...  531 us
    pallas_call x1, Pallas kernels, finish_call(): pl.pallas_call(finish_kernel, out_shape=[jax.ShapeDtypeStruct(s, t) for s...  13.9 us

profile of v4, /device:TPU:0, one launch (start us, length us, event | category | flops | bytes accessed | tf_op | source)
XLA Modules:
  0.0 552.8 jit_solution(5590173608719055526)
XLA Ops:
  0.7 1.5 convert_reduce_fusion
  2.1 1.7 fusion.2
  3.8 0.5 fusion.5
  4.3 0.8 pad_maximum_fusion
  5.2 2.6 fusion.4.h_loc
  7.8 531.0 %layer.1 = (bf16[8,2,2,2,64,4096]{5,4,3,2,1,0:T(8,128)(2,1)}, bf16[8,2,2,2,64,4096]{5,4,3,2,1,0:T(8,128)(2,1)}, bf16[16,2,2,64,4096]{4,3,2,1,0:T(8,128)(2,1)}, b...) custom-call(bf16[16,8,4096]{2,1,0:T(8,128)(2,1)} %fusion.4.h_loc, ...), custom_call_target="tpu_custom_call" | custom-call | tf_op jit(solution)/shard_map/layer/pallas_call | solution.py:892
  538.7 13.9 %finish.1 = (bf16[128,4096]{1,0:T(8,128)(2,1)}, bf16[128,4096]{1,0:T(8,128)(2,1)}, f32[1,4096]{1,0:T(1,128)}, bf16[4096,512]{1,0:T(8,128)(2,1)}, bf16[4096,512]{...) custom-call(bf16[2,128,4096]{2,1,0:T(8,128)(2,1)} %bitcast.13, ...), custom_call_target="tpu_custom_call" | custom-call | tf_op jit(solution)/shard_map/finish/pallas_call | solution.py:954
  (4 shorter events, 0.0 us)

commit v5 on v4

--- a/solution.py
+++ b/solution.py
@@ -1,5 +1,6 @@
 import jax
 import jax.numpy as jnp
+import numpy as np
 from jax import lax
 from jax.experimental import pallas as pl
 from jax.experimental.pallas import tpu as pltpu
@@ -8,6 +9,7 @@
 LN_EPS = 1e-6
 ROPE_BASE = 10000.0
 MESH = pl.DeviceIdType.MESH
+KEEP = dict(axis=-1, keepdims=True)
 F32 = jnp.float32
 BF16 = jnp.bfloat16
 ALL = slice(None)
@@ -117,11 +119,9 @@
     return [index(z, y, x, 1 - core), index(z, y, 1 - x, core), index(z, 1 - y, x, core)] + chips
 
 
-def entry_barrier(partners):
-    barrier = pltpu.get_barrier_semaphore()
-    for partner in partners:
-        pl.semaphore_signal(barrier, inc=1, device_id=(partner,), device_id_type=MESH)
-    pl.semaphore_wait(barrier, len(partners))
+def greet(semaphore, others):
+    for there in others:
+        pl.semaphore_signal(semaphore, inc=1, device_id=(there,), device_id_type=MESH)
 
 
 def dot_nt(a, b):
@@ -134,6 +134,16 @@
 
 def dot_nn(a, b):
     return jnp.dot(a, b, preferred_element_type=F32)
+
+
+def normalize(x):
+    centered = x - mean(x)
+    inv_std = lax.rsqrt(mean(centered * centered) + LN_EPS)
+    return centered * inv_std, inv_std
+
+
+def mean(v):
+    return jnp.mean(v, **KEEP)
 
 
 def add_into(dst, src, width):
@@ -468,7 +478,7 @@
 
 
 def layer_kernel(
-    h_loc, dy_loc, x_loc, w1, w3, wq, wk, wv, w2, wo, cos_t, sin_t,
+    x_loc, dy_loc, gain, w1, w3, wq, wk, wv, w2, wo, cos_t, sin_t,
     full, full_sib, parts, g_all, zo_all, g_sib, zo_sib, sums_out, dgain, dw1, dw3, dwq, dw2, dwo, dwk, dwv,
     gsend, grecv, sx, rx, sw, rw, ss, rs, sg, rg, ksend, krecv, lsem, wsem, osem, gsem,
     tsem, o1sem, o2sem, hsend, hrecv, ready, sums, *scatter_refs,
@@ -477,26 +487,35 @@
     z, y, x, core = spot
     partners = partners_of(*spot)
     sib, xn, yn, *zn = partners
-    entry_barrier(partners)
+    barrier = pltpu.get_barrier_semaphore()
+    greet(barrier, partners)
     gather = Gather(spot, full, gsend, grecv)
     scatter = Scatter(spot, parts, sums, scatter_refs)
 
     def meet(others):
-        for there in others:
-            pl.semaphore_signal(ready, inc=1, device_id=(there,), device_id_type=MESH)
+        greet(ready, others)
         pl.semaphore_wait(ready, len(others))
 
-    def activations(wcat, w2o, hv, dyv, proj, zo, g, yo, dho, probs, qs, stage):
+    def activations(wcat, w2o, hv, dyv, proj, zo, g, yo, dho, probs, qs, stage, dy_own):
+        own, far_half = (rows8(GROUP * c, GROUP) for c in (core, 1 - core))
+        takes = [pltpu.make_async_copy(x_loc, stage, lsem.at[0]), pltpu.make_async_copy(dy_loc.at[own], dy_own, lsem.at[1])]
+        start(takes)
+        wait(takes)
+
+        def norm_step(i):
+            two = pl.ds(i * 2, 2)
+            x_hat, _ = normalize(stage[two].astype(F32).reshape(BLOCK, DIM))
+            stage[two] = (gain[...] * x_hat).astype(BF16).reshape(2, ROWS, DIM)
+
+        loop(GROUP, norm_step)
+        pl.semaphore_wait(barrier, len(partners))
+
         mine = rows8(BLOCK * z + ROWS * core, ROWS)
-        locs = (h_loc, dy_loc)
         to = [full.at[:, s, y, x, mine, :] for s in PAIR]
-        swaps = [remote(locs[s].at[rows8(GROUP * (1 - core), GROUP)], to[s], (sx.at[s], rx.at[s]), sib) for s in PAIR]
-        takes = [pltpu.make_async_copy(locs[s].at[rows8(GROUP * core, GROUP)], stage.at[s], lsem.at[s]) for s in PAIR]
-        puts = [pltpu.make_async_copy(stage.at[s], to[s], lsem.at[s]) for s in PAIR]
-        start(swaps + takes)
-        for s in PAIR:
-            takes[s].wait()
-            puts[s].start()
+        away = (stage.at[far_half], dy_loc.at[far_half])
+        swaps = [remote(away[s], to[s], (sx.at[s], rx.at[s]), sib) for s in PAIR]
+        puts = [pltpu.make_async_copy(src, dst, lsem.at[s]) for s, (src, dst) in enumerate(zip((stage.at[own], dy_own), to))]
+        start(swaps + puts)
         wait(puts)
         wait_recv(swaps)
         loop(2, gather.tick)
@@ -592,8 +611,8 @@
                 query = rotate(proj[:, QCOL[hd] : QCOL[hd] + HEAD]).astype(BF16)
                 qs[hd] = query
                 scores = jnp.where(causal, dot_nt(query, keys) * scale, -1e30)
-                e = jnp.exp(scores - jnp.max(scores, axis=-1, keepdims=True))
-                p = e / jnp.sum(e, axis=-1, keepdims=True)
+                e = jnp.exp(scores - jnp.max(scores, **KEEP))
+                p = e / jnp.sum(e, **KEEP)
                 probs[hd] = p
                 zo[:, OCOL[hd] : OCOL[hd] + HEAD] = dot_nn(p.astype(BF16), vals).astype(BF16)
 
@@ -625,7 +644,7 @@
                 p = probs[hd]
                 d_probs = dot_nt(d_out, qs[3])
                 d_vals = d_vals + dot_tn(p.astype(BF16), d_out)
-                row_dot = jnp.sum(p * d_probs, axis=-1, keepdims=True)
+                row_dot = jnp.sum(p * d_probs, **KEEP)
                 d_scores = (p * (d_probs - row_dot) * scale).astype(BF16)
                 g[:, QCOL[hd] : QCOL[hd] + HEAD] = rotate(dot_nn(d_scores, qs[2]), True).astype(BF16)
                 d_keys = d_keys + dot_tn(d_scores, qs[hd])
@@ -761,7 +780,7 @@
 
         meet(partners)
         start(hops[0])
-        ticks = 2 * GROUP - 1
+        ticks = ITEMS - 1
         scatter.tick(ticks)
         wait(loads[1:])
 
@@ -810,7 +829,7 @@
 
         def gain_finish():
             results.start()
-            for k in range(len(near)):
+            for k in range(1, len(near)):
                 gain_hop(k)
             gz[z] = gpart[last]
             wait(gain_last)
@@ -859,7 +878,9 @@
         loop(STEPS // 2 - 1, second_half)
         scatter.finish()
         gain_start()
-        loop((STEPS - 2, STEPS), grad_out)
+        loop((STEPS - 2, STEPS - 1), grad_out)
+        gain_hop(0)
+        loop((STEPS - 1, STEPS), grad_out)
         kv_step(STEPS - 1)
         gain_finish()
         for u in (STEPS - 2, STEPS - 1):
@@ -870,8 +891,9 @@
 
     tall = (*TALL, DIM)
     half = DIM // 2
-    wide = [(DIM, NCAT), (NZO, DIM), tall, tall, (SEQ, NCAT), (SEQ, NZO), (SEQ, NCAT), tall, tall, (2, SEQ, SEQ), (4, SEQ, HEAD), (2, GROUP, ROWS, DIM)]
-    types = [BF16] * 4 + [F32] + [BF16] * 4 + [F32] + [BF16] * 2
+    wide = [(DIM, NCAT), (NZO, DIM), tall, tall, (SEQ, NCAT), (SEQ, NZO), (SEQ, NCAT), tall, tall, (2, SEQ, SEQ), (4, SEQ, HEAD)]
+    wide += [(ITEMS, ROWS, DIM), (GROUP, ROWS, DIM)]
+    types = [BF16] * 4 + [F32] + [BF16] * 4 + [F32] + [BF16] * 3
     pl.run_scoped(activations, *[pltpu.VMEM(s, t) for s, t in zip(wide, types)])
     narrow = [(2 * NEAR, NBIG), (2, 2, GROUP, *TALL, TILE), (2, TILE, 2 * FFN), (2, TILE, HEAD), (2, OUT, TILE), (KV, DIM), (2, TILE, HEAD), (ITEMS, ROWS, DIM)]
     totals = [(KV, DIM), (KV, half), (2, KV, EIGHTH), (2, KV, W), (KV, 2 * W), (3, KROWS, 2 * W), (BLOCK, DIM), (4, 1, DIM), (3, 1, DIM), (4, 1, DIM)]
@@ -892,7 +914,7 @@
     results = pl.pallas_call(
         layer_kernel,
         out_shape=[jax.ShapeDtypeStruct(s, t) for s, t in zip(shapes, types)],
-        in_specs=[any_spec] * (len(args) - 2) + [vmem_spec] * 2,
+        in_specs=[any_spec] * 2 + [vmem_spec] + [any_spec] * (len(args) - 5) + [vmem_spec] * 2,
         out_specs=[any_spec] * len(shapes),
         scratch_shapes=[
             *[dma(s) for s in pairs for _ in PAIR],
@@ -905,16 +927,6 @@
         name="layer",
     )(*args)
     return results[len(kept) :]
-
-
-def normalize(x):
-    centered = x - mean(x)
-    inv_std = lax.rsqrt(mean(centered * centered) + LN_EPS)
-    return centered * inv_std, inv_std
-
-
-def mean(v):
-    return jnp.mean(v, axis=-1, keepdims=True)
 
 
 def finish_kernel(sums, x_loc, dy_loc, gain, *refs):
@@ -967,26 +979,26 @@
 
 
 def rope_tables():
-    inv_freq = ROPE_BASE ** (-jnp.arange(HEAD // 2, dtype=F32) * 2.0 / HEAD)
-    pos = row_position(jnp.arange(SEQ, dtype=jnp.int32)).astype(F32)
-    angles = pos[:, None] * inv_freq[None, :]
-    cos, sin = jnp.cos(angles), jnp.sin(angles)
-    return jnp.concatenate([cos, cos], axis=1), jnp.concatenate([-sin, sin], axis=1)
+    inv_freq = np.float32(ROPE_BASE) ** (-np.arange(HEAD // 2, dtype=np.float32) * 2 / HEAD)
+    pos = row_position(np.arange(SEQ)).astype(np.float32)
+    angles = pos[:, None] * inv_freq.astype(np.float32)
+    cos, sin = np.cos(angles), np.sin(angles)
+    return np.concatenate([cos, cos], axis=1), np.concatenate([-sin, sin], axis=1)
 
 
 def solution(mesh):
     def layer_shard(x_loc, dy_loc, ln_gain, w_query, w_key, w_value, w_out, w_gate, w_up, w_down):
-        h_loc = (ln_gain * normalize(x_loc.astype(F32))[0]).astype(BF16)
+        gain = ln_gain.reshape(1, DIM)
         weights = (w_gate, w_up, w_query.reshape(DIM, HEAD), w_key, w_value, w_down, w_out.reshape(HEAD, DIM))
-        sums, *grads = layer_call(h_loc, dy_loc, x_loc, *weights, *rope_tables())
+        sums, *grads = layer_call(x_loc, dy_loc, gain, *weights, *rope_tables())
         flat = (ITEMS * ROWS, DIM)
         y_loc, grad_x, dgain, dw1, dw3, dwq, dw2, dwo, dwk, dwv = finish_call(
-            sums.reshape(2, *flat), x_loc.reshape(flat), dy_loc.reshape(flat), ln_gain.reshape(1, DIM), *grads
+            sums.reshape(2, *flat), x_loc.reshape(flat), dy_loc.reshape(flat), gain, *grads
         )
         y_loc, grad_x = (v.reshape(x_loc.shape) for v in (y_loc, grad_x))
         return y_loc, grad_x, dgain.reshape(DIM), dwq.reshape(DIM, 1, HEAD), dwk, dwv, dwo.reshape(1, HEAD, DIM), dw1, dw3, dw2
 
     act = P(None, "tp", None)
-    head, columns, lead, every = P(None, "tp", None), P(None, "tp"), P("tp"), P()
-    specs = (act, act, every, head, every, every, lead, columns, columns, lead)
+    columns, lead, every = P(None, "tp"), P("tp"), P()
+    specs = (act, act, every, act, every, every, lead, columns, columns, lead)
     return jax.shard_map(layer_shard, mesh=mesh, in_specs=specs, out_specs=specs, check_vma=False)

time: 553 us -> 547 us (0.989)
  other arithmetic: 7.11 us -> 0 us
where the time goes in v5:
time: 547 us
  Pallas kernels  546 us (100%)
    pallas_call x1, Pallas kernels, layer_call(): pl.pallas_call(layer_kernel, out_shape=[jax.ShapeDtypeStruct(s, t) for s,...  532 us
    pallas_call x1, Pallas kernels, finish_call(): pl.pallas_call(finish_kernel, out_shape=[jax.ShapeDtypeStruct(s, t) for s...  13.9 us

profile of v5, /device:TPU:0, one launch (start us, length us, event | category | flops | bytes accessed | tf_op | source)
XLA Modules:
  0.0 546.5 jit_solution(3235626398236871103)
XLA Ops:
  0.6 531.8 %layer.1 = (bf16[8,2,2,2,64,4096]{5,4,3,2,1,0:T(8,128)(2,1)}, bf16[8,2,2,2,64,4096]{5,4,3,2,1,0:T(8,128)(2,1)}, bf16[16,2,2,64,4096]{4,3,2,1,0:T(8,128)(2,1)}, b...) custom-call(bf16[16,8,4096]{2,1,0:T(8,128)(2,1)} %x_loc.1, ...), custom_call_target="tpu_custom_call" | custom-call | tf_op jit(solution)/shard_map/layer/pallas_call | solution.py:914
  532.4 13.9 %finish.1 = (bf16[128,4096]{1,0:T(8,128)(2,1)}, bf16[128,4096]{1,0:T(8,128)(2,1)}, f32[1,4096]{1,0:T(1,128)}, bf16[4096,512]{1,0:T(8,128)(2,1)}, bf16[4096,512]{...) custom-call(bf16[2,128,4096]{2,1,0:T(8,128)(2,1)} %bitcast.13, ...), custom_call_target="tpu_custom_call" | custom-call | tf_op jit(solution)/shard_map/finish/pallas_call | solution.py:966

commit v6 on v5

--- a/solution.py
+++ b/solution.py
@@ -481,7 +481,7 @@
     x_loc, dy_loc, gain, w1, w3, wq, wk, wv, w2, wo, cos_t, sin_t,
     full, full_sib, parts, g_all, zo_all, g_sib, zo_sib, sums_out, dgain, dw1, dw3, dwq, dw2, dwo, dwk, dwv,
     gsend, grecv, sx, rx, sw, rw, ss, rs, sg, rg, ksend, krecv, lsem, wsem, osem, gsem,
-    tsem, o1sem, o2sem, hsend, hrecv, ready, sums, *scatter_refs,
+    tsem, o1sem, o2sem, tosem, hsend, hrecv, ready, sums, *scatter_refs,
 ):
     spot = place()
     z, y, x, core = spot
@@ -673,7 +673,7 @@
         wait_send(swaps + far)
 
 
-    def gradients(big, tiles, out1, outq, out2, kvo, kvt, xb, kvp, k1, k2, k3, kc, k4, gacc, gpart, ggot, gz):
+    def gradients(big, tiles, out1, outq, out2, kvo, xb, kvp, k1, k2, k3, kc, k4, gacc, gpart, ggot, gz):
         x_in = pltpu.make_async_copy(x_loc, xb, gsem.at[0])
         x_in.start()
         near, away = slice(0, NEAR), slice(NEAR, 2 * NEAR)
@@ -756,13 +756,14 @@
             for c in PAIR:
                 kvo[mine, lanes(second[c], W)] = total[:, c * W : (c + 1) * W].astype(BF16)
 
+        def turned(t):
+            views = ((out1.at[s, :, lanes(t * HEAD, HEAD)], (dwk, dwv)[s].at[step_of(t, TILE)]) for s in PAIR)
+            return [pltpu.make_async_copy(src, dst, tosem.at[s, t]) for s, (src, dst) in enumerate(views)]
+
         def kv_turn(t):
-            rows = step_of(t, TILE)
             for s in PAIR:
-                kvt[s] = kvo[s * HEAD : (s + 1) * HEAD, rows].astype(F32).T.astype(BF16)
-            copies = [pltpu.make_async_copy(kvt.at[s], (dwk, dwv)[s].at[rows], osem.at[s]) for s in PAIR]
-            start(copies)
-            wait(copies)
+                out1[s, :, lanes(t * HEAD, HEAD)] = kvo[s * HEAD : (s + 1) * HEAD, step_of(t, TILE)].astype(F32).T.astype(BF16)
+            start(turned(t))
 
         works = (kv_first, kv_second, kv_third, kv_round)
 
@@ -775,6 +776,7 @@
                     if step < len(works):
                         works[step]()
                     elif step == len(hops) - 1:
+                        loop((STEPS - 2, STEPS), lambda u: wait(out_copies(u)))
                         loop(STEPS, kv_turn)
                     start(hops.get(step + 1, ()))
 
@@ -816,6 +818,7 @@
         gain_out = pltpu.make_async_copy(gpart.at[0], dgain, osem.at[1])
 
         def gain_start():
+            results.start()
             x_in.wait()
             gacc[...] = jnp.zeros_like(gacc)
             loop(GROUP, gain_step)
@@ -828,9 +831,7 @@
             start(gain_hops[k + 1 : k + 2] or gain_last)
 
         def gain_finish():
-            results.start()
-            for k in range(1, len(near)):
-                gain_hop(k)
+            gain_hop(last - 1)
             gz[z] = gpart[last]
             wait(gain_last)
             wait_send(gain_hops)
@@ -880,11 +881,13 @@
         gain_start()
         loop((STEPS - 2, STEPS - 1), grad_out)
         gain_hop(0)
+        kv_step(STEPS - 1)
+        gain_hop(1)
         loop((STEPS - 1, STEPS), grad_out)
-        kv_step(STEPS - 1)
         gain_finish()
+        loop(STEPS, lambda t: wait(turned(t)))
         for u in (STEPS - 2, STEPS - 1):
-            wait(out_copies(u) + out2_copies(u))
+            wait(out2_copies(u))
         for group in hops.values():
             wait_send(group)
 
@@ -895,7 +898,7 @@
     wide += [(ITEMS, ROWS, DIM), (GROUP, ROWS, DIM)]
     types = [BF16] * 4 + [F32] + [BF16] * 4 + [F32] + [BF16] * 3
     pl.run_scoped(activations, *[pltpu.VMEM(s, t) for s, t in zip(wide, types)])
-    narrow = [(2 * NEAR, NBIG), (2, 2, GROUP, *TALL, TILE), (2, TILE, 2 * FFN), (2, TILE, HEAD), (2, OUT, TILE), (KV, DIM), (2, TILE, HEAD), (ITEMS, ROWS, DIM)]
+    narrow = [(2 * NEAR, NBIG), (2, 2, GROUP, *TALL, TILE), (2, TILE, 2 * FFN), (2, TILE, HEAD), (2, OUT, TILE), (KV, DIM), (ITEMS, ROWS, DIM)]
     totals = [(KV, DIM), (KV, half), (2, KV, EIGHTH), (2, KV, W), (KV, 2 * W), (3, KROWS, 2 * W), (BLOCK, DIM), (4, 1, DIM), (3, 1, DIM), (4, 1, DIM)]
     buffers = [pltpu.VMEM(s, BF16) for s in narrow] + [pltpu.VMEM(s, F32) for s in totals]
     pl.run_scoped(gradients, *buffers)
@@ -918,7 +921,7 @@
         out_specs=[any_spec] * len(shapes),
         scratch_shapes=[
             *[dma(s) for s in pairs for _ in PAIR],
-            *[dma(s) for s in ((6,), (7,), (2,), (2,), (2, 2), (2, 3), (2, 2), (6,), (6,))],
+            *[dma(s) for s in ((6,), (7,), (2,), (2,), (2, 2), (2, 3), (2, 2), (2, STEPS), (6,), (6,))],
             pltpu.SemaphoreType.REGULAR,
             pltpu.VMEM((2, 2, GROUP, ROWS, DIM), BF16),
             *scatter_scratch(),

time: 547 us -> 540 us (0.987)
  Pallas kernels: 546 us -> 539 us
    pallas_call x1, Pallas kernels: 532 us -> 525 us  [layer_call(): pl.pallas_call(layer_kernel, out_shape=[jax.ShapeDtypeStruct(s, t) for s,...]
where the time goes in v6:
time: 540 us
  Pallas kernels  539 us (100%)
    pallas_call x1, Pallas kernels, layer_call(): pl.pallas_call(layer_kernel, out_shape=[jax.ShapeDtypeStruct(s, t) for s,...  525 us
    pallas_call x1, Pallas kernels, finish_call(): pl.pallas_call(finish_kernel, out_shape=[jax.ShapeDtypeStruct(s, t) for s...  13.9 us

profile of v6, /device:TPU:0, one launch (start us, length us, event | category | flops | bytes accessed | tf_op | source)
XLA Modules:
  0.0 540.1 jit_solution(16157209799469982454)
XLA Ops:
  0.6 525.4 %layer.1 = (bf16[8,2,2,2,64,4096]{5,4,3,2,1,0:T(8,128)(2,1)}, bf16[8,2,2,2,64,4096]{5,4,3,2,1,0:T(8,128)(2,1)}, bf16[16,2,2,64,4096]{4,3,2,1,0:T(8,128)(2,1)}, b...) custom-call(bf16[16,8,4096]{2,1,0:T(8,128)(2,1)} %x_loc.1, ...), custom_call_target="tpu_custom_call" | custom-call | tf_op jit(solution)/shard_map/layer/pallas_call | solution.py:917
  526.0 13.9 %finish.1 = (bf16[128,4096]{1,0:T(8,128)(2,1)}, bf16[128,4096]{1,0:T(8,128)(2,1)}, f32[1,4096]{1,0:T(1,128)}, bf16[4096,512]{1,0:T(8,128)(2,1)}, bf16[4096,512]{...) custom-call(bf16[2,128,4096]{2,1,0:T(8,128)(2,1)} %bitcast.13, ...), custom_call_target="tpu_custom_call" | custom-call | tf_op jit(solution)/shard_map/finish/pallas_call | solution.py:969

commit v7 on v6

--- a/solution.py
+++ b/solution.py
@@ -516,9 +516,10 @@
         swaps = [remote(away[s], to[s], (sx.at[s], rx.at[s]), sib) for s in PAIR]
         puts = [pltpu.make_async_copy(src, dst, lsem.at[s]) for s, (src, dst) in enumerate(zip((stage.at[own], dy_own), to))]
         start(swaps + puts)
-        wait(puts)
-        wait_recv(swaps)
-        loop(2, gather.tick)
+        for s in PAIR:
+            puts[s].wait()
+            swaps[s].wait_recv()
+            loop((s, s + 1), gather.tick)
 
         spots = (
             (w1, wcat.at[:, 0:FFN], wcat.at[:, OWN : OWN + FFN]),

time: 540 us -> 540 us (level)
  no operation moved by 1% of the time
where the time goes in v7:
time: 540 us; the launch traced here: 539 us
  Pallas kernels  539 us (100%)
    pallas_call x1, Pallas kernels, layer_call(): pl.pallas_call(layer_kernel, out_shape=[jax.ShapeDtypeStruct(s, t) for s,...  525 us
    pallas_call x1, Pallas kernels, finish_call(): pl.pallas_call(finish_kernel, out_shape=[jax.ShapeDtypeStruct(s, t) for s...  13.9 us

profile of v7, /device:TPU:0, one launch (start us, length us, event | category | flops | bytes accessed | tf_op | source)
XLA Modules:
  0.0 539.4 jit_solution(17204405175115640564)
XLA Ops:
  0.6 524.6 %layer.1 = (bf16[8,2,2,2,64,4096]{5,4,3,2,1,0:T(8,128)(2,1)}, bf16[8,2,2,2,64,4096]{5,4,3,2,1,0:T(8,128)(2,1)}, bf16[16,2,2,64,4096]{4,3,2,1,0:T(8,128)(2,1)}, b...) custom-call(bf16[16,8,4096]{2,1,0:T(8,128)(2,1)} %x_loc.1, ...), custom_call_target="tpu_custom_call" | custom-call | tf_op jit(solution)/shard_map/layer/pallas_call | solution.py:918
  525.3 13.9 %finish.1 = (bf16[128,4096]{1,0:T(8,128)(2,1)}, bf16[128,4096]{1,0:T(8,128)(2,1)}, f32[1,4096]{1,0:T(1,128)}, bf16[4096,512]{1,0:T(8,128)(2,1)}, bf16[4096,512]{...) custom-call(bf16[2,128,4096]{2,1,0:T(8,128)(2,1)} %bitcast.13, ...), custom_call_target="tpu_custom_call" | custom-call | tf_op jit(solution)/shard_map/finish/pallas_call | solution.py:970
